TPU v7x, 256 devices: a whole 4x4x8 slice. The times are simulated.
256 devices in a mesh: seq: 16 (over z, core), tp: 8 (over x_lo, y), dp: 2 (over x_hi).
Axes of the slice: x: 4 (x_hi: 2, x_lo: 2; x = x_hi * 2 + x_lo), y: 4, z: 8, core: 2. Of those that a mesh axis runs over, the one named last changes fastest.
Arguments:
- query_latent: bfloat16 [2, 4096, 1536], P('dp', 'seq', 'tp'), may hold values from -6 to 6
- key_latent: bfloat16 [2, 4096, 512], P('dp', 'seq', 'tp'), may hold values from -6 to 6
- rope_key: bfloat16 [2, 4096, 64], P('dp', 'seq'), may hold values from -6 to 6
- w_uq: bfloat16 [1536, 12288], P('seq', 'tp')
- w_uk: bfloat16 [512, 8192], P('seq', 'tp'), may hold values from -0.25 to 0.25
- w_uv: bfloat16 [512, 8192], P('seq', 'tp'), may hold values from -0.25 to 0.25
- block_order: int32 [2, 32], P('dp'), may hold values from 0 to 31, each once within a row
- segment_ids: int32 [2, 4096], P('dp'), may hold values from 0 to 3, never falling along the last dimension, each value on 1 to 2048 neighbouring positions
Outputs:
- context: bfloat16 [2, 4096, 8192], P('dp', 'seq', 'tp')
- clipped_uq: bfloat16 [1536, 12288], P('seq', 'tp')
- clipped_uk: bfloat16 [512, 8192], P('seq', 'tp')
Inputs may be any that keep to these rules, and one draw needn't show every extreme that they name: `block_order`: each row is a permutation of the 32 position blocks. `segment_ids`: never falling along positions; each document has at most 2048 positions.
All inputs are finite; a program needn't handle non-finite values.
Results may differ from a plain program's by a relative error of at most 0.012.
The roundings to bfloat16 on the way count: a program that leaves them out, or rounds other values in their place, can miss the bound.
Values may be sent and summed in bfloat16 or wider, within the bound.
No kernel may reach another device: no remote copies, remote signals or barrier semaphores. Data moves between devices by JAX's collectives and lax.ppermute only.
A program may use at most 64 MiB of HBM per device.

v0:
```python
import math

import jax
import jax.numpy as jnp
from jax import lax
from jax.experimental import pallas as pl
from jax.experimental.pallas import tpu as pltpu
from jax.sharding import PartitionSpec as P

NOPE = 128
ROPE = 64
VD = 128
CLIP = 8
BLK = 128
CHUNK = 256

rope_base = 50000.0
masked_value = -1e30
scale = 1.0 / math.sqrt(NOPE + ROPE)

ANY = pl.BlockSpec(memory_space=pl.ANY)
SMEM = pl.BlockSpec(memory_space=pltpu.SMEM)
VMEM = pl.BlockSpec(memory_space=pltpu.VMEM)


def meta_of(meta):
    return dict(z=meta[35], c=meta[36], y=meta[37], xl=meta[38])


def block_of(meta, i):
    m = meta_of(meta)
    half = i // 2
    core = jnp.where(half == 0, m["c"], 1 - m["c"])
    return meta[(m["z"] * 2 + core) * 2 + i % 2]


def start_of(meta, p):
    s = jnp.int32(0)
    for l in range(3):
        b = meta[32 + l]
        s = jnp.where(b <= p, jnp.maximum(s, b), s)
    return s


def feature_row(meta, t, each):
    m = meta_of(meta)
    x, yy = t // 4, t % 4
    dy = lax.rem(yy - m["y"] + 4, 4)
    j = jnp.where(dy == 0, 0, jnp.where(dy == 1, 2, jnp.where(dy == 2, 3, 1)))
    xr = jnp.where(x == m["xl"], 0, 1)
    return (j * 2 + xr) * each


RING = [0, -1, 1, -2, 2, -3, 3, -4]


def join_kernel(*refs):
    for j in range(8):
        refs[8][j] = refs[j][...]


def label_of(meta, p):
    label = jnp.zeros_like(p)
    for l in range(3):
        label = label + jnp.where(p >= meta[32 + l], 1, 0)
    return label


SLOTS = 38
EMPTY = 37
to_exp2 = scale * math.log2(math.e)


def attend_kernel(meta, *refs):
    q_in, w_in, kv_in, cs, pieces = refs[:2], refs[2:10], refs[10:18], refs[18], (refs[19:24], refs[24:29])
    out, hm = refs[29:31]
    q, w, kvw, lat, rope, kn, v, kr, qs, sbuf, mx, rm, acc, total, step_i, step_ch, need = refs[31:48]
    qsem, wsem, kvsem, ksem = refs[48:]
    m = meta_of(meta)
    f32, bf16 = jnp.float32, jnp.bfloat16
    first, second = [], []
    for half in range(2):
        first.append(pltpu.make_async_copy(q_in[half], q.at[half], qsem.at[half]))
    for j in range(8):
        t = lax.rem(m["z"] + RING[j] + 8, 8)
        row = pl.multiple_of(feature_row(meta, t, 192), 64)
        first.append(pltpu.make_async_copy(w_in[j], w.at[pl.ds(row, 192)], wsem.at[j]))
        row = pl.multiple_of(feature_row(meta, t, 64), 64)
        second.append(pltpu.make_async_copy(kv_in[j], kvw.at[pl.ds(row, 64)], kvsem.at[j]))
    for core in range(2):
        own, up, dn, f1, f2 = pieces[core]
        for n, (src, plane, start, count, dy) in enumerate(
            ((own, 0, 0, 8, 0), (up, 1, 0, 8, 3), (dn, 2, 0, 8, 1), (f1, 3, 0, 4, 2), (f2, 3, 4, 4, 2))
        ):
            rows = pl.ds(core * 8 + start, count)
            yq = pl.multiple_of(lax.rem(m["y"] + dy, 4) * 32, 32)
            second.append(
                pltpu.make_async_copy(src.at[:, :256, :], lat.at[plane, rows], ksem.at[core, n, 0])
            )
            second.append(
                pltpu.make_async_copy(
                    src.at[:, 256:, :], rope.at[rows, pl.ds(yq, 32), :], ksem.at[core, n, 1]
                )
            )
    for cp in first + second:
        cp.start()

    for n in range(16):
        need[n] = 0
    count = jnp.int32(0)
    for i in range(4):
        pb = block_of(meta, i)
        lo = start_of(meta, pb * BLK) // CHUNK
        hi = pb // 2
        need[hi] = 1

        def add(ch, g, i=i):
            step_i[g] = i
            step_ch[g] = ch
            need[ch] = 1
            return g + 1

        count = lax.fori_loop(lo, hi, add, count)
    step_i[count] = 3
    step_ch[count] = block_of(meta, 3) // 2
    odd = lax.rem(count, 2)

    lane64 = lax.broadcasted_iota(jnp.int32, (BLK, 64), 1)
    row64 = lax.broadcasted_iota(jnp.int32, (BLK, 64), 0)
    for cp in first:
        cp.wait()
    for half in range(2):
        full = jnp.dot(q[half], w[...], preferred_element_type=f32)
        labels = [
            jnp.where(label_of(meta, row64 + block_of(meta, half * 2 + b) * BLK) == lane64, 1.0, 0.0)
            for b in range(2)
        ]
        onehot = jnp.concatenate(labels, axis=0).astype(bf16)
        rows = slice(half * 256, half * 256 + 256)
        cos = cs[rows, :64]
        sin = cs[rows, 64:]
        for h in range(4):
            nope = full[:, h * 192 : h * 192 + 128].astype(bf16)
            r = full[:, h * 192 + 128 : h * 192 + 192]
            turned = jnp.concatenate([r[:, 32:], r[:, :32]], axis=1)
            rot = (r * cos + turned * sin).astype(bf16)
            qs[h, rows, :128] = nope
            qs[h, rows, 128:] = jnp.concatenate([rot, onehot], axis=1)

    mx[...] = jnp.full(mx.shape, masked_value, f32)
    acc[...] = jnp.zeros(acc.shape, f32)
    total[...] = jnp.zeros(total.shape, f32)
    sbuf[EMPTY] = jnp.full((4, BLK, CHUNK), masked_value, f32)
    for cp in second:
        cp.wait()

    def project(i, carry):
        j = lax.rem(i, 8)
        s = (j + 1) // 2
        dz = jnp.where(lax.rem(j, 2) == 1, -s, s)
        zz = lax.rem(m["z"] + dz + 8, 8)
        cc = jnp.where(i < 8, m["c"], 1 - m["c"])
        base = (zz * 2 + cc) * 2

        @pl.when((need[meta[base] // 2] + need[meta[base + 1] // 2]) > 0)
        def _():
            x = jnp.concatenate([lat[n, i] for n in range(4)], axis=1)
            y = jnp.dot(x, kvw[...], preferred_element_type=f32)
            fold = rope[i]
            for b in range(2):
                pb = pl.multiple_of(meta[base + b] * BLK, BLK)
                rows = slice(b * BLK, (b + 1) * BLK)
                kn[pl.ds(pb, BLK), :] = y[rows, :512].astype(bf16)
                v[pl.ds(pb, BLK), :] = y[rows, 512:].astype(bf16)
                label = label_of(meta, row64 + pb)
                apart = jnp.where((lane64 < 4) & (lane64 != label), masked_value, 0.0).astype(bf16)
                kr[pl.ds(pb, BLK), :] = jnp.concatenate(
                    [fold[:, b * 64 : b * 64 + 64], apart], axis=1
                )

        return carry

    lax.fori_loop(0, 16, project, 0)

    def scores(i, ch):
        keys = pl.ds(pl.multiple_of(ch * CHUNK, CHUNK), CHUNK)
        rows = pl.ds(pl.multiple_of(i * BLK, BLK), BLK)
        got = []
        for h in range(4):
            k = jnp.concatenate([kn[keys, h * 128 : (h + 1) * 128], kr[keys, :]], axis=1)
            got.append(
                lax.dot_general(
                    qs[h, rows, :], k, (((1,), (1,)), ((), ())), preferred_element_type=f32
                )
            )
        return got

    def keep(i, slot, h, s):
        sbuf[slot, h] = s
        mx[i, h] = jnp.maximum(mx[i, h], jnp.maximum(s[:, :128], s[:, 128:]))

    def diagonal(i, carry):
        pb = block_of(meta, i)
        ch = pb // 2
        row = lax.broadcasted_iota(jnp.int32, (BLK, CHUNK), 0) + (pb * BLK - ch * CHUNK)
        col = lax.broadcasted_iota(jnp.int32, (BLK, CHUNK), 1)
        bias = jnp.where(col <= row, 0.0, masked_value)
        for h, s in enumerate(scores(i, ch)):
            keep(i, i, h, s + bias)
        return carry

    lax.fori_loop(0, 4, diagonal, 0)

    def score_pair(n, carry):
        picks = []
        for g in (2 * n, jnp.minimum(2 * n + 1, count - 1)):
            i, ch = step_i[g], step_ch[g]
            picks.append((i, g + 4, scores(i, ch)))
        for i, slot, got in picks:
            for h, s in enumerate(got):
                keep(i, slot, h, s)
        return carry

    pairs = (count + odd) // 2
    lax.fori_loop(0, pairs, score_pair, 0)

    hm[...] = jnp.full(hm.shape, masked_value, f32)

    def finish_max(i, carry):
        for h in range(4):
            top = jnp.broadcast_to(jnp.max(mx[i, h], axis=1, keepdims=True), (BLK, 128))
            rm[i, h] = top * to_exp2
            best = jnp.max(top, axis=0, keepdims=True) * scale
            hm[h : h + 1, :] = jnp.maximum(hm[h : h + 1, :], best)
        return carry

    lax.fori_loop(0, 4, finish_max, 0)

    def mix(steps):
        for i, ch, slot in steps:
            keys = pl.ds(pl.multiple_of(ch * CHUNK, CHUNK), CHUNK)
            for h in range(4):
                s = sbuf[slot, h]
                top = rm[i, h]
                p0 = jnp.exp2(s[:, :128] * to_exp2 - top)
                p1 = jnp.exp2(s[:, 128:] * to_exp2 - top)
                total[i, h] += p0 + p1
                p = jnp.concatenate([p0, p1], axis=1).astype(bf16)
                acc[i, h] += jnp.dot(p, v[keys, h * 128 : (h + 1) * 128], preferred_element_type=f32)

    def mix_diagonal(n, carry):
        mix([(2 * n + e, block_of(meta, 2 * n + e) // 2, 2 * n + e) for e in range(2)])
        return carry

    lax.fori_loop(0, 2, mix_diagonal, 0)

    def mix_pair(n, carry):
        a, b = 2 * n, 2 * n + 1
        slot = jnp.where(b < count, b + 4, EMPTY)
        mix([(step_i[a], step_ch[a], a + 4), (step_i[b], step_ch[b], slot)])
        return carry

    lax.fori_loop(0, pairs, mix_pair, 0)

    def finish(i, carry):
        rows = pl.ds(pl.multiple_of(i * BLK, BLK), BLK)
        for h in range(4):
            whole = jnp.sum(total[i, h], axis=1, keepdims=True)
            out[rows, h * 128 : (h + 1) * 128] = (acc[i, h] / whole).astype(bf16)
        return carry

    lax.fori_loop(0, 4, finish, 0)


def shift_seq(by):
    return [(i, (i + 2 * by) % 16) for i in range(16)]


SWAP = [(i, i ^ 1) for i in range(16)]
XSWAP = [(i, i ^ 4) for i in range(8)]


def shift_y(by):
    return [(x * 4 + y, x * 4 + (y + by) % 4) for x in range(2) for y in range(4)]


def ring(x):
    up, dn, got = x, x, [x]
    for s in range(4):
        up = lax.ppermute(up, "seq", shift_seq(1))
        got.append(up)
        if s < 3:
            dn = lax.ppermute(dn, "seq", shift_seq(-1))
            got.append(dn)
    return got


def swap(x):
    return lax.ppermute(x, "seq", SWAP)


def halves(w, c, width):
    mine = lax.dynamic_slice_in_dim(w, c * width, width, 1)
    other = swap(lax.dynamic_slice_in_dim(w, (1 - c) * width, width, 1))
    first = c == 0
    return jnp.concatenate([jnp.where(first, mine, other), jnp.where(first, other, mine)], axis=0)


def of_everyone(array, axis):
    copies = jnp.broadcast_to(array, (lax.axis_size(axis), *array.shape))
    return jnp.max(lax.all_to_all(copies, axis, split_axis=0, concat_axis=0, tiled=True), axis=0)


def on_device(query_latent, key_latent, rope_key, w_uq, w_uk, w_uv, block_order, segment_ids):
    bf16, f32 = jnp.bfloat16, jnp.float32
    s, t = lax.axis_index("seq"), lax.axis_index("tp")
    z, c, y, xl = s // 2, s % 2, t % 4, t // 4
    order, labels = block_order[0], segment_ids[0]
    bounds = jnp.stack([jnp.sum((labels < l).astype(jnp.int32)) for l in (1, 2, 3)])
    meta = jnp.concatenate(
        [order, bounds, jnp.stack([z, c, y, xl]).astype(jnp.int32), jnp.zeros((9,), jnp.int32)]
    )

    wq = halves(w_uq, c, 768)
    kv = halves(
        jnp.concatenate([w_uk[:, :512], w_uv[:, :512], w_uk[:, 512:], w_uv[:, 512:]], axis=1), c, 1024
    )
    chip = lax.dynamic_slice_in_dim(order, 4 * z, 4)
    chip = jnp.where(c == 0, chip, jnp.roll(chip, 2))
    pos = (chip[:, None] * BLK + jnp.arange(BLK, dtype=jnp.int32)[None, :]).reshape(-1)
    steps = jnp.arange(ROPE // 2, dtype=f32) * (2.0 / ROPE)
    freqs = jnp.exp(-math.log(rope_base) * steps)
    angle = pos.astype(f32)[:, None] * freqs[None, :]
    cos, sin = jnp.cos(angle), jnp.sin(angle)
    cs = jnp.concatenate([cos, cos, -sin, sin], axis=1)

    kq = jnp.concatenate([key_latent[0].T, query_latent[0].T], axis=0)
    kq_x = lax.ppermute(kq, "tp", XSWAP)
    k_x = jnp.concatenate([kq[:64], kq_x[:64]], axis=0).T
    q_x = jnp.concatenate([kq[64:], kq_x[64:]], axis=0).T
    rk = rope_key[0].astype(f32)
    a, b = rk[:, :32], rk[:, 32:]
    rc, rs = cos[:256], sin[:256]
    k_rope = jnp.concatenate([a * rc - b * rs, b * rc + a * rs], axis=1).astype(bf16)
    fold = jnp.concatenate([k_rope[:128], k_rope[128:]], axis=1)
    k_one = jnp.concatenate([k_x, lax.dynamic_slice_in_dim(fold, y * 32, 32, 0)], axis=0)

    k_ring = ring(k_one)
    kv_ring = ring(kv)
    w_ring = ring(wq)
    q_parts = [q_x] + [lax.ppermute(q_x, "tp", shift_y(by)) for by in (1, -1, 2)]
    q_own = jnp.concatenate(q_parts, axis=1)
    q_sib = swap(q_own)
    k_all = pl.pallas_call(
        join_kernel,
        out_shape=jax.ShapeDtypeStruct((8, 288, 128), bf16),
        in_specs=[VMEM] * 8,
        out_specs=VMEM,
        cost_estimate=pl.CostEstimate(flops=1 << 20, bytes_accessed=2 << 20, transcendentals=0),
        name="join",
    )(*k_ring)
    k_up = lax.ppermute(k_all, "tp", shift_y(1))
    k_dn = lax.ppermute(k_all, "tp", shift_y(-1))
    k_f1 = lax.ppermute(k_up[:4], "tp", shift_y(1))
    k_f2 = lax.ppermute(k_dn[4:], "tp", shift_y(-1))
    k_own = [k_all, k_up, k_dn, k_f1, k_f2]
    k_sib = [swap(p) for p in k_own]

    vm = pltpu.VMEM
    ctx, hm = pl.pallas_call(
        attend_kernel,
        out_shape=[
            jax.ShapeDtypeStruct((512, 512), bf16),
            jax.ShapeDtypeStruct((8, 128), f32),
        ],
        in_specs=[SMEM] + [ANY] * 18 + [VMEM] + [ANY] * 10,
        out_specs=[VMEM] * 2,
        scratch_shapes=[
            vm((2, 256, 1536), bf16),
            vm((1536, 768), bf16),
            vm((512, 1024), bf16),
            vm((4, 16, 256, 128), bf16),
            vm((16, 128, 128), bf16),
            vm((4096, 512), bf16),
            vm((4096, 512), bf16),
            vm((4096, 128), bf16),
            vm((4, 512, 256), bf16),
            vm((SLOTS, 4, BLK, CHUNK), f32),
            vm((4, 4, BLK, 128), f32),
            vm((4, 4, BLK, 128), f32),
            vm((4, 4, BLK, 128), f32),
            vm((4, 4, BLK, 128), f32),
            pltpu.SMEM((40,), jnp.int32),
            pltpu.SMEM((40,), jnp.int32),
            pltpu.SMEM((16,), jnp.int32),
            pltpu.SemaphoreType.DMA((2,)),
            pltpu.SemaphoreType.DMA((8,)),
            pltpu.SemaphoreType.DMA((8,)),
            pltpu.SemaphoreType.DMA((2, 5, 2)),
        ],
        compiler_params=pltpu.CompilerParams(vmem_limit_bytes=60 << 20),
        cost_estimate=pl.CostEstimate(
            flops=20 << 30, bytes_accessed=12 << 20, transcendentals=4 << 20
        ),
        name="attend",
    )(meta, q_own, q_sib, *w_ring, *kv_ring, cs, *k_own, *k_sib)

    local_max = hm[:4, 0]
    low = jnp.full((4,), masked_value, f32)
    both = jnp.where(
        c == 0, jnp.concatenate([local_max, low]), jnp.concatenate([low, local_max])
    )
    head_max = of_everyone(both, ("seq", "dp"))
    ratio = CLIP / jnp.maximum(head_max, CLIP)
    root = jnp.sqrt(ratio)
    factors = jnp.concatenate(
        [jnp.broadcast_to(root[:, None], (8, NOPE)), jnp.broadcast_to(ratio[:, None], (8, ROPE))], axis=1
    ).reshape(8 * (NOPE + ROPE))
    clipped_uq = (w_uq.astype(f32) * factors[None, :]).astype(bf16)
    clipped_uk = (w_uk.astype(f32) * jnp.repeat(root, NOPE)[None, :]).astype(bf16)

    got = swap(ctx[256:])
    own = ctx[:256]
    first = c == 0
    context = jnp.concatenate([jnp.where(first, own, got), jnp.where(first, got, own)], axis=1)
    return (context[None], clipped_uq, clipped_uk)


def solution(mesh):
    placed = (
        P("dp", "seq", "tp"),
        P("dp", "seq", "tp"),
        P("dp", "seq", None),
        P("seq", "tp"),
        P("seq", "tp"),
        P("seq", "tp"),
        P("dp", None),
        P("dp", None),
    )
    return jax.shard_map(
        on_device,
        mesh=mesh,
        in_specs=placed,
        out_specs=(P("dp", "seq", "tp"), P("seq", "tp"), P("seq", "tp")),
        check_vma=False,
    )
```

profile of v0, /device:TPU:1, one launch (start us, length us, event | category | flops | bytes accessed | tf_op | source)
XLA Modules:
  0.0 136.9 jit_solution(8741244955056278220)
XLA Ops:
  1.6 3.3 %collective-permute-start.13 = (bf16[32,1024]{1,0:T(8,128)(2,1)S(1)}, bf16[32,1024]{1,0:T(8,128)(2,1)S(1)}, u32[]{:S(2)}, u32[]{:S(2)}) collective-permute-start(bf16[32,1024]{1,0:T(8,128)(2,1)S(1)} %constant_dynamic-slice_fusion.1), channel_id=1, source_target_pairs={{0,16},{16,0},{32,48},{48,32},{64,80},{80,64},{96,112},{112,96},{1... | collective-permute-start | bytes 196616 | tf_op jit(solution)/shard_map/ppermute | solution.py:299
  8.1 3.0 %collective-permute-done = bf16[256,256]{0,1:T(8,128)(2,1)S(1)} collective-permute-done((bf16[256,256]{0,1:T(8,128)(2,1)S(1)}, bf16[256,256]{0,1:T(8,128)(2,1)S(1)}, u32[]{:S(2)}, u32[]{:S(2)}) %collective-permute-start) | collective-permute-done | bytes 131104 | tf_op jit(solution)/shard_map/ppermute | solution.py:338
  11.4 3.9 %collective-permute-start.15 = (bf16[64,1024]{1,0:T(8,128)(2,1)S(1)}, bf16[64,1024]{1,0:T(8,128)(2,1)S(1)}, u32[]{:S(2)}, u32[]{:S(2)}) collective-permute-start(bf16[64,1024]{1,0:T(8,128)(2,1)S(1)} %pad_maximum_fusion.5.refs_10_), channel_id=1, source_target_pairs={{0,224},{16,240},{32,0},{48,16},{64,32},{80,48},{96,64},{112,80},{... | collective-permute-start | bytes 393224 | tf_op jit(solution)/shard_map/ppermute | solution.py:293
  15.3 2.7 %collective-permute-start.22 = (bf16[288,128]{1,0:T(8,128)(2,1)S(1)}, bf16[288,128]{1,0:T(8,128)(2,1)S(1)}, u32[]{:S(2)}, u32[]{:S(2)}) collective-permute-start(bf16[288,128]{1,0:T(8,128)(2,1)S(1)} %pad_maximum_fusion.6.refs_0_), channel_id=1, source_target_pairs={{0,224},{16,240},{32,0},{48,16},{64,32},{80,48},{96,64},{112,80},{... | collective-permute-start | bytes 221192 | tf_op jit(solution)/shard_map/ppermute | solution.py:293
  18.3 2.7 %collective-permute-start.17 = (bf16[64,1024]{1,0:T(8,128)(2,1)S(1)}, bf16[64,1024]{1,0:T(8,128)(2,1)S(1)}, u32[]{:S(2)}, u32[]{:S(2)}) collective-permute-start(bf16[64,1024]{1,0:T(8,128)(2,1)S(1)} %collective-permute-done.15.refs_12_), channel_id=1, source_target_pairs={{0,224},{16,240},{32,0},{48,16},{64,32},{80,48},{96,64},{112,80},{... | collective-permute-start | bytes 393224 | tf_op jit(solution)/shard_map/ppermute | solution.py:293
  21.1 2.7 %collective-permute-start.24 = (bf16[288,128]{1,0:T(8,128)(2,1)S(1)}, bf16[288,128]{1,0:T(8,128)(2,1)S(1)}, u32[]{:S(2)}, u32[]{:S(2)}) collective-permute-start(bf16[288,128]{1,0:T(8,128)(2,1)S(1)} %collective-permute-done.22.refs_2_), channel_id=1, source_target_pairs={{0,224},{16,240},{32,0},{48,16},{64,32},{80,48},{96,64},{112,80},{... | collective-permute-start | bytes 221192 | tf_op jit(solution)/shard_map/ppermute | solution.py:293
  23.8 2.7 %collective-permute-start.7 = (bf16[192,768]{1,0:T(8,128)(2,1)S(1)}, bf16[192,768]{1,0:T(8,128)(2,1)}, u32[]{:S(2)}, u32[]{:S(2)}) collective-permute-start(bf16[192,768]{1,0:T(8,128)(2,1)S(1)} %pad_maximum_fusion.1.refs_2_), channel_id=1, source_target_pairs={{0,224},{16,240},{32,0},{48,16},{64,32},{80,48},{96,64},{112,80},{... | collective-permute-start | bytes 884744 | tf_op jit(solution)/shard_map/ppermute | solution.py:293
  26.5 2.7 %collective-permute-start.26 = (bf16[288,128]{1,0:T(8,128)(2,1)S(1)}, bf16[288,128]{1,0:T(8,128)(2,1)S(1)}, u32[]{:S(2)}, u32[]{:S(2)}) collective-permute-start(bf16[288,128]{1,0:T(8,128)(2,1)S(1)} %collective-permute-done.24.refs_4_), channel_id=1, source_target_pairs={{0,224},{16,240},{32,0},{48,16},{64,32},{80,48},{96,64},{112,80},{... | collective-permute-start | bytes 221192 | tf_op jit(solution)/shard_map/ppermute | solution.py:293
  29.5 3.0 %collective-permute-start.3 = (bf16[256,384]{1,0:T(8,128)(2,1)S(1)}, bf16[256,384]{1,0:T(8,128)(2,1)S(1)}, u32[]{:S(2)}, u32[]{:S(2)}) collective-permute-start(bf16[256,384]{1,0:T(8,128)(2,1)S(1)} %maximum_bitcast_fusion.1), channel_id=1, source_target_pairs={{0,4},{2,6},{4,0},{6,2},{8,12},{10,14},{12,8},{14,10},{1,5},{3,7},... | collective-permute-start | bytes 589832 | tf_op jit(solution)/shard_map/ppermute | solution.py:351
  39.2 2.8 %collective-permute-start.19 = (bf16[64,1024]{1,0:T(8,128)(2,1)S(1)}, bf16[64,1024]{1,0:T(8,128)(2,1)S(1)}, u32[]{:S(2)}, u32[]{:S(2)}) collective-permute-start(bf16[64,1024]{1,0:T(8,128)(2,1)S(1)} %collective-permute-done.17.refs_14_), channel_id=1, source_target_pairs={{0,224},{16,240},{32,0},{48,16},{64,32},{80,48},{96,64},{112,80},{... | collective-permute-start | bytes 393224 | tf_op jit(solution)/shard_map/ppermute | solution.py:293
  41.9 2.7 %collective-permute-start.9 = (bf16[192,768]{1,0:T(8,128)(2,1)}, bf16[192,768]{1,0:T(8,128)(2,1)S(1)}, u32[]{:S(2)}, u32[]{:S(2)}) collective-permute-start(bf16[192,768]{1,0:T(8,128)(2,1)} %collective-permute-done.7.refs_4_), channel_id=1, source_target_pairs={{0,224},{16,240},{32,0},{48,16},{64,32},{80,48},{96,64},{112,80},{... | collective-permute-start | bytes 884744 | tf_op jit(solution)/shard_map/ppermute | solution.py:293
  44.6 6.6 %collective-permute-start.32 = (bf16[8,288,128]{2,1,0:T(8,128)(2,1)}, bf16[8,288,128]{2,1,0:T(8,128)(2,1)S(1)}, u32[]{:S(2)}, u32[]{:S(2)}) collective-permute-start(bf16[8,288,128]{2,1,0:T(8,128)(2,1)} %join.1.refs_19_), channel_id=1, source_target_pairs={{0,16},{16,0},{32,48},{48,32},{64,80},{80,64},{96,112},{112,96},{1... | collective-permute-start | bytes 1769480 | tf_op jit(solution)/shard_map/ppermute | solution.py:299
  52.0 3.7 %collective-permute-start.4 = (bf16[256,1536]{1,0:T(8,128)(2,1)S(1)}, bf16[256,1536]{1,0:T(8,128)(2,1)S(1)}, u32[]{:S(2)}, u32[]{:S(2)}) collective-permute-start(bf16[256,1536]{1,0:T(8,128)(2,1)S(1)} %pad_maximum_fusion.refs_0_), channel_id=1, source_target_pairs={{0,16},{16,0},{32,48},{48,32},{64,80},{80,64},{96,112},{112,96},{1... | collective-permute-start | bytes 2359304 | tf_op jit(solution)/shard_map/ppermute | solution.py:299
  55.8 3.8 %collective-permute-done.8.refs_5_ = bf16[192,768]{1,0:T(8,128)(2,1)S(1)} collective-permute-done((bf16[192,768]{1,0:T(8,128)(2,1)}, bf16[192,768]{1,0:T(8,128)(2,1)S(1)}, u32[]{:S(2)}, u32[]{:S(2)}) %collective-permute-start.8) | collective-permute-done | bytes 294944 | tf_op jit(solution)/shard_map/ppermute | solution.py:290
  61.0 6.5 %collective-permute-done.28.refs_20_ = bf16[8,288,128]{2,1,0:T(8,128)(2,1)} collective-permute-done((bf16[8,288,128]{2,1,0:T(8,128)(2,1)}, bf16[8,288,128]{2,1,0:T(8,128)(2,1)}, u32[]{:S(2)}, u32[]{:S(2)}) %collective-permute-start.28) | collective-permute-done | bytes 589856 | tf_op jit(solution)/shard_map/ppermute | solution.py:362
  69.5 3.0 %collective-permute-done.20.refs_17_ = bf16[64,1024]{1,0:T(8,128)(2,1)S(1)} collective-permute-done((bf16[64,1024]{1,0:T(8,128)(2,1)S(1)}, bf16[64,1024]{1,0:T(8,128)(2,1)S(1)}, u32[]{:S(2)}, u32[]{:S(2)}) %collective-permute-start.20) | collective-permute-done | bytes 131104 | tf_op jit(solution)/shard_map/ppermute | solution.py:290
  74.1 2.7 %collective-permute-start.34 = (bf16[8,288,128]{2,1,0:T(8,128)(2,1)}, bf16[8,288,128]{2,1,0:T(8,128)(2,1)}, u32[]{:S(2)}, u32[]{:S(2)}) collective-permute-start(bf16[8,288,128]{2,1,0:T(8,128)(2,1)} %collective-permute-done.29.refs_21_), channel_id=1, source_target_pairs={{0,16},{16,0},{32,48},{48,32},{64,80},{80,64},{96,112},{112,96},{1... | collective-permute-start | bytes 1769480 | tf_op jit(solution)/shard_map/ppermute | solution.py:299
  76.8 2.3 %collective-permute-done.31.refs_23_ = bf16[4,288,128]{2,1,0:T(8,128)(2,1)} collective-permute-done((bf16[4,288,128]{2,1,0:T(8,128)(2,1)S(1)}, bf16[4,288,128]{2,1,0:T(8,128)(2,1)}, u32[]{:S(2)}, u32[]{:S(2)}) %collective-permute-start.31) | collective-permute-done | bytes 294944 | tf_op jit(solution)/shard_map/ppermute | solution.py:365
  79.1 3.0 %collective-permute-start.36 = (bf16[4,288,128]{2,1,0:T(8,128)(2,1)}, bf16[4,288,128]{2,1,0:T(8,128)(2,1)}, u32[]{:S(2)}, u32[]{:S(2)}) collective-permute-start(bf16[4,288,128]{2,1,0:T(8,128)(2,1)} %collective-permute-done.31.refs_23_), channel_id=1, source_target_pairs={{0,16},{16,0},{32,48},{48,32},{64,80},{80,64},{96,112},{112,96},{1... | collective-permute-start | bytes 884744 | tf_op jit(solution)/shard_map/ppermute | solution.py:299
  82.1 2.6 %collective-permute-start.35 = (bf16[4,288,128]{2,1,0:T(8,128)(2,1)}, bf16[4,288,128]{2,1,0:T(8,128)(2,1)}, u32[]{:S(2)}, u32[]{:S(2)}) collective-permute-start(bf16[4,288,128]{2,1,0:T(8,128)(2,1)} %collective-permute-done.30.refs_22_), channel_id=1, source_target_pairs={{0,16},{16,0},{32,48},{48,32},{64,80},{80,64},{96,112},{112,96},{1... | collective-permute-start | bytes 884744 | tf_op jit(solution)/shard_map/ppermute | solution.py:299
  85.6 2.5 %concatenate.61.meta = s32[48]{0:T(128)} concatenate(s32[32]{0:T(128)S(1)} %bitcast.37, s32[1]{0:T(128)} %bitcast.1, s32[1]{0:T(128)} %bitcast.2, s32[1]{0:T(128)} %bitcast.3, s32[1]{0:T(128)} %bitcast.4, s32[1]{0:T(128)} %bitcast.5, s32[1]{0:T(128)} %bitcast.6, s32[1]{0:T(128)} %bitcast.7, s32[9]{0:T(128)S(1)} %broadcast.57), dimensions={0} | concatenate | bytes 384 | tf_op jit(solution)/shard_map/concatenate | solution.py:320
  89.1 24.3 %attend.1 = (bf16[512,512]{1,0:T(8,128)(2,1)}, f32[8,128]{1,0:T(8,128)}) custom-call(s32[48]{0:T(128)} %concatenate.61.meta, bf16[256,1536]{1,0:T(8,128)(2,1)} %copy-done.1, bf16[256,1536]{1,0:T(8,128)(2,1)} %copy-done.18, bf16[192,768]{1,0:T(8,128)(2,1)} %copy-done.4, bf16[192,768]{1,0:T(8,128)(2,1)} %collective-permute-done.6.refs_3_, ...), custom_call_target="tpu_custom_call" | custom-call | flops 21474836480 | bytes 12582912 | tf_op jit(solution)/shard_map/attend/pallas_call | solution.py:370
  115.1 9.8 %all-to-all-start = ((f32[32,1,8]{2,1,0:T(1,128)}), f32[32,1,8]{2,1,0:T(1,128)S(1)}, u32[]{:S(2)}, u32[]{:S(2)}) async-start(f32[32,1,8]{2,1,0:T(1,128)} %broadcast_in_dim.9), calls=%async_computation | async-start | bytes 32768 | tf_op jit(solution)/shard_map/all_to_all | solution.py:311
  126.2 8.0 %all-to-all-done = f32[32,1,8]{2,1,0:T(1,128)S(1)} async-done(((f32[32,1,8]{2,1,0:T(1,128)}), f32[32,1,8]{2,1,0:T(1,128)S(1)}, u32[]{:S(2)}, u32[]{:S(2)}) %all-to-all-start) | async-done | bytes 1056 | tf_op jit(solution)/shard_map/all_to_all | solution.py:311
  (163 shorter events, 24.5 us)
Async XLA Ops:
  6.1 12.1 %collective-permute-start.5 = (bf16[96,768]{1,0:T(8,128)(2,1)S(1)}, bf16[96,768]{1,0:T(8,128)(2,1)S(1)}, u32[]{:S(2)}, u32[]{:S(2)}) collective-permute-start(bf16[96,768]{1,0:T(8,128)(2,1)S(1)} %constant_dynamic-slice_fusion.2), channel_id=1, source_target_pairs={{0,16},{16,0},{32,48},{48,32},{64,80},{80,64},{96,112},{112,96},{1... | collective-permute-start | bytes 442376 | tf_op jit(solution)/shard_map/ppermute | solution.py:299
  18.3 11.1 %collective-permute-start.17 = (bf16[64,1024]{1,0:T(8,128)(2,1)S(1)}, bf16[64,1024]{1,0:T(8,128)(2,1)S(1)}, u32[]{:S(2)}, u32[]{:S(2)}) collective-permute-start(bf16[64,1024]{1,0:T(8,128)(2,1)S(1)} %collective-permute-done.15.refs_12_), channel_id=1, source_target_pairs={{0,224},{16,240},{32,0},{48,16},{64,32},{80,48},{96,64},{112,80},{... | collective-permute-start | bytes 393224 | tf_op jit(solution)/shard_map/ppermute | solution.py:293
  21.0 11.4 %collective-permute-start.16 = (bf16[64,1024]{1,0:T(8,128)(2,1)S(1)}, bf16[64,1024]{1,0:T(8,128)(2,1)}, u32[]{:S(2)}, u32[]{:S(2)}) collective-permute-start(bf16[64,1024]{1,0:T(8,128)(2,1)S(1)} %collective-permute-done.14.refs_11_), channel_id=1, source_target_pairs={{0,32},{16,48},{32,64},{48,80},{64,96},{80,112},{96,128},{112,144}... | collective-permute-start | bytes 393224 | tf_op jit(solution)/shard_map/ppermute | solution.py:290
  23.8 18.1 %collective-permute-start.7 = (bf16[192,768]{1,0:T(8,128)(2,1)S(1)}, bf16[192,768]{1,0:T(8,128)(2,1)}, u32[]{:S(2)}, u32[]{:S(2)}) collective-permute-start(bf16[192,768]{1,0:T(8,128)(2,1)S(1)} %pad_maximum_fusion.1.refs_2_), channel_id=1, source_target_pairs={{0,224},{16,240},{32,0},{48,16},{64,32},{80,48},{96,64},{112,80},{... | collective-permute-start | bytes 884744 | tf_op jit(solution)/shard_map/ppermute | solution.py:293
  29.5 7.4 %collective-permute-start.3 = (bf16[256,384]{1,0:T(8,128)(2,1)S(1)}, bf16[256,384]{1,0:T(8,128)(2,1)S(1)}, u32[]{:S(2)}, u32[]{:S(2)}) collective-permute-start(bf16[256,384]{1,0:T(8,128)(2,1)S(1)} %maximum_bitcast_fusion.1), channel_id=1, source_target_pairs={{0,4},{2,6},{4,0},{6,2},{8,12},{10,14},{12,8},{14,10},{1,5},{3,7},... | collective-permute-start | bytes 589832 | tf_op jit(solution)/shard_map/ppermute | solution.py:351
  33.2 8.7 %collective-permute-start.1 = (bf16[256,384]{1,0:T(8,128)(2,1)S(1)}, bf16[256,384]{1,0:T(8,128)(2,1)S(1)}, u32[]{:S(2)}, u32[]{:S(2)}) collective-permute-start(bf16[256,384]{1,0:T(8,128)(2,1)S(1)} %maximum_bitcast_fusion.1), channel_id=1, source_target_pairs={{0,2},{2,4},{4,6},{6,0},{8,10},{10,12},{12,14},{14,8},{1,3},{3,5},... | collective-permute-start | bytes 589832 | tf_op jit(solution)/shard_map/ppermute | solution.py:351
  34.3 10.4 %collective-permute-start.6 = (bf16[192,768]{1,0:T(8,128)(2,1)S(1)}, bf16[192,768]{1,0:T(8,128)(2,1)}, u32[]{:S(2)}, u32[]{:S(2)}) collective-permute-start(bf16[192,768]{1,0:T(8,128)(2,1)S(1)} %pad_maximum_fusion.1.refs_2_), channel_id=1, source_target_pairs={{0,32},{16,48},{32,64},{48,80},{64,96},{80,112},{96,128},{112,144}... | collective-permute-start | bytes 884744 | tf_op jit(solution)/shard_map/ppermute | solution.py:290
  36.9 22.7 %collective-permute-start.29 = (bf16[8,288,128]{2,1,0:T(8,128)(2,1)}, bf16[8,288,128]{2,1,0:T(8,128)(2,1)}, u32[]{:S(2)}, u32[]{:S(2)}) collective-permute-start(bf16[8,288,128]{2,1,0:T(8,128)(2,1)} %join.1.refs_19_), channel_id=1, source_target_pairs={{0,6},{2,0},{4,2},{6,4},{8,14},{10,8},{12,10},{14,12},{1,7},{3,1},... | collective-permute-start | bytes 1769480 | tf_op jit(solution)/shard_map/ppermute | solution.py:363
  39.2 12.1 %collective-permute-start.19 = (bf16[64,1024]{1,0:T(8,128)(2,1)S(1)}, bf16[64,1024]{1,0:T(8,128)(2,1)S(1)}, u32[]{:S(2)}, u32[]{:S(2)}) collective-permute-start(bf16[64,1024]{1,0:T(8,128)(2,1)S(1)} %collective-permute-done.17.refs_14_), channel_id=1, source_target_pairs={{0,224},{16,240},{32,0},{48,16},{64,32},{80,48},{96,64},{112,80},{... | collective-permute-start | bytes 393224 | tf_op jit(solution)/shard_map/ppermute | solution.py:293
  41.9 9.9 %collective-permute-start.18 = (bf16[64,1024]{1,0:T(8,128)(2,1)}, bf16[64,1024]{1,0:T(8,128)(2,1)S(1)}, u32[]{:S(2)}, u32[]{:S(2)}) collective-permute-start(bf16[64,1024]{1,0:T(8,128)(2,1)} %collective-permute-done.16.refs_13_), channel_id=1, source_target_pairs={{0,32},{16,48},{32,64},{48,80},{64,96},{80,112},{96,128},{112,144}... | collective-permute-start | bytes 393224 | tf_op jit(solution)/shard_map/ppermute | solution.py:290
  41.9 10.1 %collective-permute-start.9 = (bf16[192,768]{1,0:T(8,128)(2,1)}, bf16[192,768]{1,0:T(8,128)(2,1)S(1)}, u32[]{:S(2)}, u32[]{:S(2)}) collective-permute-start(bf16[192,768]{1,0:T(8,128)(2,1)} %collective-permute-done.7.refs_4_), channel_id=1, source_target_pairs={{0,224},{16,240},{32,0},{48,16},{64,32},{80,48},{96,64},{112,80},{... | collective-permute-start | bytes 884744 | tf_op jit(solution)/shard_map/ppermute | solution.py:293
  44.6 29.3 %collective-permute-start.32 = (bf16[8,288,128]{2,1,0:T(8,128)(2,1)}, bf16[8,288,128]{2,1,0:T(8,128)(2,1)S(1)}, u32[]{:S(2)}, u32[]{:S(2)}) collective-permute-start(bf16[8,288,128]{2,1,0:T(8,128)(2,1)} %join.1.refs_19_), channel_id=1, source_target_pairs={{0,16},{16,0},{32,48},{48,32},{64,80},{80,64},{96,112},{112,96},{1... | collective-permute-start | bytes 1769480 | tf_op jit(solution)/shard_map/ppermute | solution.py:299
  51.2 16.3 %collective-permute-start.28 = (bf16[8,288,128]{2,1,0:T(8,128)(2,1)}, bf16[8,288,128]{2,1,0:T(8,128)(2,1)}, u32[]{:S(2)}, u32[]{:S(2)}) collective-permute-start(bf16[8,288,128]{2,1,0:T(8,128)(2,1)} %join.1.refs_19_), channel_id=1, source_target_pairs={{0,2},{2,4},{4,6},{6,0},{8,10},{10,12},{12,14},{14,8},{1,3},{3,5},... | collective-permute-start | bytes 1769480 | tf_op jit(solution)/shard_map/ppermute | solution.py:362
  51.8 7.7 %collective-permute-start.8 = (bf16[192,768]{1,0:T(8,128)(2,1)}, bf16[192,768]{1,0:T(8,128)(2,1)S(1)}, u32[]{:S(2)}, u32[]{:S(2)}) collective-permute-start(bf16[192,768]{1,0:T(8,128)(2,1)} %collective-permute-done.6.refs_3_), channel_id=1, source_target_pairs={{0,32},{16,48},{32,64},{48,80},{64,96},{80,112},{96,128},{112,144}... | collective-permute-start | bytes 884744 | tf_op jit(solution)/shard_map/ppermute | solution.py:290
  52.0 24.8 %collective-permute-start.4 = (bf16[256,1536]{1,0:T(8,128)(2,1)S(1)}, bf16[256,1536]{1,0:T(8,128)(2,1)S(1)}, u32[]{:S(2)}, u32[]{:S(2)}) collective-permute-start(bf16[256,1536]{1,0:T(8,128)(2,1)S(1)} %pad_maximum_fusion.refs_0_), channel_id=1, source_target_pairs={{0,16},{16,0},{32,48},{48,32},{64,80},{80,64},{96,112},{112,96},{1... | collective-permute-start | bytes 2359304 | tf_op jit(solution)/shard_map/ppermute | solution.py:299
  59.6 14.5 %collective-permute-start.11 = (bf16[192,768]{1,0:T(8,128)(2,1)S(1)}, bf16[192,768]{1,0:T(8,128)(2,1)S(1)}, u32[]{:S(2)}, u32[]{:S(2)}) collective-permute-start(bf16[192,768]{1,0:T(8,128)(2,1)S(1)} %collective-permute-done.9.refs_6_), channel_id=1, source_target_pairs={{0,224},{16,240},{32,0},{48,16},{64,32},{80,48},{96,64},{112,80},{... | collective-permute-start | bytes 884744 | tf_op jit(solution)/shard_map/ppermute | solution.py:293
  59.6 17.1 %collective-permute-start.10 = (bf16[192,768]{1,0:T(8,128)(2,1)S(1)}, bf16[192,768]{1,0:T(8,128)(2,1)}, u32[]{:S(2)}, u32[]{:S(2)}) collective-permute-start(bf16[192,768]{1,0:T(8,128)(2,1)S(1)} %collective-permute-done.8.refs_5_), channel_id=1, source_target_pairs={{0,32},{16,48},{32,64},{48,80},{64,96},{80,112},{96,128},{112,144}... | collective-permute-start | bytes 884744 | tf_op jit(solution)/shard_map/ppermute | solution.py:290
  73.9 8.2 %collective-permute-start.30 = (bf16[4,288,128]{2,1,0:T(8,128)(2,1)S(1)}, bf16[4,288,128]{2,1,0:T(8,128)(2,1)}, u32[]{:S(2)}, u32[]{:S(2)}) collective-permute-start(bf16[4,288,128]{2,1,0:T(8,128)(2,1)S(1)} %slice.88), channel_id=1, source_target_pairs={{0,2},{2,4},{4,6},{6,0},{8,10},{10,12},{12,14},{14,8},{1,3},{3,5},... | collective-permute-start | bytes 884744 | tf_op jit(solution)/shard_map/ppermute | solution.py:364
  74.1 15.0 %collective-permute-start.34 = (bf16[8,288,128]{2,1,0:T(8,128)(2,1)}, bf16[8,288,128]{2,1,0:T(8,128)(2,1)}, u32[]{:S(2)}, u32[]{:S(2)}) collective-permute-start(bf16[8,288,128]{2,1,0:T(8,128)(2,1)} %collective-permute-done.29.refs_21_), channel_id=1, source_target_pairs={{0,16},{16,0},{32,48},{48,32},{64,80},{80,64},{96,112},{112,96},{1... | collective-permute-start | bytes 1769480 | tf_op jit(solution)/shard_map/ppermute | solution.py:299
  76.7 12.4 %collective-permute-start.33 = (bf16[8,288,128]{2,1,0:T(8,128)(2,1)}, bf16[8,288,128]{2,1,0:T(8,128)(2,1)}, u32[]{:S(2)}, u32[]{:S(2)}) collective-permute-start(bf16[8,288,128]{2,1,0:T(8,128)(2,1)} %collective-permute-done.28.refs_20_), channel_id=1, source_target_pairs={{0,16},{16,0},{32,48},{48,32},{64,80},{80,64},{96,112},{112,96},{1... | collective-permute-start | bytes 1769480 | tf_op jit(solution)/shard_map/ppermute | solution.py:299
  76.8 12.3 %collective-permute-start.12 = (bf16[192,768]{1,0:T(8,128)(2,1)}, bf16[192,768]{1,0:T(8,128)(2,1)}, u32[]{:S(2)}, u32[]{:S(2)}) collective-permute-start(bf16[192,768]{1,0:T(8,128)(2,1)} %collective-permute-done.10.refs_7_), channel_id=1, source_target_pairs={{0,32},{16,48},{32,64},{48,80},{64,96},{80,112},{96,128},{112,144}... | collective-permute-start | bytes 884744 | tf_op jit(solution)/shard_map/ppermute | solution.py:290
  79.1 9.9 %collective-permute-start.36 = (bf16[4,288,128]{2,1,0:T(8,128)(2,1)}, bf16[4,288,128]{2,1,0:T(8,128)(2,1)}, u32[]{:S(2)}, u32[]{:S(2)}) collective-permute-start(bf16[4,288,128]{2,1,0:T(8,128)(2,1)} %collective-permute-done.31.refs_23_), channel_id=1, source_target_pairs={{0,16},{16,0},{32,48},{48,32},{64,80},{80,64},{96,112},{112,96},{1... | collective-permute-start | bytes 884744 | tf_op jit(solution)/shard_map/ppermute | solution.py:299
  115.1 19.1 %all-to-all-start = ((f32[32,1,8]{2,1,0:T(1,128)}), f32[32,1,8]{2,1,0:T(1,128)S(1)}, u32[]{:S(2)}, u32[]{:S(2)}) async-start(f32[32,1,8]{2,1,0:T(1,128)} %broadcast_in_dim.9), calls=%async_computation | async-start | bytes 32768 | tf_op jit(solution)/shard_map/all_to_all | solution.py:311
  125.9 10.1 %collective-permute-start.37 = (bf16[256,512]{1,0:T(8,128)(2,1)S(1)}, bf16[256,512]{1,0:T(8,128)(2,1)S(1)}, u32[]{:S(2)}, u32[]{:S(2)}) collective-permute-start(bf16[256,512]{1,0:T(8,128)(2,1)S(1)} %slice.78), channel_id=1, source_target_pairs={{0,16},{16,0},{32,48},{48,32},{64,80},{80,64},{96,112},{112,96},{1... | collective-permute-start | bytes 786440 | tf_op jit(solution)/shard_map/ppermute | solution.py:299
  (44 other events, 506.0 us)
where the time goes:
time: 135 us; the launch traced here: 137 us
  starting transfers between devices  66.6 us (49%)
  waiting for transfers between devices  26.8 us (20%)
  Pallas kernels  26.3 us (19%)
  local copies, waits for them, and re-layouts  9.62 us (7%)
  other arithmetic  6.18 us (5%)
    pallas_call x1, Pallas kernels, on_device(): pl.pallas_call(attend_kernel, out_shape=[jax.ShapeDtypeStruct((512, 512),...  24.3 us
    ppermute x9, starting transfers between devices, ring(): dn = lax.ppermute(dn, 'seq', shift_seq(-1))  22.9 us
    ppermute x9, starting transfers between devices, swap(): return lax.ppermute(x, 'seq', SWAP)  22.4 us
    all_to_all x1, starting transfers between devices, of_everyone(): lax.all_to_all(copies, axis, split_axis=0, concat_axis=0, tiled=True)  9.82 us
    all_to_all x1, waiting for transfers between devices, of_everyone(): lax.all_to_all(copies, axis, split_axis=0, concat_axis=0, tiled=True)  7.98 us
    ppermute x12, waiting for transfers between devices, ring(): up = lax.ppermute(up, 'seq', shift_seq(1))  6.92 us
    ppermute x1, waiting for transfers between devices, on_device(): k_up = lax.ppermute(k_all, 'tp', shift_y(1))  6.5 us
    ppermute x3, starting transfers between devices, on_device(): lax.ppermute(q_x, 'tp', shift_y(by))  4.78 us
  transfers between devices with their start and end apart: 39, of which 7 were waited for; matrix products, arithmetic and copies ran while one was open for 9% of the time, Pallas kernels for 1%

commit v1 on v0

--- a/solution.py
+++ b/solution.py
@@ -23,27 +23,19 @@
 VMEM = pl.BlockSpec(memory_space=pltpu.VMEM)
 
 
-def meta_of(meta):
-    return dict(z=meta[35], c=meta[36], y=meta[37], xl=meta[38])
-
-
-def block_of(meta, i):
-    m = meta_of(meta)
-    half = i // 2
-    core = jnp.where(half == 0, m["c"], 1 - m["c"])
-    return meta[(m["z"] * 2 + core) * 2 + i % 2]
-
-
-def start_of(meta, p):
+def where_am_i():
+    s, t = lax.axis_index("seq"), lax.axis_index("tp")
+    return dict(z=s // 2, c=lax.rem(s, 2), y=lax.rem(t, 4), xl=t // 4)
+
+
+def start_of(bounds, p):
     s = jnp.int32(0)
-    for l in range(3):
-        b = meta[32 + l]
+    for b in bounds:
         s = jnp.where(b <= p, jnp.maximum(s, b), s)
     return s
 
 
-def feature_row(meta, t, each):
-    m = meta_of(meta)
+def feature_row(m, t, each):
     x, yy = t // 4, t % 4
     dy = lax.rem(yy - m["y"] + 4, 4)
     j = jnp.where(dy == 0, 0, jnp.where(dy == 1, 2, jnp.where(dy == 2, 3, 1)))
@@ -54,15 +46,78 @@
 RING = [0, -1, 1, -2, 2, -3, 3, -4]
 
 
+def split_kernel(q_t, k_t, w_uq, w_uk, w_uv, kq, w_mine, w_send, kv_mine, kv_send):
+    c = where_am_i()["c"]
+    kq[:64] = k_t[...]
+    kq[64:] = q_t[...]
+
+    def halves(own):
+        other = 1 - own
+        w_mine[...] = w_uq[:, own * 768 : own * 768 + 768]
+        w_send[...] = w_uq[:, other * 768 : other * 768 + 768]
+        for n in range(4):
+            for to, half in ((kv_mine, own), (kv_send, other)):
+                cols = slice(half * 512 + n * 128, half * 512 + n * 128 + 128)
+                to[n] = w_uk[:, cols]
+                to[4 + n] = w_uv[:, cols]
+
+    @pl.when(c == 0)
+    def _():
+        halves(0)
+
+    @pl.when(c == 1)
+    def _():
+        halves(1)
+
+
+def turn_kernel(order, rope_t, cs, share, fold):
+    m = where_am_i()
+    pos = []
+    lane = lax.broadcasted_iota(jnp.int32, (32, BLK), 1)
+    for i in range(4):
+        core = m["c"] if i < 2 else 1 - m["c"]
+        pos.append(lane + order[0, (m["z"] * 2 + core) * 2 + i % 2] * BLK)
+    steps = lax.broadcasted_iota(jnp.int32, (32, 512), 0).astype(jnp.float32) * (2.0 / ROPE)
+    freqs = jnp.exp(-math.log(rope_base) * steps)
+    angle = jnp.concatenate(pos, axis=1).astype(jnp.float32) * freqs
+    cos, sin = jnp.cos(angle), jnp.sin(angle)
+    cs[...] = jnp.concatenate([cos, cos, -sin, sin], axis=0).T
+    r = rope_t[...].astype(jnp.float32)
+    a, b, rc, rs = r[:32], r[32:], cos[:, :256], sin[:, :256]
+    both = jnp.concatenate([a * rc - b * rs, b * rc + a * rs], axis=0)
+    fold[...] = jnp.concatenate([both[:, :128], both[:, 128:]], axis=0).T.astype(jnp.bfloat16)
+    share[...] = fold[pl.ds(pl.multiple_of(m["y"] * 32, 32), 32), :]
+
+
+def rows_kernel(w_mine, w_other, wq):
+    c = where_am_i()["c"]
+    wq[pl.ds(pl.multiple_of(c * 96, 32), 96), :] = w_mine[...]
+    wq[pl.ds(pl.multiple_of((1 - c) * 96, 32), 96), :] = w_other[...]
+
+
+def pack_kernel(kq, kq_x, share, kv_mine, kv_other, k_one, q_x):
+    c = where_am_i()["c"]
+    k_one[:256] = jnp.concatenate([kq[:64], kq_x[:64]], axis=0).T
+    k_one[256:288] = share[...]
+    for n in range(8):
+        k_one[pl.ds(pl.multiple_of(288 + n * 64 + c * 32, 32), 32), :] = kv_mine[n]
+        k_one[pl.ds(pl.multiple_of(288 + n * 64 + (1 - c) * 32, 32), 32), :] = kv_other[n]
+    q_x[...] = jnp.concatenate([kq[64:], kq_x[64:]], axis=0).T
+
+
 def join_kernel(*refs):
-    for j in range(8):
-        refs[8][j] = refs[j][...]
-
-
-def label_of(meta, p):
+    ins, out, sem = refs[:8], refs[8], refs[9]
+    copies = [pltpu.make_async_copy(r.at[:288], out.at[j], sem.at[j]) for j, r in enumerate(ins)]
+    for cp in copies:
+        cp.start()
+    for cp in copies:
+        cp.wait()
+
+
+def label_of(bounds, p):
     label = jnp.zeros_like(p)
-    for l in range(3):
-        label = label + jnp.where(p >= meta[32 + l], 1, 0)
+    for b in bounds:
+        label = label + jnp.where(p >= b, 1, 0)
     return label
 
 
@@ -71,22 +126,34 @@
 to_exp2 = scale * math.log2(math.e)
 
 
-def attend_kernel(meta, *refs):
+def attend_kernel(order, seg, *refs):
     q_in, w_in, kv_in, cs, pieces = refs[:2], refs[2:10], refs[10:18], refs[18], (refs[19:24], refs[24:29])
     out, hm = refs[29:31]
     q, w, kvw, lat, rope, kn, v, kr, qs, sbuf, mx, rm, acc, total, step_i, step_ch, need = refs[31:48]
     qsem, wsem, kvsem, ksem = refs[48:]
-    m = meta_of(meta)
+    m = where_am_i()
+
+    def block_of(i):
+        core = jnp.where(i // 2 == 0, m["c"], 1 - m["c"])
+        return order[0, (m["z"] * 2 + core) * 2 + lax.rem(i, 2)]
+
     f32, bf16 = jnp.float32, jnp.bfloat16
     first, second = [], []
     for half in range(2):
         first.append(pltpu.make_async_copy(q_in[half], q.at[half], qsem.at[half]))
     for j in range(8):
         t = lax.rem(m["z"] + RING[j] + 8, 8)
-        row = pl.multiple_of(feature_row(meta, t, 192), 64)
+        row = pl.multiple_of(feature_row(m, t, 192), 64)
         first.append(pltpu.make_async_copy(w_in[j], w.at[pl.ds(row, 192)], wsem.at[j]))
-        row = pl.multiple_of(feature_row(meta, t, 64), 64)
-        second.append(pltpu.make_async_copy(kv_in[j], kvw.at[pl.ds(row, 64)], kvsem.at[j]))
+        row = pl.multiple_of(feature_row(m, t, 64), 64)
+        for n in range(8):
+            second.append(
+                pltpu.make_async_copy(
+                    kv_in[j].at[pl.ds(288 + n * 64, 64)],
+                    kvw.at[pl.ds(row, 64), pl.ds(n * 128, 128)],
+                    kvsem.at[j, n],
+                )
+            )
     for core in range(2):
         own, up, dn, f1, f2 = pieces[core]
         for n, (src, plane, start, count, dy) in enumerate(
@@ -105,12 +172,14 @@
     for cp in first + second:
         cp.start()
 
+    bounds = [jnp.sum(jnp.where(seg[...] < l, 1, 0)) for l in (1, 2, 3)]
+
     for n in range(16):
         need[n] = 0
     count = jnp.int32(0)
     for i in range(4):
-        pb = block_of(meta, i)
-        lo = start_of(meta, pb * BLK) // CHUNK
+        pb = block_of(i)
+        lo = start_of(bounds, pb * BLK) // CHUNK
         hi = pb // 2
         need[hi] = 1
 
@@ -122,7 +191,7 @@
 
         count = lax.fori_loop(lo, hi, add, count)
     step_i[count] = 3
-    step_ch[count] = block_of(meta, 3) // 2
+    step_ch[count] = block_of(3) // 2
     odd = lax.rem(count, 2)
 
     lane64 = lax.broadcasted_iota(jnp.int32, (BLK, 64), 1)
@@ -132,7 +201,7 @@
     for half in range(2):
         full = jnp.dot(q[half], w[...], preferred_element_type=f32)
         labels = [
-            jnp.where(label_of(meta, row64 + block_of(meta, half * 2 + b) * BLK) == lane64, 1.0, 0.0)
+            jnp.where(label_of(bounds, row64 + block_of(half * 2 + b) * BLK) == lane64, 1.0, 0.0)
             for b in range(2)
         ]
         onehot = jnp.concatenate(labels, axis=0).astype(bf16)
@@ -162,17 +231,17 @@
         cc = jnp.where(i < 8, m["c"], 1 - m["c"])
         base = (zz * 2 + cc) * 2
 
-        @pl.when((need[meta[base] // 2] + need[meta[base + 1] // 2]) > 0)
+        @pl.when((need[order[0, base] // 2] + need[order[0, base + 1] // 2]) > 0)
         def _():
             x = jnp.concatenate([lat[n, i] for n in range(4)], axis=1)
             y = jnp.dot(x, kvw[...], preferred_element_type=f32)
             fold = rope[i]
             for b in range(2):
-                pb = pl.multiple_of(meta[base + b] * BLK, BLK)
+                pb = pl.multiple_of(order[0, base + b] * BLK, BLK)
                 rows = slice(b * BLK, (b + 1) * BLK)
                 kn[pl.ds(pb, BLK), :] = y[rows, :512].astype(bf16)
                 v[pl.ds(pb, BLK), :] = y[rows, 512:].astype(bf16)
-                label = label_of(meta, row64 + pb)
+                label = label_of(bounds, row64 + pb)
                 apart = jnp.where((lane64 < 4) & (lane64 != label), masked_value, 0.0).astype(bf16)
                 kr[pl.ds(pb, BLK), :] = jnp.concatenate(
                     [fold[:, b * 64 : b * 64 + 64], apart], axis=1
@@ -200,7 +269,7 @@
         mx[i, h] = jnp.maximum(mx[i, h], jnp.maximum(s[:, :128], s[:, 128:]))
 
     def diagonal(i, carry):
-        pb = block_of(meta, i)
+        pb = block_of(i)
         ch = pb // 2
         row = lax.broadcasted_iota(jnp.int32, (BLK, CHUNK), 0) + (pb * BLK - ch * CHUNK)
         col = lax.broadcasted_iota(jnp.int32, (BLK, CHUNK), 1)
@@ -249,7 +318,7 @@
                 acc[i, h] += jnp.dot(p, v[keys, h * 128 : (h + 1) * 128], preferred_element_type=f32)
 
     def mix_diagonal(n, carry):
-        mix([(2 * n + e, block_of(meta, 2 * n + e) // 2, 2 * n + e) for e in range(2)])
+        mix([(2 * n + e, block_of(2 * n + e) // 2, 2 * n + e) for e in range(2)])
         return carry
 
     lax.fori_loop(0, 2, mix_diagonal, 0)
@@ -299,11 +368,18 @@
     return lax.ppermute(x, "seq", SWAP)
 
 
-def halves(w, c, width):
-    mine = lax.dynamic_slice_in_dim(w, c * width, width, 1)
-    other = swap(lax.dynamic_slice_in_dim(w, (1 - c) * width, width, 1))
-    first = c == 0
-    return jnp.concatenate([jnp.where(first, mine, other), jnp.where(first, other, mine)], axis=0)
+def call(kernel, outs, args, specs=None, scratch=(), name=None):
+    outs = [jax.ShapeDtypeStruct(shape, dtype) for shape, dtype in outs]
+    size = sum(math.prod(o.shape) * o.dtype.itemsize for o in outs)
+    return pl.pallas_call(
+        kernel,
+        out_shape=outs,
+        in_specs=specs or [VMEM] * len(args),
+        out_specs=[VMEM] * len(outs),
+        scratch_shapes=list(scratch),
+        cost_estimate=pl.CostEstimate(flops=1 << 20, bytes_accessed=2 * size, transcendentals=0),
+        name=name,
+    )(*args)
 
 
 def of_everyone(array, axis):
@@ -313,52 +389,45 @@
 
 def on_device(query_latent, key_latent, rope_key, w_uq, w_uk, w_uv, block_order, segment_ids):
     bf16, f32 = jnp.bfloat16, jnp.float32
-    s, t = lax.axis_index("seq"), lax.axis_index("tp")
-    z, c, y, xl = s // 2, s % 2, t % 4, t // 4
-    order, labels = block_order[0], segment_ids[0]
-    bounds = jnp.stack([jnp.sum((labels < l).astype(jnp.int32)) for l in (1, 2, 3)])
-    meta = jnp.concatenate(
-        [order, bounds, jnp.stack([z, c, y, xl]).astype(jnp.int32), jnp.zeros((9,), jnp.int32)]
-    )
-
-    wq = halves(w_uq, c, 768)
-    kv = halves(
-        jnp.concatenate([w_uk[:, :512], w_uv[:, :512], w_uk[:, 512:], w_uv[:, 512:]], axis=1), c, 1024
-    )
-    chip = lax.dynamic_slice_in_dim(order, 4 * z, 4)
-    chip = jnp.where(c == 0, chip, jnp.roll(chip, 2))
-    pos = (chip[:, None] * BLK + jnp.arange(BLK, dtype=jnp.int32)[None, :]).reshape(-1)
-    steps = jnp.arange(ROPE // 2, dtype=f32) * (2.0 / ROPE)
-    freqs = jnp.exp(-math.log(rope_base) * steps)
-    angle = pos.astype(f32)[:, None] * freqs[None, :]
-    cos, sin = jnp.cos(angle), jnp.sin(angle)
-    cs = jnp.concatenate([cos, cos, -sin, sin], axis=1)
-
-    kq = jnp.concatenate([key_latent[0].T, query_latent[0].T], axis=0)
+    c = where_am_i()["c"]
+    kq, w_mine, w_send, kv_mine, kv_send = call(
+        split_kernel,
+        [((256, 256), bf16)] + [((96, 768), bf16)] * 2 + [((8, 32, 128), bf16)] * 2,
+        (query_latent[0].T, key_latent[0].T, w_uq, w_uk, w_uv),
+        name="split",
+    )
     kq_x = lax.ppermute(kq, "tp", XSWAP)
-    k_x = jnp.concatenate([kq[:64], kq_x[:64]], axis=0).T
-    q_x = jnp.concatenate([kq[64:], kq_x[64:]], axis=0).T
-    rk = rope_key[0].astype(f32)
-    a, b = rk[:, :32], rk[:, 32:]
-    rc, rs = cos[:256], sin[:256]
-    k_rope = jnp.concatenate([a * rc - b * rs, b * rc + a * rs], axis=1).astype(bf16)
-    fold = jnp.concatenate([k_rope[:128], k_rope[128:]], axis=1)
-    k_one = jnp.concatenate([k_x, lax.dynamic_slice_in_dim(fold, y * 32, 32, 0)], axis=0)
-
+    w_other = swap(w_send)
+    kv_other = swap(kv_send)
+    cs, share = call(
+        turn_kernel,
+        [((512, 128), f32), ((32, 128), bf16)],
+        (block_order, rope_key[0].T),
+        specs=[SMEM, VMEM],
+        scratch=[pltpu.VMEM((128, 128), bf16)],
+        name="turn",
+    )
+    (wq,) = call(rows_kernel, [((192, 768), bf16)], (w_mine, w_other), name="rows")
+    k_one, q_x = call(
+        pack_kernel,
+        [((800, 128), bf16), ((256, 384), bf16)],
+        (kq, kq_x, share, kv_mine, kv_other),
+        name="pack",
+    )
+
+    w_ring = ring(wq)
     k_ring = ring(k_one)
-    kv_ring = ring(kv)
-    w_ring = ring(wq)
     q_parts = [q_x] + [lax.ppermute(q_x, "tp", shift_y(by)) for by in (1, -1, 2)]
     q_own = jnp.concatenate(q_parts, axis=1)
     q_sib = swap(q_own)
-    k_all = pl.pallas_call(
+    (k_all,) = call(
         join_kernel,
-        out_shape=jax.ShapeDtypeStruct((8, 288, 128), bf16),
-        in_specs=[VMEM] * 8,
-        out_specs=VMEM,
-        cost_estimate=pl.CostEstimate(flops=1 << 20, bytes_accessed=2 << 20, transcendentals=0),
+        [((8, 288, 128), bf16)],
+        k_ring,
+        specs=[ANY] * 8,
+        scratch=[pltpu.SemaphoreType.DMA((8,))],
         name="join",
-    )(*k_ring)
+    )
     k_up = lax.ppermute(k_all, "tp", shift_y(1))
     k_dn = lax.ppermute(k_all, "tp", shift_y(-1))
     k_f1 = lax.ppermute(k_up[:4], "tp", shift_y(1))
@@ -373,7 +442,7 @@
             jax.ShapeDtypeStruct((512, 512), bf16),
             jax.ShapeDtypeStruct((8, 128), f32),
         ],
-        in_specs=[SMEM] + [ANY] * 18 + [VMEM] + [ANY] * 10,
+        in_specs=[SMEM, VMEM] + [ANY] * 18 + [VMEM] + [ANY] * 10,
         out_specs=[VMEM] * 2,
         scratch_shapes=[
             vm((2, 256, 1536), bf16),
@@ -395,7 +464,7 @@
             pltpu.SMEM((16,), jnp.int32),
             pltpu.SemaphoreType.DMA((2,)),
             pltpu.SemaphoreType.DMA((8,)),
-            pltpu.SemaphoreType.DMA((8,)),
+            pltpu.SemaphoreType.DMA((8, 8)),
             pltpu.SemaphoreType.DMA((2, 5, 2)),
         ],
         compiler_params=pltpu.CompilerParams(vmem_limit_bytes=60 << 20),
@@ -403,7 +472,7 @@
             flops=20 << 30, bytes_accessed=12 << 20, transcendentals=4 << 20
         ),
         name="attend",
-    )(meta, q_own, q_sib, *w_ring, *kv_ring, cs, *k_own, *k_sib)
+    )(block_order, segment_ids[0].reshape(32, 128), q_own, q_sib, *w_ring, *k_ring, cs, *k_own, *k_sib)
 
     local_max = hm[:4, 0]
     low = jnp.full((4,), masked_value, f32)

time: 135 us -> 129 us (0.956); the launches traced: 137 us -> 129 us
  Pallas kernels: 26.3 us -> 32.1 us
  starting transfers between devices: 66.6 us -> 61.9 us
  local copies, waits for them, and re-layouts: 9.62 us -> 4.98 us
  other arithmetic: 6.18 us -> 2.47 us
    pallas_call x1 -> x5, Pallas kernels: 2 us -> 9.45 us  [call(): pl.pallas_call(kernel, out_shape=outs, in_specs=specs or [VMEM] * len(arg...]
    ppermute x9 -> x6, starting transfers between devices: 22.9 us -> 15.8 us  [ring(): dn = lax.ppermute(dn, 'seq', shift_seq(-1))]
    ppermute x1, waiting for transfers between devices: 6.5 us -> 1.78 us  [on_device(): k_up = lax.ppermute(k_all, 'tp', shift_y(1))]
    ppermute x9 -> x6, waiting for transfers between devices: 0.02 us -> 4.62 us  [ring(): dn = lax.ppermute(dn, 'seq', shift_seq(-1))]
    ppermute x1, waiting for transfers between devices: 2.99 us -> 0.01 us  [on_device(): kq_x = lax.ppermute(kq, 'tp', XSWAP)]
    concatenate x2 -> x1, local copies, waits for them, and re-layouts: 2.61 us -> 0.03 us  [on_device(): q_own = jnp.concatenate(q_parts, axis=1)]
    ppermute x1, waiting for transfers between devices: 2.32 us -> 0.01 us  [on_device(): k_f2 = lax.ppermute(k_dn[4:], 'tp', shift_y(-1))]
    ppermute x1, waiting for transfers between devices: 0.01 us -> 2.15 us  [on_device(): k_f1 = lax.ppermute(k_up[:4], 'tp', shift_y(1))]
  transfers between devices with their start and end apart: 39 -> 32, of which waited for: 7 -> 10; matrix products, arithmetic and copies ran while one was open for 9% -> 2% of each run, Pallas kernels for 1% -> 4%
where the time goes in v1:
time: 129 us
  starting transfers between devices  61.9 us (48%)
  Pallas kernels  32.1 us (25%)
  waiting for transfers between devices  26.5 us (21%)
  local copies, waits for them, and re-layouts  4.98 us (4%)
  other arithmetic  2.47 us (2%)
    pallas_call x1, Pallas kernels, on_device(): pl.pallas_call(attend_kernel, out_shape=[jax.ShapeDtypeStruct((512, 512),...  22.6 us
    ppermute x9, starting transfers between devices, swap(): return lax.ppermute(x, 'seq', SWAP)  20.3 us
    ppermute x6, starting transfers between devices, ring(): dn = lax.ppermute(dn, 'seq', shift_seq(-1))  15.8 us
    all_to_all x1, starting transfers between devices, of_everyone(): lax.all_to_all(copies, axis, split_axis=0, concat_axis=0, tiled=True)  11.5 us
    pallas_call x5, Pallas kernels, call(): pl.pallas_call(kernel, out_shape=outs, in_specs=specs or [VMEM] * len(arg...  9.45 us
    all_to_all x1, waiting for transfers between devices, of_everyone(): lax.all_to_all(copies, axis, split_axis=0, concat_axis=0, tiled=True)  7.91 us
    ppermute x8, waiting for transfers between devices, ring(): up = lax.ppermute(up, 'seq', shift_seq(1))  7.72 us
    ppermute x6, waiting for transfers between devices, ring(): dn = lax.ppermute(dn, 'seq', shift_seq(-1))  4.62 us
  transfers between devices with their start and end apart: 32, of which 10 were waited for; matrix products, arithmetic and copies ran while one was open for 2% of the time, Pallas kernels for 4%

profile of v1, /device:TPU:1, one launch (start us, length us, event | category | flops | bytes accessed | tf_op | source)
XLA Modules:
  0.0 128.8 jit_solution(11294873231530342412)
XLA Ops:
  0.6 1.9 %split.1 = (bf16[256,256]{1,0:T(8,128)(2,1)}, bf16[96,768]{1,0:T(8,128)(2,1)}, bf16[96,768]{1,0:T(8,128)(2,1)}, bf16[8,32,128]{2,1,0:T(8,128)(2,1)}, bf16[8,32,128]{2,1,0:T(8,128)(2,1)}) custom-call(bf16[192,256]{1,0:T(8,128)(2,1)} %bitcast.14, bf16[64,256]{1,0:T(8,128)(2,1)} %bitcast.15, bf16[96,1536]{1,0:T(8,128)(2,1)} %w_uq.1, bf16[32,1024]{1,0:T(8,128)(2,1)} %w_uk.1, ...), custom_call_target="tpu_custom_call" | custom-call | flops 1048576 | bytes 1114112 | tf_op jit(solution)/shard_map/split/pallas_call | solution.py:374
  2.6 2.0 %collective-permute-start = (bf16[256,256]{1,0:T(8,128)(2,1)}, bf16[256,256]{1,0:T(8,128)(2,1)S(1)}, u32[]{:S(2)}, u32[]{:S(2)}) collective-permute-start(bf16[256,256]{1,0:T(8,128)(2,1)} %get-tuple-element.14.kq), channel_id=1, source_target_pairs={{0,8},{2,10},{4,12},{6,14},{8,0},{10,2},{12,4},{14,6},{1,9},{3,11}... | collective-permute-start | bytes 393224 | tf_op jit(solution)/shard_map/ppermute | solution.py:399
  5.8 1.9 %turn.1 = (f32[512,128]{1,0:T(8,128)}, bf16[32,128]{1,0:T(8,128)(2,1)}) custom-call(s32[1,32]{1,0:T(1,128)} %order.3, bf16[64,256]{1,0:T(8,128)(2,1)} %bitcast.16), custom_call_target="tpu_custom_call" | custom-call | flops 1048576 | bytes 540672 | tf_op jit(solution)/shard_map/turn/pallas_call | solution.py:374
  8.3 1.9 %pack.1 = (bf16[800,128]{1,0:T(8,128)(2,1)}, bf16[256,384]{1,0:T(8,128)(2,1)}) custom-call(bf16[256,256]{1,0:T(8,128)(2,1)} %get-tuple-element.14.kq, bf16[256,256]{1,0:T(8,128)(2,1)} %copy-done.15, bf16[32,128]{1,0:T(8,128)(2,1)} %get-tuple-element.15.share, bf16[8,32,128]{2,1,0:T(8,128)(2,1)} %get-tuple-element.16.kv_mine, bf16[8,32,128]{2,1,0:T(8,128)(2,1)} %copy-done.16), custom_call_target="tpu_custom_call" | custom-call | flops 1048576 | bytes 802816 | tf_op jit(solution)/shard_map/pack/pallas_call | solution.py:374
  10.2 1.9 %collective-permute-start.14 = (bf16[800,128]{1,0:T(8,128)(2,1)}, bf16[800,128]{1,0:T(8,128)(2,1)S(1)}, u32[]{:S(2)}, u32[]{:S(2)}) collective-permute-start(bf16[800,128]{1,0:T(8,128)(2,1)} %get-tuple-element.21.refs_0_.refs_10_), channel_id=1, source_target_pairs={{0,32},{16,48},{32,64},{48,80},{64,96},{80,112},{96,128},{112,144}... | collective-permute-start | bytes 614408 | tf_op jit(solution)/shard_map/ppermute | solution.py:359
  13.9 3.7 %collective-permute-start.15 = (bf16[800,128]{1,0:T(8,128)(2,1)}, bf16[800,128]{1,0:T(8,128)(2,1)S(1)}, u32[]{:S(2)}, u32[]{:S(2)}) collective-permute-start(bf16[800,128]{1,0:T(8,128)(2,1)} %get-tuple-element.21.refs_0_.refs_10_), channel_id=1, source_target_pairs={{0,224},{16,240},{32,0},{48,16},{64,32},{80,48},{96,64},{112,80},{... | collective-permute-start | bytes 614408 | tf_op jit(solution)/shard_map/ppermute | solution.py:362
  17.7 2.5 %collective-permute-done.14.refs_1_.refs_11_ = bf16[800,128]{1,0:T(8,128)(2,1)S(1)} collective-permute-done((bf16[800,128]{1,0:T(8,128)(2,1)}, bf16[800,128]{1,0:T(8,128)(2,1)S(1)}, u32[]{:S(2)}, u32[]{:S(2)}) %collective-permute-start.14) | collective-permute-done | bytes 204832 | tf_op jit(solution)/shard_map/ppermute | solution.py:359
  27.9 3.0 %collective-permute-start.17 = (bf16[800,128]{1,0:T(8,128)(2,1)S(1)}, bf16[800,128]{1,0:T(8,128)(2,1)S(1)}, u32[]{:S(2)}, u32[]{:S(2)}) collective-permute-start(bf16[800,128]{1,0:T(8,128)(2,1)S(1)} %collective-permute-done.15.refs_2_.refs_12_), channel_id=1, source_target_pairs={{0,224},{16,240},{32,0},{48,16},{64,32},{80,48},{96,64},{112,80},{... | collective-permute-start | bytes 614408 | tf_op jit(solution)/shard_map/ppermute | solution.py:362
  30.9 2.7 %collective-permute-start.8 = (bf16[192,768]{1,0:T(8,128)(2,1)S(1)}, bf16[192,768]{1,0:T(8,128)(2,1)}, u32[]{:S(2)}, u32[]{:S(2)}) collective-permute-start(bf16[192,768]{1,0:T(8,128)(2,1)S(1)} %copy-done.2), channel_id=1, source_target_pairs={{0,224},{16,240},{32,0},{48,16},{64,32},{80,48},{96,64},{112,80},{... | collective-permute-start | bytes 884744 | tf_op jit(solution)/shard_map/ppermute | solution.py:362
  33.8 2.8 %collective-permute-start.19 = (bf16[800,128]{1,0:T(8,128)(2,1)S(1)}, bf16[800,128]{1,0:T(8,128)(2,1)S(1)}, u32[]{:S(2)}, u32[]{:S(2)}) collective-permute-start(bf16[800,128]{1,0:T(8,128)(2,1)S(1)} %collective-permute-done.17.refs_4_.refs_14_), channel_id=1, source_target_pairs={{0,224},{16,240},{32,0},{48,16},{64,32},{80,48},{96,64},{112,80},{... | collective-permute-start | bytes 614408 | tf_op jit(solution)/shard_map/ppermute | solution.py:362
  37.9 6.1 %collective-permute-start.5 = (bf16[256,1536]{1,0:T(8,128)(2,1)S(1)}, bf16[256,1536]{1,0:T(8,128)(2,1)S(1)}, u32[]{:S(2)}, u32[]{:S(2)}) collective-permute-start(bf16[256,1536]{1,0:T(8,128)(2,1)S(1)} %constant_dynamic-update-slice_fusion.refs_0_), channel_id=1, source_target_pairs={{0,16},{16,0},{32,48},{48,32},{64,80},{80,64},{96,112},{112,96},{1... | collective-permute-start | bytes 2359304 | tf_op jit(solution)/shard_map/ppermute | solution.py:368
  44.0 4.0 %collective-permute-done.20.refs_7_.refs_17_ = bf16[800,128]{1,0:T(8,128)(2,1)S(1)} collective-permute-done((bf16[800,128]{1,0:T(8,128)(2,1)S(1)}, bf16[800,128]{1,0:T(8,128)(2,1)S(1)}, u32[]{:S(2)}, u32[]{:S(2)}) %collective-permute-start.20) | collective-permute-done | bytes 204832 | tf_op jit(solution)/shard_map/ppermute | solution.py:359
  48.7 2.0 %join.1.refs_19_ = bf16[8,288,128]{2,1,0:T(8,128)(2,1)} custom-call(bf16[800,128]{1,0:T(8,128)(2,1)} %get-tuple-element.21.refs_0_.refs_10_, bf16[800,128]{1,0:T(8,128)(2,1)} %copy-done.4, bf16[800,128]{1,0:T(8,128)(2,1)} %copy-done.5, bf16[800,128]{1,0:T(8,128)(2,1)} %copy-done.6, bf16[800,128]{1,0:T(8,128)(2,1)} %copy-done.7, bf16[800,128]{1,0:T(8,128)(2,1)} %copy-done.8, ...), custom_call_target="tpu_custom_call" | custom-call | flops 1048576 | bytes 1179648 | tf_op jit(solution)/shard_map/join/pallas_call | solution.py:374
  51.5 2.0 %collective-permute-start.22 = (bf16[8,288,128]{2,1,0:T(8,128)(2,1)}, bf16[8,288,128]{2,1,0:T(8,128)(2,1)S(1)}, u32[]{:S(2)}, u32[]{:S(2)}) collective-permute-start(bf16[8,288,128]{2,1,0:T(8,128)(2,1)} %join.1.refs_19_), channel_id=1, source_target_pairs={{0,6},{2,0},{4,2},{6,4},{8,14},{10,8},{12,10},{14,12},{1,7},{3,1},... | collective-permute-start | bytes 1769480 | tf_op jit(solution)/shard_map/ppermute | solution.py:432
  55.0 4.6 %collective-permute-done.10.refs_6_ = bf16[192,768]{1,0:T(8,128)(2,1)S(1)} collective-permute-done((bf16[192,768]{1,0:T(8,128)(2,1)}, bf16[192,768]{1,0:T(8,128)(2,1)S(1)}, u32[]{:S(2)}, u32[]{:S(2)}) %collective-permute-start.10) | collective-permute-done | bytes 294944 | tf_op jit(solution)/shard_map/ppermute | solution.py:362
  59.6 2.4 %collective-permute-start.12 = (bf16[192,768]{1,0:T(8,128)(2,1)S(1)}, bf16[192,768]{1,0:T(8,128)(2,1)S(1)}, u32[]{:S(2)}, u32[]{:S(2)}) collective-permute-start(bf16[192,768]{1,0:T(8,128)(2,1)S(1)} %collective-permute-done.10.refs_6_), channel_id=1, source_target_pairs={{0,224},{16,240},{32,0},{48,16},{64,32},{80,48},{96,64},{112,80},{... | collective-permute-start | bytes 884744 | tf_op jit(solution)/shard_map/ppermute | solution.py:362
  63.7 4.7 %collective-permute-start.25 = (bf16[8,288,128]{2,1,0:T(8,128)(2,1)}, bf16[8,288,128]{2,1,0:T(8,128)(2,1)}, u32[]{:S(2)}, u32[]{:S(2)}) collective-permute-start(bf16[8,288,128]{2,1,0:T(8,128)(2,1)} %join.1.refs_19_), channel_id=1, source_target_pairs={{0,16},{16,0},{32,48},{48,32},{64,80},{80,64},{96,112},{112,96},{1... | collective-permute-start | bytes 1769480 | tf_op jit(solution)/shard_map/ppermute | solution.py:368
  68.6 2.7 %collective-permute-start.24 = (bf16[4,288,128]{2,1,0:T(8,128)(2,1)S(1)}, bf16[4,288,128]{2,1,0:T(8,128)(2,1)}, u32[]{:S(2)}, u32[]{:S(2)}) collective-permute-start(bf16[4,288,128]{2,1,0:T(8,128)(2,1)S(1)} %slice.21), channel_id=1, source_target_pairs={{0,6},{2,0},{4,2},{6,4},{8,14},{10,8},{12,10},{14,12},{1,7},{3,1},... | collective-permute-start | bytes 884744 | tf_op jit(solution)/shard_map/ppermute | solution.py:434
  71.3 2.7 %collective-permute-start.26 = (bf16[8,288,128]{2,1,0:T(8,128)(2,1)S(1)}, bf16[8,288,128]{2,1,0:T(8,128)(2,1)}, u32[]{:S(2)}, u32[]{:S(2)}) collective-permute-start(bf16[8,288,128]{2,1,0:T(8,128)(2,1)S(1)} %collective-permute-done.21.refs_20_), channel_id=1, source_target_pairs={{0,16},{16,0},{32,48},{48,32},{64,80},{80,64},{96,112},{112,96},{1... | collective-permute-start | bytes 1769480 | tf_op jit(solution)/shard_map/ppermute | solution.py:368
  74.0 2.2 %collective-permute-start.27 = (bf16[8,288,128]{2,1,0:T(8,128)(2,1)S(1)}, bf16[8,288,128]{2,1,0:T(8,128)(2,1)}, u32[]{:S(2)}, u32[]{:S(2)}) collective-permute-start(bf16[8,288,128]{2,1,0:T(8,128)(2,1)S(1)} %collective-permute-done.22.refs_21_), channel_id=1, source_target_pairs={{0,16},{16,0},{32,48},{48,32},{64,80},{80,64},{96,112},{112,96},{1... | collective-permute-start | bytes 1769480 | tf_op jit(solution)/shard_map/ppermute | solution.py:368
  76.2 2.2 %collective-permute-done.23.refs_22_ = bf16[4,288,128]{2,1,0:T(8,128)(2,1)} collective-permute-done((bf16[4,288,128]{2,1,0:T(8,128)(2,1)S(1)}, bf16[4,288,128]{2,1,0:T(8,128)(2,1)}, u32[]{:S(2)}, u32[]{:S(2)}) %collective-permute-start.23) | collective-permute-done | bytes 294944 | tf_op jit(solution)/shard_map/ppermute | solution.py:433
  81.3 22.6 %attend.1 = (bf16[512,512]{1,0:T(8,128)(2,1)}, f32[8,128]{1,0:T(8,128)}) custom-call(s32[1,32]{1,0:T(1,128)} %order.3, s32[32,128]{1,0:T(8,128)} %bitcast.17, bf16[256,1536]{1,0:T(8,128)(2,1)} %copy-done.17, bf16[256,1536]{1,0:T(8,128)(2,1)} %copy-done.18, bf16[192,768]{1,0:T(8,128)(2,1)} %rows.1.refs_2_, bf16[192,768]{1,0:T(8,128)(2,1)} %collective-permute-done.7.refs_3_, ...), custom_call_target="tpu_custom_call" | custom-call | flops 21474836480 | bytes 12582912 | tf_op jit(solution)/shard_map/attend/pallas_call | solution.py:439
  105.4 11.5 %all-to-all-start = ((f32[32,1,8]{2,1,0:T(1,128)}), f32[32,1,8]{2,1,0:T(1,128)S(1)}, u32[]{:S(2)}, u32[]{:S(2)}) async-start(f32[32,1,8]{2,1,0:T(1,128)} %broadcast_in_dim.9), calls=%async_computation | async-start | bytes 32768 | tf_op jit(solution)/shard_map/all_to_all | solution.py:387
  118.2 7.9 %all-to-all-done = f32[32,1,8]{2,1,0:T(1,128)S(1)} async-done(((f32[32,1,8]{2,1,0:T(1,128)}), f32[32,1,8]{2,1,0:T(1,128)S(1)}, u32[]{:S(2)}, u32[]{:S(2)}) %all-to-all-start) | async-done | bytes 1056 | tf_op jit(solution)/shard_map/all_to_all | solution.py:387
  (115 shorter events, 26.0 us)
Async XLA Ops:
  10.2 10.0 %collective-permute-start.14 = (bf16[800,128]{1,0:T(8,128)(2,1)}, bf16[800,128]{1,0:T(8,128)(2,1)S(1)}, u32[]{:S(2)}, u32[]{:S(2)}) collective-permute-start(bf16[800,128]{1,0:T(8,128)(2,1)} %get-tuple-element.21.refs_0_.refs_10_), channel_id=1, source_target_pairs={{0,32},{16,48},{32,64},{48,80},{64,96},{80,112},{96,128},{112,144}... | collective-permute-start | bytes 614408 | tf_op jit(solution)/shard_map/ppermute | solution.py:359
  12.1 10.9 %collective-permute-start.6 = (bf16[96,768]{1,0:T(8,128)(2,1)S(1)}, bf16[96,768]{1,0:T(8,128)(2,1)S(1)}, u32[]{:S(2)}, u32[]{:S(2)}) collective-permute-start(bf16[96,768]{1,0:T(8,128)(2,1)S(1)} %copy-done.23), channel_id=1, source_target_pairs={{0,16},{16,0},{32,48},{48,32},{64,80},{80,64},{96,112},{112,96},{1... | collective-permute-start | bytes 442376 | tf_op jit(solution)/shard_map/ppermute | solution.py:368
  13.9 13.9 %collective-permute-start.15 = (bf16[800,128]{1,0:T(8,128)(2,1)}, bf16[800,128]{1,0:T(8,128)(2,1)S(1)}, u32[]{:S(2)}, u32[]{:S(2)}) collective-permute-start(bf16[800,128]{1,0:T(8,128)(2,1)} %get-tuple-element.21.refs_0_.refs_10_), channel_id=1, source_target_pairs={{0,224},{16,240},{32,0},{48,16},{64,32},{80,48},{96,64},{112,80},{... | collective-permute-start | bytes 614408 | tf_op jit(solution)/shard_map/ppermute | solution.py:362
  20.2 10.6 %collective-permute-start.16 = (bf16[800,128]{1,0:T(8,128)(2,1)S(1)}, bf16[800,128]{1,0:T(8,128)(2,1)S(1)}, u32[]{:S(2)}, u32[]{:S(2)}) collective-permute-start(bf16[800,128]{1,0:T(8,128)(2,1)S(1)} %collective-permute-done.14.refs_1_.refs_11_), channel_id=1, source_target_pairs={{0,32},{16,48},{32,64},{48,80},{64,96},{80,112},{96,128},{112,144}... | collective-permute-start | bytes 614408 | tf_op jit(solution)/shard_map/ppermute | solution.py:359
  21.5 9.4 %collective-permute-start.3 = (bf16[256,384]{1,0:T(8,128)(2,1)}, bf16[256,384]{1,0:T(8,128)(2,1)S(1)}, u32[]{:S(2)}, u32[]{:S(2)}) collective-permute-start(bf16[256,384]{1,0:T(8,128)(2,1)} %get-tuple-element.18), channel_id=1, source_target_pairs={{0,6},{2,0},{4,2},{6,4},{8,14},{10,8},{12,10},{14,12},{1,7},{3,1},... | collective-permute-start | bytes 589832 | tf_op jit(solution)/shard_map/ppermute | solution.py:420
  25.4 8.2 %collective-permute-start.7 = (bf16[192,768]{1,0:T(8,128)(2,1)}, bf16[192,768]{1,0:T(8,128)(2,1)}, u32[]{:S(2)}, u32[]{:S(2)}) collective-permute-start(bf16[192,768]{1,0:T(8,128)(2,1)} %rows.1.refs_2_), channel_id=1, source_target_pairs={{0,32},{16,48},{32,64},{48,80},{64,96},{80,112},{96,128},{112,144}... | collective-permute-start | bytes 884744 | tf_op jit(solution)/shard_map/ppermute | solution.py:359
  26.2 11.6 %collective-permute-start.4 = (bf16[256,384]{1,0:T(8,128)(2,1)S(1)}, bf16[256,384]{1,0:T(8,128)(2,1)S(1)}, u32[]{:S(2)}, u32[]{:S(2)}) collective-permute-start(bf16[256,384]{1,0:T(8,128)(2,1)S(1)} %copy-done.11), channel_id=1, source_target_pairs={{0,4},{2,6},{4,0},{6,2},{8,12},{10,14},{12,8},{14,10},{1,5},{3,7},... | collective-permute-start | bytes 589832 | tf_op jit(solution)/shard_map/ppermute | solution.py:420
  30.9 22.6 %collective-permute-start.8 = (bf16[192,768]{1,0:T(8,128)(2,1)S(1)}, bf16[192,768]{1,0:T(8,128)(2,1)}, u32[]{:S(2)}, u32[]{:S(2)}) collective-permute-start(bf16[192,768]{1,0:T(8,128)(2,1)S(1)} %copy-done.2), channel_id=1, source_target_pairs={{0,224},{16,240},{32,0},{48,16},{64,32},{80,48},{96,64},{112,80},{... | collective-permute-start | bytes 884744 | tf_op jit(solution)/shard_map/ppermute | solution.py:362
  33.7 20.9 %collective-permute-start.9 = (bf16[192,768]{1,0:T(8,128)(2,1)}, bf16[192,768]{1,0:T(8,128)(2,1)}, u32[]{:S(2)}, u32[]{:S(2)}) collective-permute-start(bf16[192,768]{1,0:T(8,128)(2,1)} %collective-permute-done.7.refs_3_), channel_id=1, source_target_pairs={{0,32},{16,48},{32,64},{48,80},{64,96},{80,112},{96,128},{112,144}... | collective-permute-start | bytes 884744 | tf_op jit(solution)/shard_map/ppermute | solution.py:359
  33.8 10.1 %collective-permute-start.19 = (bf16[800,128]{1,0:T(8,128)(2,1)S(1)}, bf16[800,128]{1,0:T(8,128)(2,1)S(1)}, u32[]{:S(2)}, u32[]{:S(2)}) collective-permute-start(bf16[800,128]{1,0:T(8,128)(2,1)S(1)} %collective-permute-done.17.refs_4_.refs_14_), channel_id=1, source_target_pairs={{0,224},{16,240},{32,0},{48,16},{64,32},{80,48},{96,64},{112,80},{... | collective-permute-start | bytes 614408 | tf_op jit(solution)/shard_map/ppermute | solution.py:362
  37.8 10.2 %collective-permute-start.20 = (bf16[800,128]{1,0:T(8,128)(2,1)S(1)}, bf16[800,128]{1,0:T(8,128)(2,1)S(1)}, u32[]{:S(2)}, u32[]{:S(2)}) collective-permute-start(bf16[800,128]{1,0:T(8,128)(2,1)S(1)} %collective-permute-done.18.refs_5_.refs_15_), channel_id=1, source_target_pairs={{0,32},{16,48},{32,64},{48,80},{64,96},{80,112},{96,128},{112,144}... | collective-permute-start | bytes 614408 | tf_op jit(solution)/shard_map/ppermute | solution.py:359
  37.9 33.4 %collective-permute-start.5 = (bf16[256,1536]{1,0:T(8,128)(2,1)S(1)}, bf16[256,1536]{1,0:T(8,128)(2,1)S(1)}, u32[]{:S(2)}, u32[]{:S(2)}) collective-permute-start(bf16[256,1536]{1,0:T(8,128)(2,1)S(1)} %constant_dynamic-update-slice_fusion.refs_0_), channel_id=1, source_target_pairs={{0,16},{16,0},{32,48},{48,32},{64,80},{80,64},{96,112},{112,96},{1... | collective-permute-start | bytes 2359304 | tf_op jit(solution)/shard_map/ppermute | solution.py:368
  50.7 13.0 %collective-permute-start.21 = (bf16[8,288,128]{2,1,0:T(8,128)(2,1)}, bf16[8,288,128]{2,1,0:T(8,128)(2,1)S(1)}, u32[]{:S(2)}, u32[]{:S(2)}) collective-permute-start(bf16[8,288,128]{2,1,0:T(8,128)(2,1)} %join.1.refs_19_), channel_id=1, source_target_pairs={{0,2},{2,4},{4,6},{6,0},{8,10},{10,12},{12,14},{14,8},{1,3},{3,5},... | collective-permute-start | bytes 1769480 | tf_op jit(solution)/shard_map/ppermute | solution.py:431
  51.5 16.9 %collective-permute-start.22 = (bf16[8,288,128]{2,1,0:T(8,128)(2,1)}, bf16[8,288,128]{2,1,0:T(8,128)(2,1)S(1)}, u32[]{:S(2)}, u32[]{:S(2)}) collective-permute-start(bf16[8,288,128]{2,1,0:T(8,128)(2,1)} %join.1.refs_19_), channel_id=1, source_target_pairs={{0,6},{2,0},{4,2},{6,4},{8,14},{10,8},{12,10},{14,12},{1,7},{3,1},... | collective-permute-start | bytes 1769480 | tf_op jit(solution)/shard_map/ppermute | solution.py:432
  54.7 7.3 %collective-permute-start.11 = (bf16[192,768]{1,0:T(8,128)(2,1)}, bf16[192,768]{1,0:T(8,128)(2,1)S(1)}, u32[]{:S(2)}, u32[]{:S(2)}) collective-permute-start(bf16[192,768]{1,0:T(8,128)(2,1)} %collective-permute-done.9.refs_5_), channel_id=1, source_target_pairs={{0,32},{16,48},{32,64},{48,80},{64,96},{80,112},{96,128},{112,144}... | collective-permute-start | bytes 884744 | tf_op jit(solution)/shard_map/ppermute | solution.py:359
  59.6 9.0 %collective-permute-start.12 = (bf16[192,768]{1,0:T(8,128)(2,1)S(1)}, bf16[192,768]{1,0:T(8,128)(2,1)S(1)}, u32[]{:S(2)}, u32[]{:S(2)}) collective-permute-start(bf16[192,768]{1,0:T(8,128)(2,1)S(1)} %collective-permute-done.10.refs_6_), channel_id=1, source_target_pairs={{0,224},{16,240},{32,0},{48,16},{64,32},{80,48},{96,64},{112,80},{... | collective-permute-start | bytes 884744 | tf_op jit(solution)/shard_map/ppermute | solution.py:362
  61.9 12.1 %collective-permute-start.13 = (bf16[192,768]{1,0:T(8,128)(2,1)S(1)}, bf16[192,768]{1,0:T(8,128)(2,1)S(1)}, u32[]{:S(2)}, u32[]{:S(2)}) collective-permute-start(bf16[192,768]{1,0:T(8,128)(2,1)S(1)} %collective-permute-done.11.refs_7_), channel_id=1, source_target_pairs={{0,32},{16,48},{32,64},{48,80},{64,96},{80,112},{96,128},{112,144}... | collective-permute-start | bytes 884744 | tf_op jit(solution)/shard_map/ppermute | solution.py:359
  63.7 15.9 %collective-permute-start.25 = (bf16[8,288,128]{2,1,0:T(8,128)(2,1)}, bf16[8,288,128]{2,1,0:T(8,128)(2,1)}, u32[]{:S(2)}, u32[]{:S(2)}) collective-permute-start(bf16[8,288,128]{2,1,0:T(8,128)(2,1)} %join.1.refs_19_), channel_id=1, source_target_pairs={{0,16},{16,0},{32,48},{48,32},{64,80},{80,64},{96,112},{112,96},{1... | collective-permute-start | bytes 1769480 | tf_op jit(solution)/shard_map/ppermute | solution.py:368
  68.4 9.9 %collective-permute-start.23 = (bf16[4,288,128]{2,1,0:T(8,128)(2,1)S(1)}, bf16[4,288,128]{2,1,0:T(8,128)(2,1)}, u32[]{:S(2)}, u32[]{:S(2)}) collective-permute-start(bf16[4,288,128]{2,1,0:T(8,128)(2,1)S(1)} %slice.20), channel_id=1, source_target_pairs={{0,2},{2,4},{4,6},{6,0},{8,10},{10,12},{12,14},{14,8},{1,3},{3,5},... | collective-permute-start | bytes 884744 | tf_op jit(solution)/shard_map/ppermute | solution.py:433
  68.6 10.7 %collective-permute-start.24 = (bf16[4,288,128]{2,1,0:T(8,128)(2,1)S(1)}, bf16[4,288,128]{2,1,0:T(8,128)(2,1)}, u32[]{:S(2)}, u32[]{:S(2)}) collective-permute-start(bf16[4,288,128]{2,1,0:T(8,128)(2,1)S(1)} %slice.21), channel_id=1, source_target_pairs={{0,6},{2,0},{4,2},{6,4},{8,14},{10,8},{12,10},{14,12},{1,7},{3,1},... | collective-permute-start | bytes 884744 | tf_op jit(solution)/shard_map/ppermute | solution.py:434
  71.3 9.9 %collective-permute-start.26 = (bf16[8,288,128]{2,1,0:T(8,128)(2,1)S(1)}, bf16[8,288,128]{2,1,0:T(8,128)(2,1)}, u32[]{:S(2)}, u32[]{:S(2)}) collective-permute-start(bf16[8,288,128]{2,1,0:T(8,128)(2,1)S(1)} %collective-permute-done.21.refs_20_), channel_id=1, source_target_pairs={{0,16},{16,0},{32,48},{48,32},{64,80},{80,64},{96,112},{112,96},{1... | collective-permute-start | bytes 1769480 | tf_op jit(solution)/shard_map/ppermute | solution.py:368
  74.0 7.2 %collective-permute-start.27 = (bf16[8,288,128]{2,1,0:T(8,128)(2,1)S(1)}, bf16[8,288,128]{2,1,0:T(8,128)(2,1)}, u32[]{:S(2)}, u32[]{:S(2)}) collective-permute-start(bf16[8,288,128]{2,1,0:T(8,128)(2,1)S(1)} %collective-permute-done.22.refs_21_), channel_id=1, source_target_pairs={{0,16},{16,0},{32,48},{48,32},{64,80},{80,64},{96,112},{112,96},{1... | collective-permute-start | bytes 1769480 | tf_op jit(solution)/shard_map/ppermute | solution.py:368
  105.4 20.7 %all-to-all-start = ((f32[32,1,8]{2,1,0:T(1,128)}), f32[32,1,8]{2,1,0:T(1,128)S(1)}, u32[]{:S(2)}, u32[]{:S(2)}) async-start(f32[32,1,8]{2,1,0:T(1,128)} %broadcast_in_dim.9), calls=%async_computation | async-start | bytes 32768 | tf_op jit(solution)/shard_map/all_to_all | solution.py:387
  117.9 10.0 %collective-permute-start.30 = (bf16[256,512]{1,0:T(8,128)(2,1)S(1)}, bf16[256,512]{1,0:T(8,128)(2,1)S(1)}, u32[]{:S(2)}, u32[]{:S(2)}) collective-permute-start(bf16[256,512]{1,0:T(8,128)(2,1)S(1)} %slice.18), channel_id=1, source_target_pairs={{0,16},{16,0},{32,48},{48,32},{64,80},{80,64},{96,112},{112,96},{1... | collective-permute-start | bytes 786440 | tf_op jit(solution)/shard_map/ppermute | solution.py:368
  (32 other events, 243.5 us)

commit v2 on v1

--- a/solution.py
+++ b/solution.py
@@ -7,9 +7,9 @@
 from jax.experimental.pallas import tpu as pltpu
 from jax.sharding import PartitionSpec as P
 
+
 NOPE = 128
 ROPE = 64
-VD = 128
 CLIP = 8
 BLK = 128
 CHUNK = 256
@@ -46,17 +46,29 @@
 RING = [0, -1, 1, -2, 2, -3, 3, -4]
 
 
+W_COLS = [[h * 192 + e * 32 for e in range(4)] for h in range(4)] + [
+    [h * 192 + 128 for h in range(4)],
+    [h * 192 + 160 for h in range(4)],
+]
+
+
 def split_kernel(q_t, k_t, w_uq, w_uk, w_uv, kq, w_mine, w_send, kv_mine, kv_send):
     c = where_am_i()["c"]
     kq[:64] = k_t[...]
     kq[64:] = q_t[...]
 
     def halves(own):
-        other = 1 - own
-        w_mine[...] = w_uq[:, own * 768 : own * 768 + 768]
-        w_send[...] = w_uq[:, other * 768 : other * 768 + 768]
-        for n in range(4):
-            for to, half in ((kv_mine, own), (kv_send, other)):
+        for to, half in ((w_mine, own), (w_send, 1 - own)):
+            for n, cols in enumerate(W_COLS):
+                base = half * 768
+                if n < 4:
+                    block = w_uq[:, base + cols[0] : base + cols[0] + 128]
+                else:
+                    block = jnp.concatenate([w_uq[:, base + k : base + k + 32] for k in cols], axis=1)
+                for b in range(3):
+                    to[n * 3 + b] = block[b * 32 : (b + 1) * 32]
+        for to, half in ((kv_mine, own), (kv_send, 1 - own)):
+            for n in range(4):
                 cols = slice(half * 512 + n * 128, half * 512 + n * 128 + 128)
                 to[n] = w_uk[:, cols]
                 to[4 + n] = w_uv[:, cols]
@@ -81,7 +93,7 @@
     freqs = jnp.exp(-math.log(rope_base) * steps)
     angle = jnp.concatenate(pos, axis=1).astype(jnp.float32) * freqs
     cos, sin = jnp.cos(angle), jnp.sin(angle)
-    cs[...] = jnp.concatenate([cos, cos, -sin, sin], axis=0).T
+    cs[...] = jnp.concatenate([cos] * 4 + [sin] * 4, axis=0).T
     r = rope_t[...].astype(jnp.float32)
     a, b, rc, rs = r[:32], r[32:], cos[:, :256], sin[:, :256]
     both = jnp.concatenate([a * rc - b * rs, b * rc + a * rs], axis=0)
@@ -89,25 +101,23 @@
     share[...] = fold[pl.ds(pl.multiple_of(m["y"] * 32, 32), 32), :]
 
 
-def rows_kernel(w_mine, w_other, wq):
+def pack_kernel(kq, kq_x, share, w_mine, w_other, kv_mine, kv_other, k_one, w_one, q_x):
     c = where_am_i()["c"]
-    wq[pl.ds(pl.multiple_of(c * 96, 32), 96), :] = w_mine[...]
-    wq[pl.ds(pl.multiple_of((1 - c) * 96, 32), 96), :] = w_other[...]
-
-
-def pack_kernel(kq, kq_x, share, kv_mine, kv_other, k_one, q_x):
-    c = where_am_i()["c"]
-    k_one[:256] = jnp.concatenate([kq[:64], kq_x[:64]], axis=0).T
-    k_one[256:288] = share[...]
-    for n in range(8):
-        k_one[pl.ds(pl.multiple_of(288 + n * 64 + c * 32, 32), 32), :] = kv_mine[n]
-        k_one[pl.ds(pl.multiple_of(288 + n * 64 + (1 - c) * 32, 32), 32), :] = kv_other[n]
+    lat = jnp.concatenate([kq[:64], kq_x[:64]], axis=0).T
+    for b in range(8):
+        k_one[b] = lat[b * 32 : (b + 1) * 32]
+    k_one[8] = share[...]
+    for core, w, kv in ((c, w_mine, kv_mine), (1 - c, w_other, kv_other)):
+        for n in range(6):
+            w_one[pl.ds(n * 6 + core * 3, 3)] = w[n * 3 : n * 3 + 3]
+        for n in range(8):
+            w_one[36 + n * 2 + core] = kv[n]
     q_x[...] = jnp.concatenate([kq[64:], kq_x[64:]], axis=0).T
 
 
 def join_kernel(*refs):
     ins, out, sem = refs[:8], refs[8], refs[9]
-    copies = [pltpu.make_async_copy(r.at[:288], out.at[j], sem.at[j]) for j, r in enumerate(ins)]
+    copies = [pltpu.make_async_copy(r, out.at[j], sem.at[j]) for j, r in enumerate(ins)]
     for cp in copies:
         cp.start()
     for cp in copies:
@@ -127,10 +137,10 @@
 
 
 def attend_kernel(order, seg, *refs):
-    q_in, w_in, kv_in, cs, pieces = refs[:2], refs[2:10], refs[10:18], refs[18], (refs[19:24], refs[24:29])
-    out, hm = refs[29:31]
-    q, w, kvw, lat, rope, kn, v, kr, qs, sbuf, mx, rm, acc, total, step_i, step_ch, need = refs[31:48]
-    qsem, wsem, kvsem, ksem = refs[48:]
+    q_in, w_in, cs, pieces = refs[:2], refs[2:10], refs[10], (refs[11:16], refs[16:21])
+    out, hm = refs[21:23]
+    q, wp, w, kvw, lat, rope, kn, v, kr, qs, sbuf, mx, rm, acc, total, step_i, step_ch, need = refs[23:41]
+    qsem, wsem, ksem = refs[41:]
     m = where_am_i()
 
     def block_of(i):
@@ -142,18 +152,7 @@
     for half in range(2):
         first.append(pltpu.make_async_copy(q_in[half], q.at[half], qsem.at[half]))
     for j in range(8):
-        t = lax.rem(m["z"] + RING[j] + 8, 8)
-        row = pl.multiple_of(feature_row(m, t, 192), 64)
-        first.append(pltpu.make_async_copy(w_in[j], w.at[pl.ds(row, 192)], wsem.at[j]))
-        row = pl.multiple_of(feature_row(m, t, 64), 64)
-        for n in range(8):
-            second.append(
-                pltpu.make_async_copy(
-                    kv_in[j].at[pl.ds(288 + n * 64, 64)],
-                    kvw.at[pl.ds(row, 64), pl.ds(n * 128, 128)],
-                    kvsem.at[j, n],
-                )
-            )
+        first.append(pltpu.make_async_copy(w_in[j], wp.at[j], wsem.at[j]))
     for core in range(2):
         own, up, dn, f1, f2 = pieces[core]
         for n, (src, plane, start, count, dy) in enumerate(
@@ -162,11 +161,11 @@
             rows = pl.ds(core * 8 + start, count)
             yq = pl.multiple_of(lax.rem(m["y"] + dy, 4) * 32, 32)
             second.append(
-                pltpu.make_async_copy(src.at[:, :256, :], lat.at[plane, rows], ksem.at[core, n, 0])
+                pltpu.make_async_copy(src.at[:, :8], lat.at[plane, rows], ksem.at[core, n, 0])
             )
             second.append(
                 pltpu.make_async_copy(
-                    src.at[:, 256:, :], rope.at[rows, pl.ds(yq, 32), :], ksem.at[core, n, 1]
+                    src.at[:, 8], rope.at[rows, pl.ds(yq, 32), :], ksem.at[core, n, 1]
                 )
             )
     for cp in first + second:
@@ -194,27 +193,35 @@
     step_ch[count] = block_of(3) // 2
     odd = lax.rem(count, 2)
 
-    lane64 = lax.broadcasted_iota(jnp.int32, (BLK, 64), 1)
-    row64 = lax.broadcasted_iota(jnp.int32, (BLK, 64), 0)
     for cp in first:
         cp.wait()
+    for j in range(8):
+        t = lax.rem(m["z"] + RING[j] + 8, 8)
+        row = pl.multiple_of(feature_row(m, t, 192), 64)
+        for n in range(6):
+            w[pl.ds(row, 192), n * 128 : (n + 1) * 128] = wp[j, n * 6 : n * 6 + 6].reshape(192, 128)
+        row = pl.multiple_of(feature_row(m, t, 64), 64)
+        for n in range(8):
+            kvw[pl.ds(row, 64), n * 128 : (n + 1) * 128] = wp[j, 36 + n * 2 : 38 + n * 2].reshape(64, 128)
+
+    lane = lax.broadcasted_iota(jnp.int32, (BLK, 128), 1)
+    line = lax.broadcasted_iota(jnp.int32, (BLK, 128), 0)
     for half in range(2):
         full = jnp.dot(q[half], w[...], preferred_element_type=f32)
-        labels = [
-            jnp.where(label_of(bounds, row64 + block_of(half * 2 + b) * BLK) == lane64, 1.0, 0.0)
-            for b in range(2)
-        ]
-        onehot = jnp.concatenate(labels, axis=0).astype(bf16)
-        rows = slice(half * 256, half * 256 + 256)
-        cos = cs[rows, :64]
-        sin = cs[rows, 64:]
-        for h in range(4):
-            nope = full[:, h * 192 : h * 192 + 128].astype(bf16)
-            r = full[:, h * 192 + 128 : h * 192 + 192]
-            turned = jnp.concatenate([r[:, 32:], r[:, :32]], axis=1)
-            rot = (r * cos + turned * sin).astype(bf16)
-            qs[h, rows, :128] = nope
-            qs[h, rows, 128:] = jnp.concatenate([rot, onehot], axis=1)
+        for b in range(2):
+            part = slice(b * BLK, (b + 1) * BLK)
+            rows = slice(half * 256 + b * BLK, half * 256 + (b + 1) * BLK)
+            label = label_of(bounds, line + block_of(half * 2 + b) * BLK)
+            onehot = jnp.where(lane == label + 64, 1.0, 0.0)
+            cos, sin = cs[rows, :128], cs[rows, 128:]
+            x, y = full[part, 512:640], full[part, 640:]
+            rot = (x * cos - y * sin, y * cos + x * sin)
+            for h in range(4):
+                r0 = pltpu.roll(rot[0], (128 - 32 * h) % 128, 1) if h else rot[0]
+                r1 = pltpu.roll(rot[1], (32 - 32 * h) % 128, 1) if h != 1 else rot[1]
+                tail = jnp.where(lane < 32, r0, jnp.where(lane < 64, r1, onehot))
+                qs[h, rows, :128] = full[part, h * 128 : (h + 1) * 128].astype(bf16)
+                qs[h, rows, 128:] = tail.astype(bf16)
 
     mx[...] = jnp.full(mx.shape, masked_value, f32)
     acc[...] = jnp.zeros(acc.shape, f32)
@@ -233,7 +240,7 @@
 
         @pl.when((need[order[0, base] // 2] + need[order[0, base + 1] // 2]) > 0)
         def _():
-            x = jnp.concatenate([lat[n, i] for n in range(4)], axis=1)
+            x = jnp.concatenate([lat[n, i].reshape(256, 128) for n in range(4)], axis=1)
             y = jnp.dot(x, kvw[...], preferred_element_type=f32)
             fold = rope[i]
             for b in range(2):
@@ -241,10 +248,10 @@
                 rows = slice(b * BLK, (b + 1) * BLK)
                 kn[pl.ds(pb, BLK), :] = y[rows, :512].astype(bf16)
                 v[pl.ds(pb, BLK), :] = y[rows, 512:].astype(bf16)
-                label = label_of(bounds, row64 + pb)
-                apart = jnp.where((lane64 < 4) & (lane64 != label), masked_value, 0.0).astype(bf16)
+                label = label_of(bounds, line[:, :64] + pb)
+                apart = jnp.where((lane[:, :64] < 4) & (lane[:, :64] != label), masked_value, 0.0)
                 kr[pl.ds(pb, BLK), :] = jnp.concatenate(
-                    [fold[:, b * 64 : b * 64 + 64], apart], axis=1
+                    [fold[:, b * 64 : b * 64 + 64], apart.astype(bf16)], axis=1
                 )
 
         return carry
@@ -355,10 +362,10 @@
 
 def ring(x):
     up, dn, got = x, x, [x]
-    for s in range(4):
+    for s in range(1, 5):
         up = lax.ppermute(up, "seq", shift_seq(1))
         got.append(up)
-        if s < 3:
+        if s < 4:
             dn = lax.ppermute(dn, "seq", shift_seq(-1))
             got.append(dn)
     return got
@@ -368,7 +375,7 @@
     return lax.ppermute(x, "seq", SWAP)
 
 
-def call(kernel, outs, args, specs=None, scratch=(), name=None):
+def call(kernel, outs, args, specs=None, scratch=()):
     outs = [jax.ShapeDtypeStruct(shape, dtype) for shape, dtype in outs]
     size = sum(math.prod(o.shape) * o.dtype.itemsize for o in outs)
     return pl.pallas_call(
@@ -378,13 +385,7 @@
         out_specs=[VMEM] * len(outs),
         scratch_shapes=list(scratch),
         cost_estimate=pl.CostEstimate(flops=1 << 20, bytes_accessed=2 * size, transcendentals=0),
-        name=name,
     )(*args)
-
-
-def of_everyone(array, axis):
-    copies = jnp.broadcast_to(array, (lax.axis_size(axis), *array.shape))
-    return jnp.max(lax.all_to_all(copies, axis, split_axis=0, concat_axis=0, tiled=True), axis=0)
 
 
 def on_device(query_latent, key_latent, rope_key, w_uq, w_uk, w_uv, block_order, segment_ids):
@@ -392,41 +393,36 @@
     c = where_am_i()["c"]
     kq, w_mine, w_send, kv_mine, kv_send = call(
         split_kernel,
-        [((256, 256), bf16)] + [((96, 768), bf16)] * 2 + [((8, 32, 128), bf16)] * 2,
+        [((256, 256), bf16)] + [((18, 32, 128), bf16)] * 2 + [((8, 32, 128), bf16)] * 2,
         (query_latent[0].T, key_latent[0].T, w_uq, w_uk, w_uv),
-        name="split",
     )
     kq_x = lax.ppermute(kq, "tp", XSWAP)
     w_other = swap(w_send)
     kv_other = swap(kv_send)
     cs, share = call(
         turn_kernel,
-        [((512, 128), f32), ((32, 128), bf16)],
+        [((512, 256), f32), ((32, 128), bf16)],
         (block_order, rope_key[0].T),
         specs=[SMEM, VMEM],
         scratch=[pltpu.VMEM((128, 128), bf16)],
-        name="turn",
-    )
-    (wq,) = call(rows_kernel, [((192, 768), bf16)], (w_mine, w_other), name="rows")
-    k_one, q_x = call(
+    )
+    k_one, w_one, q_x = call(
         pack_kernel,
-        [((800, 128), bf16), ((256, 384), bf16)],
-        (kq, kq_x, share, kv_mine, kv_other),
-        name="pack",
-    )
-
-    w_ring = ring(wq)
+        [((9, 32, 128), bf16), ((52, 32, 128), bf16), ((256, 384), bf16)],
+        (kq, kq_x, share, w_mine, w_other, kv_mine, kv_other),
+    )
+
     k_ring = ring(k_one)
+    w_ring = ring(w_one)
     q_parts = [q_x] + [lax.ppermute(q_x, "tp", shift_y(by)) for by in (1, -1, 2)]
     q_own = jnp.concatenate(q_parts, axis=1)
     q_sib = swap(q_own)
     (k_all,) = call(
         join_kernel,
-        [((8, 288, 128), bf16)],
+        [((8, 9, 32, 128), bf16)],
         k_ring,
         specs=[ANY] * 8,
         scratch=[pltpu.SemaphoreType.DMA((8,))],
-        name="join",
     )
     k_up = lax.ppermute(k_all, "tp", shift_y(1))
     k_dn = lax.ppermute(k_all, "tp", shift_y(-1))
@@ -442,13 +438,14 @@
             jax.ShapeDtypeStruct((512, 512), bf16),
             jax.ShapeDtypeStruct((8, 128), f32),
         ],
-        in_specs=[SMEM, VMEM] + [ANY] * 18 + [VMEM] + [ANY] * 10,
+        in_specs=[SMEM, VMEM] + [ANY] * 10 + [VMEM] + [ANY] * 10,
         out_specs=[VMEM] * 2,
         scratch_shapes=[
             vm((2, 256, 1536), bf16),
+            vm((8, 52, 32, 128), bf16),
             vm((1536, 768), bf16),
             vm((512, 1024), bf16),
-            vm((4, 16, 256, 128), bf16),
+            vm((4, 16, 8, 32, 128), bf16),
             vm((16, 128, 128), bf16),
             vm((4096, 512), bf16),
             vm((4096, 512), bf16),
@@ -464,7 +461,6 @@
             pltpu.SMEM((16,), jnp.int32),
             pltpu.SemaphoreType.DMA((2,)),
             pltpu.SemaphoreType.DMA((8,)),
-            pltpu.SemaphoreType.DMA((8, 8)),
             pltpu.SemaphoreType.DMA((2, 5, 2)),
         ],
         compiler_params=pltpu.CompilerParams(vmem_limit_bytes=60 << 20),
@@ -472,14 +468,21 @@
             flops=20 << 30, bytes_accessed=12 << 20, transcendentals=4 << 20
         ),
         name="attend",
-    )(block_order, segment_ids[0].reshape(32, 128), q_own, q_sib, *w_ring, *k_ring, cs, *k_own, *k_sib)
+    )(block_order, segment_ids[0].reshape(32, 128), q_own, q_sib, *w_ring, cs, *k_own, *k_sib)
 
     local_max = hm[:4, 0]
     low = jnp.full((4,), masked_value, f32)
     both = jnp.where(
         c == 0, jnp.concatenate([local_max, low]), jnp.concatenate([low, local_max])
     )
-    head_max = of_everyone(both, ("seq", "dp"))
+    everyone = jnp.broadcast_to(both, (32, 8))
+    everyone = lax.all_to_all(everyone, ("seq", "dp"), split_axis=0, concat_axis=0, tiled=True)
+    got = swap(ctx[256:])
+    own = ctx[:256]
+    first = c == 0
+    context = jnp.concatenate([jnp.where(first, own, got), jnp.where(first, got, own)], axis=1)
+    everyone, context = lax.optimization_barrier((everyone, context))
+    head_max = jnp.max(everyone, axis=0)
     ratio = CLIP / jnp.maximum(head_max, CLIP)
     root = jnp.sqrt(ratio)
     factors = jnp.concatenate(
@@ -488,10 +491,6 @@
     clipped_uq = (w_uq.astype(f32) * factors[None, :]).astype(bf16)
     clipped_uk = (w_uk.astype(f32) * jnp.repeat(root, NOPE)[None, :]).astype(bf16)
 
-    got = swap(ctx[256:])
-    own = ctx[:256]
-    first = c == 0
-    context = jnp.concatenate([jnp.where(first, own, got), jnp.where(first, got, own)], axis=1)
     return (context[None], clipped_uq, clipped_uk)
 
 

time: 129 us -> 145 us (1.12)
  waiting for transfers between devices: 26.5 us -> 48.4 us
  starting transfers between devices: 61.9 us -> 52.2 us
  Pallas kernels: 32.1 us -> 34.5 us
    ppermute x8, waiting for transfers between devices: 7.72 us -> 22.1 us  [ring(): up = lax.ppermute(up, 'seq', shift_seq(1))]
    ppermute x3, waiting for transfers between devices: 0.71 us -> 11.3 us  [on_device(): lax.ppermute(q_x, 'tp', shift_y(by))]
    all_to_all x1, starting transfers between devices: 11.5 us -> 6.71 us  [on_device(): lax.all_to_all(everyone, ('seq', 'dp'), split_axis=0, concat_axis=0, tile...]
    ppermute x6, waiting for transfers between devices: 4.62 us -> 0.02 us  [ring(): dn = lax.ppermute(dn, 'seq', shift_seq(-1))]
    pallas_call x1, Pallas kernels: 22.6 us -> 26.3 us  [on_device(): pl.pallas_call(attend_kernel, out_shape=[jax.ShapeDtypeStruct((512, 512),...]
    ppermute x1, waiting for transfers between devices: 0.01 us -> 3.07 us  [on_device(): kq_x = lax.ppermute(kq, 'tp', XSWAP)]
    ppermute x3, starting transfers between devices: 4.46 us -> 6.74 us  [on_device(): lax.ppermute(q_x, 'tp', shift_y(by))]
    ppermute x8, starting transfers between devices: 2.33 us -> 0.1 us  [ring(): up = lax.ppermute(up, 'seq', shift_seq(1))]
  transfers between devices with their start and end apart: 32 -> 32, of which waited for: 10 -> 14; matrix products, arithmetic and copies ran while one was open for 2% -> 1% of each run, Pallas kernels for 4% -> 3%
where the time goes in v2:
time: 145 us
  starting transfers between devices  52.2 us (36%)
  waiting for transfers between devices  48.4 us (33%)
  Pallas kernels  34.5 us (24%)
  local copies, waits for them, and re-layouts  5.98 us (4%)
  other arithmetic  2.44 us (2%)
    pallas_call x1, Pallas kernels, on_device(): pl.pallas_call(attend_kernel, out_shape=[jax.ShapeDtypeStruct((512, 512),...  26.3 us
    ppermute x8, waiting for transfers between devices, ring(): up = lax.ppermute(up, 'seq', shift_seq(1))  22.1 us
    ppermute x9, starting transfers between devices, swap(): return lax.ppermute(x, 'seq', SWAP)  21.1 us
    ppermute x6, starting transfers between devices, ring(): dn = lax.ppermute(dn, 'seq', shift_seq(-1))  13.7 us
    ppermute x3, waiting for transfers between devices, on_device(): lax.ppermute(q_x, 'tp', shift_y(by))  11.3 us
    all_to_all x1, waiting for transfers between devices, on_device(): lax.all_to_all(everyone, ('seq', 'dp'), split_axis=0, concat_axis=0, tile...  8.33 us
    pallas_call x4, Pallas kernels, call(): pl.pallas_call(kernel, out_shape=outs, in_specs=specs or [VMEM] * len(arg...  8.17 us
    ppermute x3, starting transfers between devices, on_device(): lax.ppermute(q_x, 'tp', shift_y(by))  6.74 us
  transfers between devices with their start and end apart: 32, of which 14 were waited for; matrix products, arithmetic and copies ran while one was open for 1% of the time, Pallas kernels for 3%

profile of v2, /device:TPU:1, one launch (start us, length us, event | category | flops | bytes accessed | tf_op | source)
XLA Modules:
  0.0 144.5 jit_solution(12874572991575792838)
XLA Ops:
  0.6 2.1 %shard_map.103 = (bf16[256,256]{1,0:T(8,128)(2,1)}, bf16[18,32,128]{2,1,0:T(8,128)(2,1)}, bf16[18,32,128]{2,1,0:T(8,128)(2,1)}, bf16[8,32,128]{2,1,0:T(8,128)(2,1)}, bf16[8,32,128]{2,1,0:T(8,128)(2,1)}) custom-call(bf16[192,256]{1,0:T(8,128)(2,1)} %bitcast.15, bf16[64,256]{1,0:T(8,128)(2,1)} %bitcast.17, bf16[96,1536]{1,0:T(8,128)(2,1)} %w_uq.1, ...), custom_call_target="tpu_custom_call" | custom-call | flops 1048576 | bytes 1114112 | tf_op jit(solution)/shard_map/pallas_call | solution.py:381
  2.7 3.2 %collective-permute-start.1 = (bf16[18,32,128]{2,1,0:T(8,128)(2,1)}, bf16[18,32,128]{2,1,0:T(8,128)(2,1)S(1)}, u32[]{:S(2)}, u32[]{:S(2)}) collective-permute-start(bf16[18,32,128]{2,1,0:T(8,128)(2,1)} %get-tuple-element.20), channel_id=1, source_target_pairs={{0,16},{16,0},{32,48},{48,32},{64,80},{80,64},{96,112},{112,96},{1... | collective-permute-start | bytes 442376 | tf_op jit(solution)/shard_map/ppermute | solution.py:375
  6.0 2.0 %shard_map.104 = (f32[512,256]{1,0:T(8,128)}, bf16[32,128]{1,0:T(8,128)(2,1)}) custom-call(s32[1,32]{1,0:T(1,128)} %order.3, bf16[64,256]{1,0:T(8,128)(2,1)} %bitcast.18), custom_call_target="tpu_custom_call" | custom-call | flops 1048576 | bytes 1064960 | tf_op jit(solution)/shard_map/pallas_call | solution.py:381
  8.1 3.1 %collective-permute-done.kq_x = bf16[256,256]{1,0:T(8,128)(2,1)S(1)} collective-permute-done((bf16[256,256]{1,0:T(8,128)(2,1)}, bf16[256,256]{1,0:T(8,128)(2,1)S(1)}, u32[]{:S(2)}, u32[]{:S(2)}) %collective-permute-start) | collective-permute-done | bytes 131104 | tf_op jit(solution)/shard_map/ppermute | solution.py:399
  11.8 2.1 %shard_map.105 = (bf16[9,32,128]{2,1,0:T(8,128)(2,1)}, bf16[52,32,128]{2,1,0:T(8,128)(2,1)}, bf16[256,384]{1,0:T(8,128)(2,1)}) custom-call(bf16[256,256]{1,0:T(8,128)(2,1)} %get-tuple-element.17.kq, bf16[256,256]{1,0:T(8,128)(2,1)} %copy-done.8, bf16[32,128]{1,0:T(8,128)(2,1)} %get-tuple-element.18.share, bf16[18,32,128]{2,1,0:T(8,128)(2,1)} %get-tuple-element.19.w_mine, ...), custom_call_target="tpu_custom_call" | custom-call | flops 1048576 | bytes 1392640 | tf_op jit(solution)/shard_map/pallas_call | solution.py:381
  13.9 3.9 %collective-permute-start.15 = (bf16[9,32,128]{2,1,0:T(8,128)(2,1)}, bf16[9,32,128]{2,1,0:T(8,128)(2,1)S(1)}, u32[]{:S(2)}, u32[]{:S(2)}) collective-permute-start(bf16[9,32,128]{2,1,0:T(8,128)(2,1)} %get-tuple-element.26.refs_0_), channel_id=1, source_target_pairs={{0,224},{16,240},{32,0},{48,16},{64,32},{80,48},{96,64},{112,80},{... | collective-permute-start | bytes 221192 | tf_op jit(solution)/shard_map/ppermute | solution.py:369
  17.8 1.9 %collective-permute-done.14.refs_1_ = bf16[9,32,128]{2,1,0:T(8,128)(2,1)S(1)} collective-permute-done((bf16[9,32,128]{2,1,0:T(8,128)(2,1)}, bf16[9,32,128]{2,1,0:T(8,128)(2,1)S(1)}, u32[]{:S(2)}, u32[]{:S(2)}) %collective-permute-start.14) | collective-permute-done | bytes 73760 | tf_op jit(solution)/shard_map/ppermute | solution.py:366
  19.7 2.7 %collective-permute-start.17 = (bf16[9,32,128]{2,1,0:T(8,128)(2,1)S(1)}, bf16[9,32,128]{2,1,0:T(8,128)(2,1)S(1)}, u32[]{:S(2)}, u32[]{:S(2)}) collective-permute-start(bf16[9,32,128]{2,1,0:T(8,128)(2,1)S(1)} %collective-permute-done.15.refs_2_), channel_id=1, source_target_pairs={{0,224},{16,240},{32,0},{48,16},{64,32},{80,48},{96,64},{112,80},{... | collective-permute-start | bytes 221192 | tf_op jit(solution)/shard_map/ppermute | solution.py:369
  25.4 2.7 %collective-permute-start.19 = (bf16[9,32,128]{2,1,0:T(8,128)(2,1)S(1)}, bf16[9,32,128]{2,1,0:T(8,128)(2,1)S(1)}, u32[]{:S(2)}, u32[]{:S(2)}) collective-permute-start(bf16[9,32,128]{2,1,0:T(8,128)(2,1)S(1)} %collective-permute-done.17.refs_4_), channel_id=1, source_target_pairs={{0,224},{16,240},{32,0},{48,16},{64,32},{80,48},{96,64},{112,80},{... | collective-permute-start | bytes 221192 | tf_op jit(solution)/shard_map/ppermute | solution.py:369
  28.5 2.7 %collective-permute-start.4 = (bf16[256,384]{1,0:T(8,128)(2,1)}, bf16[256,384]{1,0:T(8,128)(2,1)S(1)}, u32[]{:S(2)}, u32[]{:S(2)}) collective-permute-start(bf16[256,384]{1,0:T(8,128)(2,1)} %get-tuple-element.23), channel_id=1, source_target_pairs={{0,6},{2,0},{4,2},{6,4},{8,14},{10,8},{12,10},{14,12},{1,7},{3,1},... | collective-permute-start | bytes 589832 | tf_op jit(solution)/shard_map/ppermute | solution.py:417
  31.3 1.9 %collective-permute-done.20.refs_7_ = bf16[9,32,128]{2,1,0:T(8,128)(2,1)S(1)} collective-permute-done((bf16[9,32,128]{2,1,0:T(8,128)(2,1)S(1)}, bf16[9,32,128]{2,1,0:T(8,128)(2,1)S(1)}, u32[]{:S(2)}, u32[]{:S(2)}) %collective-permute-start.20) | collective-permute-done | bytes 73760 | tf_op jit(solution)/shard_map/ppermute | solution.py:366
  33.9 2.0 %shard_map.106.refs_11_ = bf16[8,9,32,128]{3,2,1,0:T(8,128)(2,1)} custom-call(bf16[9,32,128]{2,1,0:T(8,128)(2,1)} %get-tuple-element.26.refs_0_, bf16[9,32,128]{2,1,0:T(8,128)(2,1)} %copy-done.9, bf16[9,32,128]{2,1,0:T(8,128)(2,1)} %copy-done.10, bf16[9,32,128]{2,1,0:T(8,128)(2,1)} %copy-done.11, bf16[9,32,128]{2,1,0:T(8,128)(2,1)} %copy-done.12, ...), custom_call_target="tpu_custom_call" | custom-call | flops 1048576 | bytes 1179648 | tf_op jit(solution)/shard_map/pallas_call | solution.py:381
  37.1 2.7 %collective-permute-start.5 = (bf16[256,384]{1,0:T(8,128)(2,1)S(1)}, bf16[256,384]{1,0:T(8,128)(2,1)S(1)}, u32[]{:S(2)}, u32[]{:S(2)}) collective-permute-start(bf16[256,384]{1,0:T(8,128)(2,1)S(1)} %copy-done.4), channel_id=1, source_target_pairs={{0,4},{2,6},{4,0},{6,2},{8,12},{10,14},{12,8},{14,10},{1,5},{3,7},... | collective-permute-start | bytes 589832 | tf_op jit(solution)/shard_map/ppermute | solution.py:417
  39.9 11.3 %collective-permute-done.5 = bf16[256,384]{1,0:T(8,128)(2,1)S(1)} collective-permute-done((bf16[256,384]{1,0:T(8,128)(2,1)S(1)}, bf16[256,384]{1,0:T(8,128)(2,1)S(1)}, u32[]{:S(2)}, u32[]{:S(2)}) %collective-permute-start.5) | collective-permute-done | bytes 196640 | tf_op jit(solution)/shard_map/ppermute | solution.py:417
  51.3 7.2 %collective-permute-start.6 = (bf16[256,1536]{1,0:T(8,128)(2,1)S(1)}, bf16[256,1536]{1,0:T(8,128)(2,1)S(1)}, u32[]{:S(2)}, u32[]{:S(2)}) collective-permute-start(bf16[256,1536]{1,0:T(8,128)(2,1)S(1)} %constant_dynamic-update-slice_fusion.refs_0_), channel_id=1, source_target_pairs={{0,16},{16,0},{32,48},{48,32},{64,80},{80,64},{96,112},{112,96},{1... | collective-permute-start | bytes 2359304 | tf_op jit(solution)/shard_map/ppermute | solution.py:375
  58.6 2.6 %collective-permute-start.10 = (bf16[52,32,128]{2,1,0:T(8,128)(2,1)S(1)}, bf16[52,32,128]{2,1,0:T(8,128)(2,1)S(1)}, u32[]{:S(2)}, u32[]{:S(2)}) collective-permute-start(bf16[52,32,128]{2,1,0:T(8,128)(2,1)S(1)} %collective-permute-done.8.refs_4_), channel_id=1, source_target_pairs={{0,224},{16,240},{32,0},{48,16},{64,32},{80,48},{96,64},{112,80},{... | collective-permute-start | bytes 1277960 | tf_op jit(solution)/shard_map/ppermute | solution.py:369
  62.0 9.3 %collective-permute-done.9.refs_5_ = bf16[52,32,128]{2,1,0:T(8,128)(2,1)S(1)} collective-permute-done((bf16[52,32,128]{2,1,0:T(8,128)(2,1)}, bf16[52,32,128]{2,1,0:T(8,128)(2,1)S(1)}, u32[]{:S(2)}, u32[]{:S(2)}) %collective-permute-start.9) | collective-permute-done | bytes 426016 | tf_op jit(solution)/shard_map/ppermute | solution.py:366
  76.8 2.2 %collective-permute-start.26 = (bf16[8,9,32,128]{3,2,1,0:T(8,128)(2,1)S(1)}, bf16[8,9,32,128]{3,2,1,0:T(8,128)(2,1)S(1)}, u32[]{:S(2)}, u32[]{:S(2)}) collective-permute-start(bf16[8,9,32,128]{3,2,1,0:T(8,128)(2,1)S(1)} %collective-permute-done.21.refs_12_), channel_id=1, source_target_pairs={{0,16},{16,0},{32,48},{48,32},{64,80},{80,64},{96,112},{112,96},{1... | collective-permute-start | bytes 1769480 | tf_op jit(solution)/shard_map/ppermute | solution.py:375
  83.5 2.5 %collective-permute-start.28 = (bf16[4,9,32,128]{3,2,1,0:T(8,128)(2,1)S(1)}, bf16[4,9,32,128]{3,2,1,0:T(8,128)(2,1)S(1)}, u32[]{:S(2)}, u32[]{:S(2)}) collective-permute-start(bf16[4,9,32,128]{3,2,1,0:T(8,128)(2,1)S(1)} %collective-permute-done.23.refs_14_), channel_id=1, source_target_pairs={{0,16},{16,0},{32,48},{48,32},{64,80},{80,64},{96,112},{112,96},{1... | collective-permute-start | bytes 884744 | tf_op jit(solution)/shard_map/ppermute | solution.py:375
  88.5 5.2 %collective-permute-done.13.refs_9_ = bf16[52,32,128]{2,1,0:T(8,128)(2,1)S(1)} collective-permute-done((bf16[52,32,128]{2,1,0:T(8,128)(2,1)S(1)}, bf16[52,32,128]{2,1,0:T(8,128)(2,1)S(1)}, u32[]{:S(2)}, u32[]{:S(2)}) %collective-permute-start.13) | collective-permute-done | bytes 426016 | tf_op jit(solution)/shard_map/ppermute | solution.py:366
  94.5 26.3 %attend.1 = (bf16[512,512]{1,0:T(8,128)(2,1)}, f32[8,128]{1,0:T(8,128)}) custom-call(s32[1,32]{1,0:T(1,128)} %order.3, s32[32,128]{1,0:T(8,128)} %bitcast.19, bf16[256,1536]{1,0:T(8,128)(2,1)} %copy-done.17, bf16[256,1536]{1,0:T(8,128)(2,1)} %copy-done.19, bf16[52,32,128]{2,1,0:T(8,128)(2,1)} %get-tuple-element.24.refs_2_, ...), custom_call_target="tpu_custom_call" | custom-call | flops 21474836480 | bytes 12582912 | tf_op jit(solution)/shard_map/attend/pallas_call | solution.py:435
  121.9 3.3 %collective-permute-start.30 = (bf16[256,512]{1,0:T(8,128)(2,1)S(1)}, bf16[256,512]{1,0:T(8,128)(2,1)S(1)}, u32[]{:S(2)}, u32[]{:S(2)}) collective-permute-start(bf16[256,512]{1,0:T(8,128)(2,1)S(1)} %slice.19), channel_id=1, source_target_pairs={{0,16},{16,0},{32,48},{48,32},{64,80},{80,64},{96,112},{112,96},{1... | collective-permute-start | bytes 786440 | tf_op jit(solution)/shard_map/ppermute | solution.py:375
  126.7 6.7 %all-to-all-start = ((f32[32,1,8]{2,1,0:T(1,128)}), f32[32,1,8]{2,1,0:T(1,128)S(1)}, u32[]{:S(2)}, u32[]{:S(2)}) async-start(f32[32,1,8]{2,1,0:T(1,128)} %broadcast_in_dim.8), calls=%async_computation | async-start | bytes 32768 | tf_op jit(solution)/shard_map/all_to_all | solution.py:479
  134.3 8.3 %all-to-all-done = f32[32,1,8]{2,1,0:T(1,128)S(1)} async-done(((f32[32,1,8]{2,1,0:T(1,128)}), f32[32,1,8]{2,1,0:T(1,128)S(1)}, u32[]{:S(2)}, u32[]{:S(2)}) %all-to-all-start) | async-done | bytes 1056 | tf_op jit(solution)/shard_map/all_to_all | solution.py:479
  (134 shorter events, 25.5 us)
Async XLA Ops:
  2.7 8.4 %collective-permute-start.1 = (bf16[18,32,128]{2,1,0:T(8,128)(2,1)}, bf16[18,32,128]{2,1,0:T(8,128)(2,1)S(1)}, u32[]{:S(2)}, u32[]{:S(2)}) collective-permute-start(bf16[18,32,128]{2,1,0:T(8,128)(2,1)} %get-tuple-element.20), channel_id=1, source_target_pairs={{0,16},{16,0},{32,48},{48,32},{64,80},{80,64},{96,112},{112,96},{1... | collective-permute-start | bytes 442376 | tf_op jit(solution)/shard_map/ppermute | solution.py:375
  13.9 5.8 %collective-permute-start.14 = (bf16[9,32,128]{2,1,0:T(8,128)(2,1)}, bf16[9,32,128]{2,1,0:T(8,128)(2,1)S(1)}, u32[]{:S(2)}, u32[]{:S(2)}) collective-permute-start(bf16[9,32,128]{2,1,0:T(8,128)(2,1)} %get-tuple-element.26.refs_0_), channel_id=1, source_target_pairs={{0,32},{16,48},{32,64},{48,80},{64,96},{80,112},{96,128},{112,144}... | collective-permute-start | bytes 221192 | tf_op jit(solution)/shard_map/ppermute | solution.py:366
  13.9 5.8 %collective-permute-start.15 = (bf16[9,32,128]{2,1,0:T(8,128)(2,1)}, bf16[9,32,128]{2,1,0:T(8,128)(2,1)S(1)}, u32[]{:S(2)}, u32[]{:S(2)}) collective-permute-start(bf16[9,32,128]{2,1,0:T(8,128)(2,1)} %get-tuple-element.26.refs_0_), channel_id=1, source_target_pairs={{0,224},{16,240},{32,0},{48,16},{64,32},{80,48},{96,64},{112,80},{... | collective-permute-start | bytes 221192 | tf_op jit(solution)/shard_map/ppermute | solution.py:369
  24.1 15.7 %collective-permute-start.3 = (bf16[256,384]{1,0:T(8,128)(2,1)}, bf16[256,384]{1,0:T(8,128)(2,1)S(1)}, u32[]{:S(2)}, u32[]{:S(2)}) collective-permute-start(bf16[256,384]{1,0:T(8,128)(2,1)} %get-tuple-element.23), channel_id=1, source_target_pairs={{0,2},{2,4},{4,6},{6,0},{8,10},{10,12},{12,14},{14,8},{1,3},{3,5},... | collective-permute-start | bytes 589832 | tf_op jit(solution)/shard_map/ppermute | solution.py:417
  25.4 5.9 %collective-permute-start.19 = (bf16[9,32,128]{2,1,0:T(8,128)(2,1)S(1)}, bf16[9,32,128]{2,1,0:T(8,128)(2,1)S(1)}, u32[]{:S(2)}, u32[]{:S(2)}) collective-permute-start(bf16[9,32,128]{2,1,0:T(8,128)(2,1)S(1)} %collective-permute-done.17.refs_4_), channel_id=1, source_target_pairs={{0,224},{16,240},{32,0},{48,16},{64,32},{80,48},{96,64},{112,80},{... | collective-permute-start | bytes 221192 | tf_op jit(solution)/shard_map/ppermute | solution.py:369
  28.5 11.3 %collective-permute-start.4 = (bf16[256,384]{1,0:T(8,128)(2,1)}, bf16[256,384]{1,0:T(8,128)(2,1)S(1)}, u32[]{:S(2)}, u32[]{:S(2)}) collective-permute-start(bf16[256,384]{1,0:T(8,128)(2,1)} %get-tuple-element.23), channel_id=1, source_target_pairs={{0,6},{2,0},{4,2},{6,4},{8,14},{10,8},{12,10},{14,12},{1,7},{3,1},... | collective-permute-start | bytes 589832 | tf_op jit(solution)/shard_map/ppermute | solution.py:417
  31.3 27.2 %collective-permute-start.7 = (bf16[52,32,128]{2,1,0:T(8,128)(2,1)}, bf16[52,32,128]{2,1,0:T(8,128)(2,1)}, u32[]{:S(2)}, u32[]{:S(2)}) collective-permute-start(bf16[52,32,128]{2,1,0:T(8,128)(2,1)} %get-tuple-element.24.refs_2_), channel_id=1, source_target_pairs={{0,32},{16,48},{32,64},{48,80},{64,96},{80,112},{96,128},{112,144}... | collective-permute-start | bytes 1277960 | tf_op jit(solution)/shard_map/ppermute | solution.py:366
  36.0 25.3 %collective-permute-start.21 = (bf16[8,9,32,128]{3,2,1,0:T(8,128)(2,1)}, bf16[8,9,32,128]{3,2,1,0:T(8,128)(2,1)S(1)}, u32[]{:S(2)}, u32[]{:S(2)}) collective-permute-start(bf16[8,9,32,128]{3,2,1,0:T(8,128)(2,1)} %shard_map.106.refs_11_), channel_id=1, source_target_pairs={{0,2},{2,4},{4,6},{6,0},{8,10},{10,12},{12,14},{14,8},{1,3},{3,5},... | collective-permute-start | bytes 1769480 | tf_op jit(solution)/shard_map/ppermute | solution.py:427
  37.1 14.1 %collective-permute-start.5 = (bf16[256,384]{1,0:T(8,128)(2,1)S(1)}, bf16[256,384]{1,0:T(8,128)(2,1)S(1)}, u32[]{:S(2)}, u32[]{:S(2)}) collective-permute-start(bf16[256,384]{1,0:T(8,128)(2,1)S(1)} %copy-done.4), channel_id=1, source_target_pairs={{0,4},{2,6},{4,0},{6,2},{8,12},{10,14},{12,8},{14,10},{1,5},{3,7},... | collective-permute-start | bytes 589832 | tf_op jit(solution)/shard_map/ppermute | solution.py:417
  39.8 18.8 %collective-permute-start.8 = (bf16[52,32,128]{2,1,0:T(8,128)(2,1)S(1)}, bf16[52,32,128]{2,1,0:T(8,128)(2,1)S(1)}, u32[]{:S(2)}, u32[]{:S(2)}) collective-permute-start(bf16[52,32,128]{2,1,0:T(8,128)(2,1)S(1)} %copy-done.23), channel_id=1, source_target_pairs={{0,224},{16,240},{32,0},{48,16},{64,32},{80,48},{96,64},{112,80},{... | collective-permute-start | bytes 1277960 | tf_op jit(solution)/shard_map/ppermute | solution.py:369
  51.3 25.6 %collective-permute-start.6 = (bf16[256,1536]{1,0:T(8,128)(2,1)S(1)}, bf16[256,1536]{1,0:T(8,128)(2,1)S(1)}, u32[]{:S(2)}, u32[]{:S(2)}) collective-permute-start(bf16[256,1536]{1,0:T(8,128)(2,1)S(1)} %constant_dynamic-update-slice_fusion.refs_0_), channel_id=1, source_target_pairs={{0,16},{16,0},{32,48},{48,32},{64,80},{80,64},{96,112},{112,96},{1... | collective-permute-start | bytes 2359304 | tf_op jit(solution)/shard_map/ppermute | solution.py:375
  58.5 14.8 %collective-permute-start.22 = (bf16[8,9,32,128]{3,2,1,0:T(8,128)(2,1)S(1)}, bf16[8,9,32,128]{3,2,1,0:T(8,128)(2,1)S(1)}, u32[]{:S(2)}, u32[]{:S(2)}) collective-permute-start(bf16[8,9,32,128]{3,2,1,0:T(8,128)(2,1)S(1)} %copy-done.1), channel_id=1, source_target_pairs={{0,6},{2,0},{4,2},{6,4},{8,14},{10,8},{12,10},{14,12},{1,7},{3,1},... | collective-permute-start | bytes 1769480 | tf_op jit(solution)/shard_map/ppermute | solution.py:428
  58.5 12.8 %collective-permute-start.9 = (bf16[52,32,128]{2,1,0:T(8,128)(2,1)}, bf16[52,32,128]{2,1,0:T(8,128)(2,1)S(1)}, u32[]{:S(2)}, u32[]{:S(2)}) collective-permute-start(bf16[52,32,128]{2,1,0:T(8,128)(2,1)} %collective-permute-done.7.refs_3_), channel_id=1, source_target_pairs={{0,32},{16,48},{32,64},{48,80},{64,96},{80,112},{96,128},{112,144}... | collective-permute-start | bytes 1277960 | tf_op jit(solution)/shard_map/ppermute | solution.py:366
  58.6 13.8 %collective-permute-start.10 = (bf16[52,32,128]{2,1,0:T(8,128)(2,1)S(1)}, bf16[52,32,128]{2,1,0:T(8,128)(2,1)S(1)}, u32[]{:S(2)}, u32[]{:S(2)}) collective-permute-start(bf16[52,32,128]{2,1,0:T(8,128)(2,1)S(1)} %collective-permute-done.8.refs_4_), channel_id=1, source_target_pairs={{0,224},{16,240},{32,0},{48,16},{64,32},{80,48},{96,64},{112,80},{... | collective-permute-start | bytes 1277960 | tf_op jit(solution)/shard_map/ppermute | solution.py:369
  61.3 13.9 %collective-permute-start.25 = (bf16[8,9,32,128]{3,2,1,0:T(8,128)(2,1)S(1)}, bf16[8,9,32,128]{3,2,1,0:T(8,128)(2,1)S(1)}, u32[]{:S(2)}, u32[]{:S(2)}) collective-permute-start(bf16[8,9,32,128]{3,2,1,0:T(8,128)(2,1)S(1)} %copy-done.1), channel_id=1, source_target_pairs={{0,16},{16,0},{32,48},{48,32},{64,80},{80,64},{96,112},{112,96},{1... | collective-permute-start | bytes 1769480 | tf_op jit(solution)/shard_map/ppermute | solution.py:375
  71.3 8.8 %collective-permute-start.23 = (bf16[4,9,32,128]{3,2,1,0:T(8,128)(2,1)S(1)}, bf16[4,9,32,128]{3,2,1,0:T(8,128)(2,1)S(1)}, u32[]{:S(2)}, u32[]{:S(2)}) collective-permute-start(bf16[4,9,32,128]{3,2,1,0:T(8,128)(2,1)S(1)} %slice.20), channel_id=1, source_target_pairs={{0,2},{2,4},{4,6},{6,0},{8,10},{10,12},{12,14},{14,8},{1,3},{3,5},... | collective-permute-start | bytes 884744 | tf_op jit(solution)/shard_map/ppermute | solution.py:429
  72.4 11.1 %collective-permute-start.11 = (bf16[52,32,128]{2,1,0:T(8,128)(2,1)S(1)}, bf16[52,32,128]{2,1,0:T(8,128)(2,1)S(1)}, u32[]{:S(2)}, u32[]{:S(2)}) collective-permute-start(bf16[52,32,128]{2,1,0:T(8,128)(2,1)S(1)} %collective-permute-done.9.refs_5_), channel_id=1, source_target_pairs={{0,32},{16,48},{32,64},{48,80},{64,96},{80,112},{96,128},{112,144}... | collective-permute-start | bytes 1277960 | tf_op jit(solution)/shard_map/ppermute | solution.py:366
  73.3 12.7 %collective-permute-start.12 = (bf16[52,32,128]{2,1,0:T(8,128)(2,1)S(1)}, bf16[52,32,128]{2,1,0:T(8,128)(2,1)S(1)}, u32[]{:S(2)}, u32[]{:S(2)}) collective-permute-start(bf16[52,32,128]{2,1,0:T(8,128)(2,1)S(1)} %collective-permute-done.10.refs_6_), channel_id=1, source_target_pairs={{0,224},{16,240},{32,0},{48,16},{64,32},{80,48},{96,64},{112,80},{... | collective-permute-start | bytes 1277960 | tf_op jit(solution)/shard_map/ppermute | solution.py:369
  75.2 8.3 %collective-permute-start.24 = (bf16[4,9,32,128]{3,2,1,0:T(8,128)(2,1)S(1)}, bf16[4,9,32,128]{3,2,1,0:T(8,128)(2,1)S(1)}, u32[]{:S(2)}, u32[]{:S(2)}) collective-permute-start(bf16[4,9,32,128]{3,2,1,0:T(8,128)(2,1)S(1)} %slice.21), channel_id=1, source_target_pairs={{0,6},{2,0},{4,2},{6,4},{8,14},{10,8},{12,10},{14,12},{1,7},{3,1},... | collective-permute-start | bytes 884744 | tf_op jit(solution)/shard_map/ppermute | solution.py:430
  76.8 10.7 %collective-permute-start.26 = (bf16[8,9,32,128]{3,2,1,0:T(8,128)(2,1)S(1)}, bf16[8,9,32,128]{3,2,1,0:T(8,128)(2,1)S(1)}, u32[]{:S(2)}, u32[]{:S(2)}) collective-permute-start(bf16[8,9,32,128]{3,2,1,0:T(8,128)(2,1)S(1)} %collective-permute-done.21.refs_12_), channel_id=1, source_target_pairs={{0,16},{16,0},{32,48},{48,32},{64,80},{80,64},{96,112},{112,96},{1... | collective-permute-start | bytes 1769480 | tf_op jit(solution)/shard_map/ppermute | solution.py:375
  80.1 7.5 %collective-permute-start.27 = (bf16[8,9,32,128]{3,2,1,0:T(8,128)(2,1)S(1)}, bf16[8,9,32,128]{3,2,1,0:T(8,128)(2,1)S(1)}, u32[]{:S(2)}, u32[]{:S(2)}) collective-permute-start(bf16[8,9,32,128]{3,2,1,0:T(8,128)(2,1)S(1)} %collective-permute-done.22.refs_13_), channel_id=1, source_target_pairs={{0,16},{16,0},{32,48},{48,32},{64,80},{80,64},{96,112},{112,96},{1... | collective-permute-start | bytes 1769480 | tf_op jit(solution)/shard_map/ppermute | solution.py:375
  83.5 10.2 %collective-permute-start.13 = (bf16[52,32,128]{2,1,0:T(8,128)(2,1)S(1)}, bf16[52,32,128]{2,1,0:T(8,128)(2,1)S(1)}, u32[]{:S(2)}, u32[]{:S(2)}) collective-permute-start(bf16[52,32,128]{2,1,0:T(8,128)(2,1)S(1)} %collective-permute-done.11.refs_7_), channel_id=1, source_target_pairs={{0,32},{16,48},{32,64},{48,80},{64,96},{80,112},{96,128},{112,144}... | collective-permute-start | bytes 1277960 | tf_op jit(solution)/shard_map/ppermute | solution.py:366
  121.9 11.5 %collective-permute-start.30 = (bf16[256,512]{1,0:T(8,128)(2,1)S(1)}, bf16[256,512]{1,0:T(8,128)(2,1)S(1)}, u32[]{:S(2)}, u32[]{:S(2)}) collective-permute-start(bf16[256,512]{1,0:T(8,128)(2,1)S(1)} %slice.19), channel_id=1, source_target_pairs={{0,16},{16,0},{32,48},{48,32},{64,80},{80,64},{96,112},{112,96},{1... | collective-permute-start | bytes 786440 | tf_op jit(solution)/shard_map/ppermute | solution.py:375
  126.7 16.0 %all-to-all-start = ((f32[32,1,8]{2,1,0:T(1,128)}), f32[32,1,8]{2,1,0:T(1,128)S(1)}, u32[]{:S(2)}, u32[]{:S(2)}) async-start(f32[32,1,8]{2,1,0:T(1,128)} %broadcast_in_dim.8), calls=%async_computation | async-start | bytes 32768 | tf_op jit(solution)/shard_map/all_to_all | solution.py:479
  (42 other events, 385.6 us)

commit v3 on v2

--- a/solution.py
+++ b/solution.py
@@ -124,6 +124,21 @@
         cp.wait()
 
 
+def clip_kernel(everyone, w_uq, w_uk, clipped_uq, clipped_uk):
+    head_max = everyone[0]
+    for n in range(1, 32):
+        head_max = jnp.maximum(head_max, everyone[n])
+    ratio = CLIP / jnp.maximum(head_max, CLIP)
+    root = jnp.sqrt(ratio)
+    for out, w, width in ((clipped_uq, w_uq, NOPE + ROPE), (clipped_uk, w_uk, NOPE)):
+        lane = lax.broadcasted_iota(jnp.int32, (1, 8 * width), 1)
+        factor = jnp.ones((1, 8 * width), jnp.float32)
+        for h in range(8):
+            here = jnp.where(lane < h * width + NOPE, root[:, h : h + 1], ratio[:, h : h + 1])
+            factor = jnp.where(lane >= h * width, here, factor)
+        out[...] = (w[...].astype(jnp.float32) * factor).astype(jnp.bfloat16)
+
+
 def label_of(bounds, p):
     label = jnp.zeros_like(p)
     for b in bounds:
@@ -138,9 +153,9 @@
 
 def attend_kernel(order, seg, *refs):
     q_in, w_in, cs, pieces = refs[:2], refs[2:10], refs[10], (refs[11:16], refs[16:21])
-    out, hm = refs[21:23]
-    q, wp, w, kvw, lat, rope, kn, v, kr, qs, sbuf, mx, rm, acc, total, step_i, step_ch, need = refs[23:41]
-    qsem, wsem, ksem = refs[41:]
+    out, out_send, hm_out = refs[21:24]
+    hm, q, wp, w, kvw, lat, rope, kn, v, kr, qs, sbuf, mx, rm, acc, total, step_i, step_ch, need = refs[24:43]
+    qsem, wsem, ksem = refs[43:]
     m = where_am_i()
 
     def block_of(i):
@@ -307,10 +322,12 @@
             top = jnp.broadcast_to(jnp.max(mx[i, h], axis=1, keepdims=True), (BLK, 128))
             rm[i, h] = top * to_exp2
             best = jnp.max(top, axis=0, keepdims=True) * scale
-            hm[h : h + 1, :] = jnp.maximum(hm[h : h + 1, :], best)
+            best = jnp.where(lane[:1] == m["c"] * 4 + h, best, masked_value)
+            hm[:1, :] = jnp.maximum(hm[:1, :], best)
         return carry
 
     lax.fori_loop(0, 4, finish_max, 0)
+    hm_out[...] = jnp.broadcast_to(hm[:1, :8].reshape(1, 1, 8), (32, 1, 8))
 
     def mix(steps):
         for i, ch, slot in steps:
@@ -338,14 +355,16 @@
 
     lax.fori_loop(0, pairs, mix_pair, 0)
 
-    def finish(i, carry):
-        rows = pl.ds(pl.multiple_of(i * BLK, BLK), BLK)
-        for h in range(4):
-            whole = jnp.sum(total[i, h], axis=1, keepdims=True)
-            out[rows, h * 128 : (h + 1) * 128] = (acc[i, h] / whole).astype(bf16)
-        return carry
-
-    lax.fori_loop(0, 4, finish, 0)
+    for to, first_block in ((out, 0), (out_send, 2)):
+
+        def finish(i, carry, to=to, first_block=first_block):
+            rows = pl.ds(pl.multiple_of(i * BLK, BLK), BLK)
+            for h in range(4):
+                whole = jnp.sum(total[i + first_block, h], axis=1, keepdims=True)
+                to[rows, h * 128 : (h + 1) * 128] = (acc[i + first_block, h] / whole).astype(bf16)
+            return carry
+
+        lax.fori_loop(0, 2, finish, 0)
 
 
 def shift_seq(by):
@@ -432,15 +451,17 @@
     k_sib = [swap(p) for p in k_own]
 
     vm = pltpu.VMEM
-    ctx, hm = pl.pallas_call(
+    ctx, ctx_send, everyone = pl.pallas_call(
         attend_kernel,
         out_shape=[
-            jax.ShapeDtypeStruct((512, 512), bf16),
-            jax.ShapeDtypeStruct((8, 128), f32),
+            jax.ShapeDtypeStruct((256, 512), bf16),
+            jax.ShapeDtypeStruct((256, 512), bf16),
+            jax.ShapeDtypeStruct((32, 1, 8), f32),
         ],
         in_specs=[SMEM, VMEM] + [ANY] * 10 + [VMEM] + [ANY] * 10,
-        out_specs=[VMEM] * 2,
+        out_specs=[VMEM] * 3,
         scratch_shapes=[
+            vm((8, 128), f32),
             vm((2, 256, 1536), bf16),
             vm((8, 52, 32, 128), bf16),
             vm((1536, 768), bf16),
@@ -470,27 +491,14 @@
         name="attend",
     )(block_order, segment_ids[0].reshape(32, 128), q_own, q_sib, *w_ring, cs, *k_own, *k_sib)
 
-    local_max = hm[:4, 0]
-    low = jnp.full((4,), masked_value, f32)
-    both = jnp.where(
-        c == 0, jnp.concatenate([local_max, low]), jnp.concatenate([low, local_max])
-    )
-    everyone = jnp.broadcast_to(both, (32, 8))
     everyone = lax.all_to_all(everyone, ("seq", "dp"), split_axis=0, concat_axis=0, tiled=True)
-    got = swap(ctx[256:])
-    own = ctx[:256]
+    got = swap(ctx_send)
     first = c == 0
-    context = jnp.concatenate([jnp.where(first, own, got), jnp.where(first, got, own)], axis=1)
+    context = jnp.concatenate([jnp.where(first, ctx, got), jnp.where(first, got, ctx)], axis=1)
     everyone, context = lax.optimization_barrier((everyone, context))
-    head_max = jnp.max(everyone, axis=0)
-    ratio = CLIP / jnp.maximum(head_max, CLIP)
-    root = jnp.sqrt(ratio)
-    factors = jnp.concatenate(
-        [jnp.broadcast_to(root[:, None], (8, NOPE)), jnp.broadcast_to(ratio[:, None], (8, ROPE))], axis=1
-    ).reshape(8 * (NOPE + ROPE))
-    clipped_uq = (w_uq.astype(f32) * factors[None, :]).astype(bf16)
-    clipped_uk = (w_uk.astype(f32) * jnp.repeat(root, NOPE)[None, :]).astype(bf16)
-
+    clipped_uq, clipped_uk = call(
+        clip_kernel, [((96, 1536), bf16), ((32, 1024), bf16)], (everyone, w_uq, w_uk)
+    )
     return (context[None], clipped_uq, clipped_uk)
 
 

time: 145 us -> 143 us (0.986)
  local copies, waits for them, and re-layouts: 5.98 us -> 3.77 us
  Pallas kernels: 34.5 us -> 36.3 us
    pallas_call x4 -> x5, Pallas kernels: 8.17 us -> 10 us  [call(): pl.pallas_call(kernel, out_shape=outs, in_specs=specs or [VMEM] * len(arg...]
    unnamed x71 -> x65, local copies, waits for them, and re-layouts: 3.86 us -> 3.7 us
where the time goes in v3:
time: 143 us
  starting transfers between devices  52.3 us (37%)
  waiting for transfers between devices  47.4 us (33%)
  Pallas kernels  36.3 us (25%)
  local copies, waits for them, and re-layouts  3.77 us (3%)
  other arithmetic  1.85 us (1%)
    pallas_call x1, Pallas kernels, on_device(): pl.pallas_call(attend_kernel, out_shape=[jax.ShapeDtypeStruct((256, 512),...  26.3 us
    ppermute x8, waiting for transfers between devices, ring(): up = lax.ppermute(up, 'seq', shift_seq(1))  22.1 us
    ppermute x9, starting transfers between devices, swap(): return lax.ppermute(x, 'seq', SWAP)  21.2 us
    ppermute x6, starting transfers between devices, ring(): dn = lax.ppermute(dn, 'seq', shift_seq(-1))  13.7 us
    ppermute x3, waiting for transfers between devices, on_device(): lax.ppermute(q_x, 'tp', shift_y(by))  11.3 us
    pallas_call x5, Pallas kernels, call(): pl.pallas_call(kernel, out_shape=outs, in_specs=specs or [VMEM] * len(arg...  10 us
    all_to_all x1, waiting for transfers between devices, on_device(): lax.all_to_all(everyone, ('seq', 'dp'), split_axis=0, concat_axis=0, tile...  7.4 us
    all_to_all x1, starting transfers between devices, on_device(): lax.all_to_all(everyone, ('seq', 'dp'), split_axis=0, concat_axis=0, tile...  6.75 us
  transfers between devices with their start and end apart: 32, of which 14 were waited for; matrix products, arithmetic and copies ran while one was open for 1% of the time, Pallas kernels for 3%

profile of v3, /device:TPU:1, one launch (start us, length us, event | category | flops | bytes accessed | tf_op | source)
XLA Modules:
  0.0 142.6 jit_solution(1685014884257000986)
XLA Ops:
  0.6 2.1 %shard_map.103 = (bf16[256,256]{1,0:T(8,128)(2,1)}, bf16[18,32,128]{2,1,0:T(8,128)(2,1)}, bf16[18,32,128]{2,1,0:T(8,128)(2,1)}, bf16[8,32,128]{2,1,0:T(8,128)(2,1)}, bf16[8,32,128]{2,1,0:T(8,128)(2,1)}) custom-call(bf16[192,256]{1,0:T(8,128)(2,1)} %bitcast.12, bf16[64,256]{1,0:T(8,128)(2,1)} %bitcast.13, bf16[96,1536]{1,0:T(8,128)(2,1)} %w_uq.3, ...), custom_call_target="tpu_custom_call" | custom-call | flops 1048576 | bytes 1114112 | tf_op jit(solution)/shard_map/pallas_call | solution.py:400
  2.7 3.2 %collective-permute-start.1 = (bf16[18,32,128]{2,1,0:T(8,128)(2,1)}, bf16[18,32,128]{2,1,0:T(8,128)(2,1)S(1)}, u32[]{:S(2)}, u32[]{:S(2)}) collective-permute-start(bf16[18,32,128]{2,1,0:T(8,128)(2,1)} %get-tuple-element.23), channel_id=1, source_target_pairs={{0,16},{16,0},{32,48},{48,32},{64,80},{80,64},{96,112},{112,96},{1... | collective-permute-start | bytes 442376 | tf_op jit(solution)/shard_map/ppermute | solution.py:394
  6.0 2.0 %shard_map.104 = (f32[512,256]{1,0:T(8,128)}, bf16[32,128]{1,0:T(8,128)(2,1)}) custom-call(s32[1,32]{1,0:T(1,128)} %order.3, bf16[64,256]{1,0:T(8,128)(2,1)} %bitcast.14), custom_call_target="tpu_custom_call" | custom-call | flops 1048576 | bytes 1064960 | tf_op jit(solution)/shard_map/pallas_call | solution.py:400
  8.1 3.0 %collective-permute-done.kq_x = bf16[256,256]{1,0:T(8,128)(2,1)S(1)} collective-permute-done((bf16[256,256]{1,0:T(8,128)(2,1)}, bf16[256,256]{1,0:T(8,128)(2,1)S(1)}, u32[]{:S(2)}, u32[]{:S(2)}) %collective-permute-start) | collective-permute-done | bytes 131104 | tf_op jit(solution)/shard_map/ppermute | solution.py:418
  11.8 2.1 %shard_map.105 = (bf16[9,32,128]{2,1,0:T(8,128)(2,1)}, bf16[52,32,128]{2,1,0:T(8,128)(2,1)}, bf16[256,384]{1,0:T(8,128)(2,1)}) custom-call(bf16[256,256]{1,0:T(8,128)(2,1)} %get-tuple-element.20.kq, bf16[256,256]{1,0:T(8,128)(2,1)} %copy-done.5, bf16[32,128]{1,0:T(8,128)(2,1)} %get-tuple-element.21.share, bf16[18,32,128]{2,1,0:T(8,128)(2,1)} %get-tuple-element.22.w_mine, ...), custom_call_target="tpu_custom_call" | custom-call | flops 1048576 | bytes 1392640 | tf_op jit(solution)/shard_map/pallas_call | solution.py:400
  13.9 3.9 %collective-permute-start.15 = (bf16[9,32,128]{2,1,0:T(8,128)(2,1)}, bf16[9,32,128]{2,1,0:T(8,128)(2,1)S(1)}, u32[]{:S(2)}, u32[]{:S(2)}) collective-permute-start(bf16[9,32,128]{2,1,0:T(8,128)(2,1)} %get-tuple-element.29.refs_0_), channel_id=1, source_target_pairs={{0,224},{16,240},{32,0},{48,16},{64,32},{80,48},{96,64},{112,80},{... | collective-permute-start | bytes 221192 | tf_op jit(solution)/shard_map/ppermute | solution.py:388
  17.7 1.9 %collective-permute-done.14.refs_1_ = bf16[9,32,128]{2,1,0:T(8,128)(2,1)S(1)} collective-permute-done((bf16[9,32,128]{2,1,0:T(8,128)(2,1)}, bf16[9,32,128]{2,1,0:T(8,128)(2,1)S(1)}, u32[]{:S(2)}, u32[]{:S(2)}) %collective-permute-start.14) | collective-permute-done | bytes 73760 | tf_op jit(solution)/shard_map/ppermute | solution.py:385
  19.7 2.7 %collective-permute-start.17 = (bf16[9,32,128]{2,1,0:T(8,128)(2,1)S(1)}, bf16[9,32,128]{2,1,0:T(8,128)(2,1)S(1)}, u32[]{:S(2)}, u32[]{:S(2)}) collective-permute-start(bf16[9,32,128]{2,1,0:T(8,128)(2,1)S(1)} %collective-permute-done.15.refs_2_), channel_id=1, source_target_pairs={{0,224},{16,240},{32,0},{48,16},{64,32},{80,48},{96,64},{112,80},{... | collective-permute-start | bytes 221192 | tf_op jit(solution)/shard_map/ppermute | solution.py:388
  25.4 2.7 %collective-permute-start.19 = (bf16[9,32,128]{2,1,0:T(8,128)(2,1)S(1)}, bf16[9,32,128]{2,1,0:T(8,128)(2,1)S(1)}, u32[]{:S(2)}, u32[]{:S(2)}) collective-permute-start(bf16[9,32,128]{2,1,0:T(8,128)(2,1)S(1)} %collective-permute-done.17.refs_4_), channel_id=1, source_target_pairs={{0,224},{16,240},{32,0},{48,16},{64,32},{80,48},{96,64},{112,80},{... | collective-permute-start | bytes 221192 | tf_op jit(solution)/shard_map/ppermute | solution.py:388
  28.5 2.7 %collective-permute-start.4 = (bf16[256,384]{1,0:T(8,128)(2,1)}, bf16[256,384]{1,0:T(8,128)(2,1)S(1)}, u32[]{:S(2)}, u32[]{:S(2)}) collective-permute-start(bf16[256,384]{1,0:T(8,128)(2,1)} %get-tuple-element.26), channel_id=1, source_target_pairs={{0,6},{2,0},{4,2},{6,4},{8,14},{10,8},{12,10},{14,12},{1,7},{3,1},... | collective-permute-start | bytes 589832 | tf_op jit(solution)/shard_map/ppermute | solution.py:436
  31.3 1.9 %collective-permute-done.20.refs_7_ = bf16[9,32,128]{2,1,0:T(8,128)(2,1)S(1)} collective-permute-done((bf16[9,32,128]{2,1,0:T(8,128)(2,1)S(1)}, bf16[9,32,128]{2,1,0:T(8,128)(2,1)S(1)}, u32[]{:S(2)}, u32[]{:S(2)}) %collective-permute-start.20) | collective-permute-done | bytes 73760 | tf_op jit(solution)/shard_map/ppermute | solution.py:385
  33.9 2.0 %shard_map.106.refs_11_ = bf16[8,9,32,128]{3,2,1,0:T(8,128)(2,1)} custom-call(bf16[9,32,128]{2,1,0:T(8,128)(2,1)} %get-tuple-element.29.refs_0_, bf16[9,32,128]{2,1,0:T(8,128)(2,1)} %copy-done.6, bf16[9,32,128]{2,1,0:T(8,128)(2,1)} %copy-done.7, bf16[9,32,128]{2,1,0:T(8,128)(2,1)} %copy-done.8, bf16[9,32,128]{2,1,0:T(8,128)(2,1)} %copy-done.9, ...), custom_call_target="tpu_custom_call" | custom-call | flops 1048576 | bytes 1179648 | tf_op jit(solution)/shard_map/pallas_call | solution.py:400
  37.0 2.7 %collective-permute-start.5 = (bf16[256,384]{1,0:T(8,128)(2,1)S(1)}, bf16[256,384]{1,0:T(8,128)(2,1)S(1)}, u32[]{:S(2)}, u32[]{:S(2)}) collective-permute-start(bf16[256,384]{1,0:T(8,128)(2,1)S(1)} %copy-done.1), channel_id=1, source_target_pairs={{0,4},{2,6},{4,0},{6,2},{8,12},{10,14},{12,8},{14,10},{1,5},{3,7},... | collective-permute-start | bytes 589832 | tf_op jit(solution)/shard_map/ppermute | solution.py:436
  39.9 11.3 %collective-permute-done.5 = bf16[256,384]{1,0:T(8,128)(2,1)S(1)} collective-permute-done((bf16[256,384]{1,0:T(8,128)(2,1)S(1)}, bf16[256,384]{1,0:T(8,128)(2,1)S(1)}, u32[]{:S(2)}, u32[]{:S(2)}) %collective-permute-start.5) | collective-permute-done | bytes 196640 | tf_op jit(solution)/shard_map/ppermute | solution.py:436
  51.2 7.3 %collective-permute-start.6 = (bf16[256,1536]{1,0:T(8,128)(2,1)S(1)}, bf16[256,1536]{1,0:T(8,128)(2,1)S(1)}, u32[]{:S(2)}, u32[]{:S(2)}) collective-permute-start(bf16[256,1536]{1,0:T(8,128)(2,1)S(1)} %constant_dynamic-update-slice_fusion.refs_0_), channel_id=1, source_target_pairs={{0,16},{16,0},{32,48},{48,32},{64,80},{80,64},{96,112},{112,96},{1... | collective-permute-start | bytes 2359304 | tf_op jit(solution)/shard_map/ppermute | solution.py:394
  58.6 2.6 %collective-permute-start.10 = (bf16[52,32,128]{2,1,0:T(8,128)(2,1)S(1)}, bf16[52,32,128]{2,1,0:T(8,128)(2,1)S(1)}, u32[]{:S(2)}, u32[]{:S(2)}) collective-permute-start(bf16[52,32,128]{2,1,0:T(8,128)(2,1)S(1)} %collective-permute-done.8.refs_4_), channel_id=1, source_target_pairs={{0,224},{16,240},{32,0},{48,16},{64,32},{80,48},{96,64},{112,80},{... | collective-permute-start | bytes 1277960 | tf_op jit(solution)/shard_map/ppermute | solution.py:388
  61.9 9.3 %collective-permute-done.9.refs_5_ = bf16[52,32,128]{2,1,0:T(8,128)(2,1)S(1)} collective-permute-done((bf16[52,32,128]{2,1,0:T(8,128)(2,1)}, bf16[52,32,128]{2,1,0:T(8,128)(2,1)S(1)}, u32[]{:S(2)}, u32[]{:S(2)}) %collective-permute-start.9) | collective-permute-done | bytes 426016 | tf_op jit(solution)/shard_map/ppermute | solution.py:385
  76.8 2.2 %collective-permute-start.26 = (bf16[8,9,32,128]{3,2,1,0:T(8,128)(2,1)S(1)}, bf16[8,9,32,128]{3,2,1,0:T(8,128)(2,1)S(1)}, u32[]{:S(2)}, u32[]{:S(2)}) collective-permute-start(bf16[8,9,32,128]{3,2,1,0:T(8,128)(2,1)S(1)} %collective-permute-done.21.refs_12_), channel_id=1, source_target_pairs={{0,16},{16,0},{32,48},{48,32},{64,80},{80,64},{96,112},{112,96},{1... | collective-permute-start | bytes 1769480 | tf_op jit(solution)/shard_map/ppermute | solution.py:394
  83.5 2.5 %collective-permute-start.28 = (bf16[4,9,32,128]{3,2,1,0:T(8,128)(2,1)S(1)}, bf16[4,9,32,128]{3,2,1,0:T(8,128)(2,1)S(1)}, u32[]{:S(2)}, u32[]{:S(2)}) collective-permute-start(bf16[4,9,32,128]{3,2,1,0:T(8,128)(2,1)S(1)} %collective-permute-done.23.refs_14_), channel_id=1, source_target_pairs={{0,16},{16,0},{32,48},{48,32},{64,80},{80,64},{96,112},{112,96},{1... | collective-permute-start | bytes 884744 | tf_op jit(solution)/shard_map/ppermute | solution.py:394
  88.4 5.2 %collective-permute-done.13.refs_9_ = bf16[52,32,128]{2,1,0:T(8,128)(2,1)S(1)} collective-permute-done((bf16[52,32,128]{2,1,0:T(8,128)(2,1)S(1)}, bf16[52,32,128]{2,1,0:T(8,128)(2,1)S(1)}, u32[]{:S(2)}, u32[]{:S(2)}) %collective-permute-start.13) | collective-permute-done | bytes 426016 | tf_op jit(solution)/shard_map/ppermute | solution.py:385
  94.5 26.3 %attend.1 = (bf16[256,512]{1,0:T(8,128)(2,1)}, bf16[256,512]{1,0:T(8,128)(2,1)}, f32[32,1,8]{2,1,0:T(1,128)}) custom-call(s32[1,32]{1,0:T(1,128)} %order.3, s32[32,128]{1,0:T(8,128)} %bitcast.15, bf16[256,1536]{1,0:T(8,128)(2,1)} %copy-done.15, bf16[256,1536]{1,0:T(8,128)(2,1)} %copy-done.16, bf16[52,32,128]{2,1,0:T(8,128)(2,1)} %get-tuple-element.27.refs_2_, ...), custom_call_target="tpu_custom_call" | custom-call | flops 21474836480 | bytes 12582912 | tf_op jit(solution)/shard_map/attend/pallas_call | solution.py:454
  120.7 3.3 %collective-permute-start.30 = (bf16[256,512]{1,0:T(8,128)(2,1)}, bf16[256,512]{1,0:T(8,128)(2,1)S(1)}, u32[]{:S(2)}, u32[]{:S(2)}) collective-permute-start(bf16[256,512]{1,0:T(8,128)(2,1)} %get-tuple-element.32), channel_id=1, source_target_pairs={{0,16},{16,0},{32,48},{48,32},{64,80},{80,64},{96,112},{112,96},{1... | collective-permute-start | bytes 786440 | tf_op jit(solution)/shard_map/ppermute | solution.py:394
  124.1 6.8 %all-to-all-start = ((f32[32,1,8]{2,1,0:T(1,128)}), f32[32,1,8]{2,1,0:T(1,128)S(1)}, u32[]{:S(2)}, u32[]{:S(2)}) async-start(f32[32,1,8]{2,1,0:T(1,128)} %get-tuple-element.30), calls=%async_computation | async-start | bytes 32768 | tf_op jit(solution)/shard_map/all_to_all | solution.py:494
  132.7 7.4 %all-to-all-done.everyone = f32[32,1,8]{2,1,0:T(1,128)S(1)} async-done(((f32[32,1,8]{2,1,0:T(1,128)}), f32[32,1,8]{2,1,0:T(1,128)S(1)}, u32[]{:S(2)}, u32[]{:S(2)}) %all-to-all-start) | async-done | bytes 1056 | tf_op jit(solution)/shard_map/all_to_all | solution.py:494
  (116 shorter events, 24.6 us)
Async XLA Ops:
  2.7 8.4 %collective-permute-start.1 = (bf16[18,32,128]{2,1,0:T(8,128)(2,1)}, bf16[18,32,128]{2,1,0:T(8,128)(2,1)S(1)}, u32[]{:S(2)}, u32[]{:S(2)}) collective-permute-start(bf16[18,32,128]{2,1,0:T(8,128)(2,1)} %get-tuple-element.23), channel_id=1, source_target_pairs={{0,16},{16,0},{32,48},{48,32},{64,80},{80,64},{96,112},{112,96},{1... | collective-permute-start | bytes 442376 | tf_op jit(solution)/shard_map/ppermute | solution.py:394
  13.9 5.8 %collective-permute-start.14 = (bf16[9,32,128]{2,1,0:T(8,128)(2,1)}, bf16[9,32,128]{2,1,0:T(8,128)(2,1)S(1)}, u32[]{:S(2)}, u32[]{:S(2)}) collective-permute-start(bf16[9,32,128]{2,1,0:T(8,128)(2,1)} %get-tuple-element.29.refs_0_), channel_id=1, source_target_pairs={{0,32},{16,48},{32,64},{48,80},{64,96},{80,112},{96,128},{112,144}... | collective-permute-start | bytes 221192 | tf_op jit(solution)/shard_map/ppermute | solution.py:385
  13.9 5.8 %collective-permute-start.15 = (bf16[9,32,128]{2,1,0:T(8,128)(2,1)}, bf16[9,32,128]{2,1,0:T(8,128)(2,1)S(1)}, u32[]{:S(2)}, u32[]{:S(2)}) collective-permute-start(bf16[9,32,128]{2,1,0:T(8,128)(2,1)} %get-tuple-element.29.refs_0_), channel_id=1, source_target_pairs={{0,224},{16,240},{32,0},{48,16},{64,32},{80,48},{96,64},{112,80},{... | collective-permute-start | bytes 221192 | tf_op jit(solution)/shard_map/ppermute | solution.py:388
  24.1 15.6 %collective-permute-start.3 = (bf16[256,384]{1,0:T(8,128)(2,1)}, bf16[256,384]{1,0:T(8,128)(2,1)S(1)}, u32[]{:S(2)}, u32[]{:S(2)}) collective-permute-start(bf16[256,384]{1,0:T(8,128)(2,1)} %get-tuple-element.26), channel_id=1, source_target_pairs={{0,2},{2,4},{4,6},{6,0},{8,10},{10,12},{12,14},{14,8},{1,3},{3,5},... | collective-permute-start | bytes 589832 | tf_op jit(solution)/shard_map/ppermute | solution.py:436
  25.4 5.9 %collective-permute-start.19 = (bf16[9,32,128]{2,1,0:T(8,128)(2,1)S(1)}, bf16[9,32,128]{2,1,0:T(8,128)(2,1)S(1)}, u32[]{:S(2)}, u32[]{:S(2)}) collective-permute-start(bf16[9,32,128]{2,1,0:T(8,128)(2,1)S(1)} %collective-permute-done.17.refs_4_), channel_id=1, source_target_pairs={{0,224},{16,240},{32,0},{48,16},{64,32},{80,48},{96,64},{112,80},{... | collective-permute-start | bytes 221192 | tf_op jit(solution)/shard_map/ppermute | solution.py:388
  28.5 11.3 %collective-permute-start.4 = (bf16[256,384]{1,0:T(8,128)(2,1)}, bf16[256,384]{1,0:T(8,128)(2,1)S(1)}, u32[]{:S(2)}, u32[]{:S(2)}) collective-permute-start(bf16[256,384]{1,0:T(8,128)(2,1)} %get-tuple-element.26), channel_id=1, source_target_pairs={{0,6},{2,0},{4,2},{6,4},{8,14},{10,8},{12,10},{14,12},{1,7},{3,1},... | collective-permute-start | bytes 589832 | tf_op jit(solution)/shard_map/ppermute | solution.py:436
  31.3 27.2 %collective-permute-start.7 = (bf16[52,32,128]{2,1,0:T(8,128)(2,1)}, bf16[52,32,128]{2,1,0:T(8,128)(2,1)}, u32[]{:S(2)}, u32[]{:S(2)}) collective-permute-start(bf16[52,32,128]{2,1,0:T(8,128)(2,1)} %get-tuple-element.27.refs_2_), channel_id=1, source_target_pairs={{0,32},{16,48},{32,64},{48,80},{64,96},{80,112},{96,128},{112,144}... | collective-permute-start | bytes 1277960 | tf_op jit(solution)/shard_map/ppermute | solution.py:385
  35.9 25.3 %collective-permute-start.21 = (bf16[8,9,32,128]{3,2,1,0:T(8,128)(2,1)}, bf16[8,9,32,128]{3,2,1,0:T(8,128)(2,1)S(1)}, u32[]{:S(2)}, u32[]{:S(2)}) collective-permute-start(bf16[8,9,32,128]{3,2,1,0:T(8,128)(2,1)} %shard_map.106.refs_11_), channel_id=1, source_target_pairs={{0,2},{2,4},{4,6},{6,0},{8,10},{10,12},{12,14},{14,8},{1,3},{3,5},... | collective-permute-start | bytes 1769480 | tf_op jit(solution)/shard_map/ppermute | solution.py:446
  37.0 14.1 %collective-permute-start.5 = (bf16[256,384]{1,0:T(8,128)(2,1)S(1)}, bf16[256,384]{1,0:T(8,128)(2,1)S(1)}, u32[]{:S(2)}, u32[]{:S(2)}) collective-permute-start(bf16[256,384]{1,0:T(8,128)(2,1)S(1)} %copy-done.1), channel_id=1, source_target_pairs={{0,4},{2,6},{4,0},{6,2},{8,12},{10,14},{12,8},{14,10},{1,5},{3,7},... | collective-permute-start | bytes 589832 | tf_op jit(solution)/shard_map/ppermute | solution.py:436
  39.8 18.8 %collective-permute-start.8 = (bf16[52,32,128]{2,1,0:T(8,128)(2,1)S(1)}, bf16[52,32,128]{2,1,0:T(8,128)(2,1)S(1)}, u32[]{:S(2)}, u32[]{:S(2)}) collective-permute-start(bf16[52,32,128]{2,1,0:T(8,128)(2,1)S(1)} %copy-done.20), channel_id=1, source_target_pairs={{0,224},{16,240},{32,0},{48,16},{64,32},{80,48},{96,64},{112,80},{... | collective-permute-start | bytes 1277960 | tf_op jit(solution)/shard_map/ppermute | solution.py:388
  51.2 25.6 %collective-permute-start.6 = (bf16[256,1536]{1,0:T(8,128)(2,1)S(1)}, bf16[256,1536]{1,0:T(8,128)(2,1)S(1)}, u32[]{:S(2)}, u32[]{:S(2)}) collective-permute-start(bf16[256,1536]{1,0:T(8,128)(2,1)S(1)} %constant_dynamic-update-slice_fusion.refs_0_), channel_id=1, source_target_pairs={{0,16},{16,0},{32,48},{48,32},{64,80},{80,64},{96,112},{112,96},{1... | collective-permute-start | bytes 2359304 | tf_op jit(solution)/shard_map/ppermute | solution.py:394
  58.5 14.8 %collective-permute-start.22 = (bf16[8,9,32,128]{3,2,1,0:T(8,128)(2,1)S(1)}, bf16[8,9,32,128]{3,2,1,0:T(8,128)(2,1)S(1)}, u32[]{:S(2)}, u32[]{:S(2)}) collective-permute-start(bf16[8,9,32,128]{3,2,1,0:T(8,128)(2,1)S(1)} %copy-done), channel_id=1, source_target_pairs={{0,6},{2,0},{4,2},{6,4},{8,14},{10,8},{12,10},{14,12},{1,7},{3,1},... | collective-permute-start | bytes 1769480 | tf_op jit(solution)/shard_map/ppermute | solution.py:447
  58.5 12.8 %collective-permute-start.9 = (bf16[52,32,128]{2,1,0:T(8,128)(2,1)}, bf16[52,32,128]{2,1,0:T(8,128)(2,1)S(1)}, u32[]{:S(2)}, u32[]{:S(2)}) collective-permute-start(bf16[52,32,128]{2,1,0:T(8,128)(2,1)} %collective-permute-done.7.refs_3_), channel_id=1, source_target_pairs={{0,32},{16,48},{32,64},{48,80},{64,96},{80,112},{96,128},{112,144}... | collective-permute-start | bytes 1277960 | tf_op jit(solution)/shard_map/ppermute | solution.py:385
  58.6 13.8 %collective-permute-start.10 = (bf16[52,32,128]{2,1,0:T(8,128)(2,1)S(1)}, bf16[52,32,128]{2,1,0:T(8,128)(2,1)S(1)}, u32[]{:S(2)}, u32[]{:S(2)}) collective-permute-start(bf16[52,32,128]{2,1,0:T(8,128)(2,1)S(1)} %collective-permute-done.8.refs_4_), channel_id=1, source_target_pairs={{0,224},{16,240},{32,0},{48,16},{64,32},{80,48},{96,64},{112,80},{... | collective-permute-start | bytes 1277960 | tf_op jit(solution)/shard_map/ppermute | solution.py:388
  61.2 13.9 %collective-permute-start.25 = (bf16[8,9,32,128]{3,2,1,0:T(8,128)(2,1)S(1)}, bf16[8,9,32,128]{3,2,1,0:T(8,128)(2,1)S(1)}, u32[]{:S(2)}, u32[]{:S(2)}) collective-permute-start(bf16[8,9,32,128]{3,2,1,0:T(8,128)(2,1)S(1)} %copy-done), channel_id=1, source_target_pairs={{0,16},{16,0},{32,48},{48,32},{64,80},{80,64},{96,112},{112,96},{1... | collective-permute-start | bytes 1769480 | tf_op jit(solution)/shard_map/ppermute | solution.py:394
  71.2 8.8 %collective-permute-start.23 = (bf16[4,9,32,128]{3,2,1,0:T(8,128)(2,1)S(1)}, bf16[4,9,32,128]{3,2,1,0:T(8,128)(2,1)S(1)}, u32[]{:S(2)}, u32[]{:S(2)}) collective-permute-start(bf16[4,9,32,128]{3,2,1,0:T(8,128)(2,1)S(1)} %slice.8), channel_id=1, source_target_pairs={{0,2},{2,4},{4,6},{6,0},{8,10},{10,12},{12,14},{14,8},{1,3},{3,5},... | collective-permute-start | bytes 884744 | tf_op jit(solution)/shard_map/ppermute | solution.py:448
  72.4 11.1 %collective-permute-start.11 = (bf16[52,32,128]{2,1,0:T(8,128)(2,1)S(1)}, bf16[52,32,128]{2,1,0:T(8,128)(2,1)S(1)}, u32[]{:S(2)}, u32[]{:S(2)}) collective-permute-start(bf16[52,32,128]{2,1,0:T(8,128)(2,1)S(1)} %collective-permute-done.9.refs_5_), channel_id=1, source_target_pairs={{0,32},{16,48},{32,64},{48,80},{64,96},{80,112},{96,128},{112,144}... | collective-permute-start | bytes 1277960 | tf_op jit(solution)/shard_map/ppermute | solution.py:385
  73.3 12.7 %collective-permute-start.12 = (bf16[52,32,128]{2,1,0:T(8,128)(2,1)S(1)}, bf16[52,32,128]{2,1,0:T(8,128)(2,1)S(1)}, u32[]{:S(2)}, u32[]{:S(2)}) collective-permute-start(bf16[52,32,128]{2,1,0:T(8,128)(2,1)S(1)} %collective-permute-done.10.refs_6_), channel_id=1, source_target_pairs={{0,224},{16,240},{32,0},{48,16},{64,32},{80,48},{96,64},{112,80},{... | collective-permute-start | bytes 1277960 | tf_op jit(solution)/shard_map/ppermute | solution.py:388
  75.2 8.3 %collective-permute-start.24 = (bf16[4,9,32,128]{3,2,1,0:T(8,128)(2,1)S(1)}, bf16[4,9,32,128]{3,2,1,0:T(8,128)(2,1)S(1)}, u32[]{:S(2)}, u32[]{:S(2)}) collective-permute-start(bf16[4,9,32,128]{3,2,1,0:T(8,128)(2,1)S(1)} %slice.9), channel_id=1, source_target_pairs={{0,6},{2,0},{4,2},{6,4},{8,14},{10,8},{12,10},{14,12},{1,7},{3,1},... | collective-permute-start | bytes 884744 | tf_op jit(solution)/shard_map/ppermute | solution.py:449
  76.8 10.7 %collective-permute-start.26 = (bf16[8,9,32,128]{3,2,1,0:T(8,128)(2,1)S(1)}, bf16[8,9,32,128]{3,2,1,0:T(8,128)(2,1)S(1)}, u32[]{:S(2)}, u32[]{:S(2)}) collective-permute-start(bf16[8,9,32,128]{3,2,1,0:T(8,128)(2,1)S(1)} %collective-permute-done.21.refs_12_), channel_id=1, source_target_pairs={{0,16},{16,0},{32,48},{48,32},{64,80},{80,64},{96,112},{112,96},{1... | collective-permute-start | bytes 1769480 | tf_op jit(solution)/shard_map/ppermute | solution.py:394
  80.0 7.5 %collective-permute-start.27 = (bf16[8,9,32,128]{3,2,1,0:T(8,128)(2,1)S(1)}, bf16[8,9,32,128]{3,2,1,0:T(8,128)(2,1)S(1)}, u32[]{:S(2)}, u32[]{:S(2)}) collective-permute-start(bf16[8,9,32,128]{3,2,1,0:T(8,128)(2,1)S(1)} %collective-permute-done.22.refs_13_), channel_id=1, source_target_pairs={{0,16},{16,0},{32,48},{48,32},{64,80},{80,64},{96,112},{112,96},{1... | collective-permute-start | bytes 1769480 | tf_op jit(solution)/shard_map/ppermute | solution.py:394
  83.4 10.2 %collective-permute-start.13 = (bf16[52,32,128]{2,1,0:T(8,128)(2,1)S(1)}, bf16[52,32,128]{2,1,0:T(8,128)(2,1)S(1)}, u32[]{:S(2)}, u32[]{:S(2)}) collective-permute-start(bf16[52,32,128]{2,1,0:T(8,128)(2,1)S(1)} %collective-permute-done.11.refs_7_), channel_id=1, source_target_pairs={{0,32},{16,48},{32,64},{48,80},{64,96},{80,112},{96,128},{112,144}... | collective-permute-start | bytes 1277960 | tf_op jit(solution)/shard_map/ppermute | solution.py:385
  120.7 10.1 %collective-permute-start.30 = (bf16[256,512]{1,0:T(8,128)(2,1)}, bf16[256,512]{1,0:T(8,128)(2,1)S(1)}, u32[]{:S(2)}, u32[]{:S(2)}) collective-permute-start(bf16[256,512]{1,0:T(8,128)(2,1)} %get-tuple-element.32), channel_id=1, source_target_pairs={{0,16},{16,0},{32,48},{48,32},{64,80},{80,64},{96,112},{112,96},{1... | collective-permute-start | bytes 786440 | tf_op jit(solution)/shard_map/ppermute | solution.py:394
  124.1 16.0 %all-to-all-start = ((f32[32,1,8]{2,1,0:T(1,128)}), f32[32,1,8]{2,1,0:T(1,128)S(1)}, u32[]{:S(2)}, u32[]{:S(2)}) async-start(f32[32,1,8]{2,1,0:T(1,128)} %get-tuple-element.30), calls=%async_computation | async-start | bytes 32768 | tf_op jit(solution)/shard_map/all_to_all | solution.py:494
  (39 other events, 362.6 us)

commit v4 on v3

--- a/solution.py
+++ b/solution.py
@@ -44,6 +44,10 @@
 
 
 RING = [0, -1, 1, -2, 2, -3, 3, -4]
+
+
+def ring_shift(j):
+    return jnp.where(lax.rem(j, 2) == 1, -((j + 1) // 2), (j + 1) // 2)
 
 
 W_COLS = [[h * 192 + e * 32 for e in range(4)] for h in range(4)] + [
@@ -152,10 +156,11 @@
 
 
 def attend_kernel(order, seg, *refs):
-    q_in, w_in, cs, pieces = refs[:2], refs[2:10], refs[10], (refs[11:16], refs[16:21])
+    q_in, w_in, refs = refs[:2], refs[2:11], refs[1:]
+    cs, pieces = refs[10], (refs[11:16], refs[16:21])
     out, out_send, hm_out = refs[21:24]
-    hm, q, wp, w, kvw, lat, rope, kn, v, kr, qs, sbuf, mx, rm, acc, total, step_i, step_ch, need = refs[24:43]
-    qsem, wsem, ksem = refs[43:]
+    hm, q, wp, w, kvw, lat, rope, kn, v, kr, qs, sbuf, mx, rm, acc, total, step_i, step_ch, need, use = refs[24:44]
+    qsem, wsem, ksem = refs[44:]
     m = where_am_i()
 
     def block_of(i):
@@ -166,8 +171,10 @@
     first, second = [], []
     for half in range(2):
         first.append(pltpu.make_async_copy(q_in[half], q.at[half], qsem.at[half]))
-    for j in range(8):
+    for j in range(7):
         first.append(pltpu.make_async_copy(w_in[j], wp.at[j], wsem.at[j]))
+    for e in range(2):
+        first.append(pltpu.make_async_copy(w_in[7 + e], wp.at[7, pl.ds(26 * e, 26)], wsem.at[7 + e]))
     for core in range(2):
         own, up, dn, f1, f2 = pieces[core]
         for n, (src, plane, start, count, dy) in enumerate(
@@ -206,7 +213,6 @@
         count = lax.fori_loop(lo, hi, add, count)
     step_i[count] = 3
     step_ch[count] = block_of(3) // 2
-    odd = lax.rem(count, 2)
 
     for cp in first:
         cp.wait()
@@ -245,17 +251,21 @@
     for cp in second:
         cp.wait()
 
-    def project(i, carry):
-        j = lax.rem(i, 8)
-        s = (j + 1) // 2
-        dz = jnp.where(lax.rem(j, 2) == 1, -s, s)
-        zz = lax.rem(m["z"] + dz + 8, 8)
-        cc = jnp.where(i < 8, m["c"], 1 - m["c"])
-        base = (zz * 2 + cc) * 2
-
-        @pl.when((need[order[0, base] // 2] + need[order[0, base + 1] // 2]) > 0)
-        def _():
-            x = jnp.concatenate([lat[n, i].reshape(256, 128) for n in range(4)], axis=1)
+    def place(i):
+        zz = lax.rem(m["z"] + ring_shift(lax.rem(i, 8)) + 8, 8)
+        return (zz * 2 + jnp.where(i < 8, m["c"], 1 - m["c"])) * 2
+
+    def pick(i, n):
+        base = place(i)
+        use[n] = i
+        return n + jnp.minimum(need[order[0, base] // 2] + need[order[0, base + 1] // 2], 1)
+
+    used = lax.fori_loop(0, 16, pick, jnp.int32(0))
+
+    def project(n, carry):
+        for i in (use[2 * n], use[jnp.minimum(2 * n + 1, used - 1)]):
+            base = place(i)
+            x = jnp.concatenate([lat[e, i].reshape(256, 128) for e in range(4)], axis=1)
             y = jnp.dot(x, kvw[...], preferred_element_type=f32)
             fold = rope[i]
             for b in range(2):
@@ -268,10 +278,9 @@
                 kr[pl.ds(pb, BLK), :] = jnp.concatenate(
                     [fold[:, b * 64 : b * 64 + 64], apart.astype(bf16)], axis=1
                 )
-
         return carry
 
-    lax.fori_loop(0, 16, project, 0)
+    lax.fori_loop(0, (used + 1) // 2, project, 0)
 
     def scores(i, ch):
         keys = pl.ds(pl.multiple_of(ch * CHUNK, CHUNK), CHUNK)
@@ -302,9 +311,10 @@
 
     lax.fori_loop(0, 4, diagonal, 0)
 
-    def score_pair(n, carry):
+    def score_four(n, carry):
         picks = []
-        for g in (2 * n, jnp.minimum(2 * n + 1, count - 1)):
+        for e in range(4):
+            g = jnp.minimum(4 * n + e, count - 1)
             i, ch = step_i[g], step_ch[g]
             picks.append((i, g + 4, scores(i, ch)))
         for i, slot, got in picks:
@@ -312,8 +322,8 @@
                 keep(i, slot, h, s)
         return carry
 
-    pairs = (count + odd) // 2
-    lax.fori_loop(0, pairs, score_pair, 0)
+    fours = (count + 3) // 4
+    lax.fori_loop(0, fours, score_four, 0)
 
     hm[...] = jnp.full(hm.shape, masked_value, f32)
 
@@ -347,13 +357,16 @@
 
     lax.fori_loop(0, 2, mix_diagonal, 0)
 
-    def mix_pair(n, carry):
-        a, b = 2 * n, 2 * n + 1
-        slot = jnp.where(b < count, b + 4, EMPTY)
-        mix([(step_i[a], step_ch[a], a + 4), (step_i[b], step_ch[b], slot)])
+    def mix_four(n, carry):
+        steps = []
+        for e in range(4):
+            g = 4 * n + e
+            at = jnp.minimum(g, count)
+            steps.append((step_i[at], step_ch[at], jnp.where(g < count, g + 4, EMPTY)))
+        mix(steps)
         return carry
 
-    lax.fori_loop(0, pairs, mix_pair, 0)
+    lax.fori_loop(0, fours, mix_four, 0)
 
     for to, first_block in ((out, 0), (out_send, 2)):
 
@@ -379,19 +392,23 @@
     return [(x * 4 + y, x * 4 + (y + by) % 4) for x in range(2) for y in range(4)]
 
 
-def ring(x):
+def move(x, axis, perm):
+    return lax.ppermute(x, axis, perm)
+
+
+def ring(x, last=4):
     up, dn, got = x, x, [x]
-    for s in range(1, 5):
-        up = lax.ppermute(up, "seq", shift_seq(1))
+    for s in range(1, last + 1):
+        up = move(up, "seq", shift_seq(1))
         got.append(up)
         if s < 4:
-            dn = lax.ppermute(dn, "seq", shift_seq(-1))
+            dn = move(dn, "seq", shift_seq(-1))
             got.append(dn)
     return got
 
 
 def swap(x):
-    return lax.ppermute(x, "seq", SWAP)
+    return move(x, "seq", SWAP)
 
 
 def call(kernel, outs, args, specs=None, scratch=()):
@@ -415,7 +432,7 @@
         [((256, 256), bf16)] + [((18, 32, 128), bf16)] * 2 + [((8, 32, 128), bf16)] * 2,
         (query_latent[0].T, key_latent[0].T, w_uq, w_uk, w_uv),
     )
-    kq_x = lax.ppermute(kq, "tp", XSWAP)
+    kq_x = move(kq, "tp", XSWAP)
     w_other = swap(w_send)
     kv_other = swap(kv_send)
     cs, share = call(
@@ -432,8 +449,9 @@
     )
 
     k_ring = ring(k_one)
-    w_ring = ring(w_one)
-    q_parts = [q_x] + [lax.ppermute(q_x, "tp", shift_y(by)) for by in (1, -1, 2)]
+    w_ring = ring(w_one, 3)
+    w_ring += [move(w_ring[5][:26], "seq", shift_seq(1)), move(w_ring[6][26:], "seq", shift_seq(-1))]
+    q_parts = [q_x] + [move(q_x, "tp", shift_y(by)) for by in (1, -1, 2)]
     q_own = jnp.concatenate(q_parts, axis=1)
     q_sib = swap(q_own)
     (k_all,) = call(
@@ -443,10 +461,10 @@
         specs=[ANY] * 8,
         scratch=[pltpu.SemaphoreType.DMA((8,))],
     )
-    k_up = lax.ppermute(k_all, "tp", shift_y(1))
-    k_dn = lax.ppermute(k_all, "tp", shift_y(-1))
-    k_f1 = lax.ppermute(k_up[:4], "tp", shift_y(1))
-    k_f2 = lax.ppermute(k_dn[4:], "tp", shift_y(-1))
+    k_up = move(k_all, "tp", shift_y(1))
+    k_dn = move(k_all, "tp", shift_y(-1))
+    k_f1 = move(k_up[:4], "tp", shift_y(1))
+    k_f2 = move(k_dn[4:], "tp", shift_y(-1))
     k_own = [k_all, k_up, k_dn, k_f1, k_f2]
     k_sib = [swap(p) for p in k_own]
 
@@ -458,7 +476,7 @@
             jax.ShapeDtypeStruct((256, 512), bf16),
             jax.ShapeDtypeStruct((32, 1, 8), f32),
         ],
-        in_specs=[SMEM, VMEM] + [ANY] * 10 + [VMEM] + [ANY] * 10,
+        in_specs=[SMEM, VMEM] + [ANY] * 11 + [VMEM] + [ANY] * 10,
         out_specs=[VMEM] * 3,
         scratch_shapes=[
             vm((8, 128), f32),
@@ -480,8 +498,9 @@
             pltpu.SMEM((40,), jnp.int32),
             pltpu.SMEM((40,), jnp.int32),
             pltpu.SMEM((16,), jnp.int32),
+            pltpu.SMEM((17,), jnp.int32),
             pltpu.SemaphoreType.DMA((2,)),
-            pltpu.SemaphoreType.DMA((8,)),
+            pltpu.SemaphoreType.DMA((9,)),
             pltpu.SemaphoreType.DMA((2, 5, 2)),
         ],
         compiler_params=pltpu.CompilerParams(vmem_limit_bytes=60 << 20),

time: 143 us -> 146 us (1.021)
  starting transfers between devices: 52.3 us -> 59.9 us
  Pallas kernels: 36.3 us -> 34.5 us
  waiting for transfers between devices: 47.4 us -> 45.7 us
  local copies, waits for them, and re-layouts: 3.77 us -> 2.24 us
    ppermute x31 -> x32, starting transfers between devices: 45.6 us -> 53.2 us  [move(): return lax.ppermute(x, axis, perm)]
    pallas_call x1, Pallas kernels: 26.3 us -> 24.5 us  [on_device(): pl.pallas_call(attend_kernel, out_shape=[jax.ShapeDtypeStruct((256, 512),...]
    ppermute x31 -> x32, waiting for transfers between devices: 40 us -> 38.3 us  [move(): return lax.ppermute(x, axis, perm)]
    unnamed x65 -> x63, local copies, waits for them, and re-layouts: 3.7 us -> 2.14 us
  transfers between devices with their start and end apart: 32 -> 33, of which waited for: 14 -> 10; matrix products, arithmetic and copies ran while one was open for 1% -> 1% of each run, Pallas kernels for 3% -> 3%
where the time goes in v4:
time: 146 us; the launch traced here: 145 us
  starting transfers between devices  59.9 us (41%)
  waiting for transfers between devices  45.7 us (31%)
  Pallas kernels  34.5 us (24%)
  local copies, waits for them, and re-layouts  2.24 us (2%)
  other arithmetic  1.85 us (1%)
    ppermute x32, starting transfers between devices, move(): return lax.ppermute(x, axis, perm)  53.2 us
    ppermute x32, waiting for transfers between devices, move(): return lax.ppermute(x, axis, perm)  38.3 us
    pallas_call x1, Pallas kernels, on_device(): pl.pallas_call(attend_kernel, out_shape=[jax.ShapeDtypeStruct((256, 512),...  24.5 us
    pallas_call x5, Pallas kernels, call(): pl.pallas_call(kernel, out_shape=outs, in_specs=specs or [VMEM] * len(arg...  10 us
    all_to_all x1, waiting for transfers between devices, on_device(): lax.all_to_all(everyone, ('seq', 'dp'), split_axis=0, concat_axis=0, tile...  7.4 us
    all_to_all x1, starting transfers between devices, on_device(): lax.all_to_all(everyone, ('seq', 'dp'), split_axis=0, concat_axis=0, tile...  6.7 us
  transfers between devices with their start and end apart: 33, of which 10 were waited for; matrix products, arithmetic and copies ran while one was open for 1% of the time, Pallas kernels for 3%

profile of v4, /device:TPU:1, one launch (start us, length us, event | category | flops | bytes accessed | tf_op | source)
XLA Modules:
  0.0 145.3 jit_solution(14118149505909309039)
XLA Ops:
  0.6 2.1 %shard_map.103 = (bf16[256,256]{1,0:T(8,128)(2,1)}, bf16[18,32,128]{2,1,0:T(8,128)(2,1)}, bf16[18,32,128]{2,1,0:T(8,128)(2,1)}, bf16[8,32,128]{2,1,0:T(8,128)(2,1)}, bf16[8,32,128]{2,1,0:T(8,128)(2,1)}) custom-call(bf16[192,256]{1,0:T(8,128)(2,1)} %bitcast.12, bf16[64,256]{1,0:T(8,128)(2,1)} %bitcast.13, bf16[96,1536]{1,0:T(8,128)(2,1)} %w_uq.3, ...), custom_call_target="tpu_custom_call" | custom-call | flops 1048576 | bytes 1114112 | tf_op jit(solution)/shard_map/pallas_call | solution.py:417
  2.7 3.2 %collective-permute-start.1 = (bf16[18,32,128]{2,1,0:T(8,128)(2,1)}, bf16[18,32,128]{2,1,0:T(8,128)(2,1)S(1)}, u32[]{:S(2)}, u32[]{:S(2)}) collective-permute-start(bf16[18,32,128]{2,1,0:T(8,128)(2,1)} %get-tuple-element.23), channel_id=1, source_target_pairs={{0,16},{16,0},{32,48},{48,32},{64,80},{80,64},{96,112},{112,96},{1... | collective-permute-start | bytes 442376 | tf_op jit(solution)/shard_map/ppermute | solution.py:396
  8.1 3.0 %collective-permute-done.kq_x = bf16[256,256]{1,0:T(8,128)(2,1)S(1)} collective-permute-done((bf16[256,256]{1,0:T(8,128)(2,1)}, bf16[256,256]{1,0:T(8,128)(2,1)S(1)}, u32[]{:S(2)}, u32[]{:S(2)}) %collective-permute-start) | collective-permute-done | bytes 131104 | tf_op jit(solution)/shard_map/ppermute | solution.py:396
  11.8 2.1 %shard_map.105 = (bf16[9,32,128]{2,1,0:T(8,128)(2,1)}, bf16[52,32,128]{2,1,0:T(8,128)(2,1)}, bf16[256,384]{1,0:T(8,128)(2,1)}) custom-call(bf16[256,256]{1,0:T(8,128)(2,1)} %get-tuple-element.20.kq, bf16[256,256]{1,0:T(8,128)(2,1)} %copy-done.4, bf16[32,128]{1,0:T(8,128)(2,1)} %get-tuple-element.21.share, bf16[18,32,128]{2,1,0:T(8,128)(2,1)} %get-tuple-element.22.w_mine, ...), custom_call_target="tpu_custom_call" | custom-call | flops 1048576 | bytes 1392640 | tf_op jit(solution)/shard_map/pallas_call | solution.py:417
  15.4 2.4 %collective-permute-start.16 = (bf16[9,32,128]{2,1,0:T(8,128)(2,1)}, bf16[9,32,128]{2,1,0:T(8,128)(2,1)S(1)}, u32[]{:S(2)}, u32[]{:S(2)}) collective-permute-start(bf16[9,32,128]{2,1,0:T(8,128)(2,1)} %get-tuple-element.29.refs_0_), channel_id=1, source_target_pairs={{0,224},{16,240},{32,0},{48,16},{64,32},{80,48},{96,64},{112,80},{... | collective-permute-start | bytes 221192 | tf_op jit(solution)/shard_map/ppermute | solution.py:396
  17.8 11.0 %collective-permute-done.15.refs_1_ = bf16[9,32,128]{2,1,0:T(8,128)(2,1)S(1)} collective-permute-done((bf16[9,32,128]{2,1,0:T(8,128)(2,1)}, bf16[9,32,128]{2,1,0:T(8,128)(2,1)S(1)}, u32[]{:S(2)}, u32[]{:S(2)}) %collective-permute-start.15) | collective-permute-done | bytes 73760 | tf_op jit(solution)/shard_map/ppermute | solution.py:396
  28.8 2.7 %collective-permute-start.8 = (bf16[52,32,128]{2,1,0:T(8,128)(2,1)}, bf16[52,32,128]{2,1,0:T(8,128)(2,1)}, u32[]{:S(2)}, u32[]{:S(2)}) collective-permute-start(bf16[52,32,128]{2,1,0:T(8,128)(2,1)} %get-tuple-element.27.refs_2_), channel_id=1, source_target_pairs={{0,224},{16,240},{32,0},{48,16},{64,32},{80,48},{96,64},{112,80},{... | collective-permute-start | bytes 1277960 | tf_op jit(solution)/shard_map/ppermute | solution.py:396
  34.6 6.1 %collective-permute-done.18.refs_4_ = bf16[9,32,128]{2,1,0:T(8,128)(2,1)S(1)} collective-permute-done((bf16[9,32,128]{2,1,0:T(8,128)(2,1)S(1)}, bf16[9,32,128]{2,1,0:T(8,128)(2,1)S(1)}, u32[]{:S(2)}, u32[]{:S(2)}) %collective-permute-start.18) | collective-permute-done | bytes 73760 | tf_op jit(solution)/shard_map/ppermute | solution.py:396
  40.7 3.5 %collective-permute-start.20 = (bf16[9,32,128]{2,1,0:T(8,128)(2,1)S(1)}, bf16[9,32,128]{2,1,0:T(8,128)(2,1)S(1)}, u32[]{:S(2)}, u32[]{:S(2)}) collective-permute-start(bf16[9,32,128]{2,1,0:T(8,128)(2,1)S(1)} %collective-permute-done.18.refs_4_), channel_id=1, source_target_pairs={{0,224},{16,240},{32,0},{48,16},{64,32},{80,48},{96,64},{112,80},{... | collective-permute-start | bytes 221192 | tf_op jit(solution)/shard_map/ppermute | solution.py:396
  44.2 2.7 %collective-permute-start.4 = (bf16[256,384]{1,0:T(8,128)(2,1)}, bf16[256,384]{1,0:T(8,128)(2,1)S(1)}, u32[]{:S(2)}, u32[]{:S(2)}) collective-permute-start(bf16[256,384]{1,0:T(8,128)(2,1)} %get-tuple-element.26), channel_id=1, source_target_pairs={{0,6},{2,0},{4,2},{6,4},{8,14},{10,8},{12,10},{14,12},{1,7},{3,1},... | collective-permute-start | bytes 589832 | tf_op jit(solution)/shard_map/ppermute | solution.py:396
  46.9 4.4 %collective-permute-done.21.refs_7_ = bf16[9,32,128]{2,1,0:T(8,128)(2,1)S(1)} collective-permute-done((bf16[9,32,128]{2,1,0:T(8,128)(2,1)S(1)}, bf16[9,32,128]{2,1,0:T(8,128)(2,1)S(1)}, u32[]{:S(2)}, u32[]{:S(2)}) %collective-permute-start.21) | collective-permute-done | bytes 73760 | tf_op jit(solution)/shard_map/ppermute | solution.py:396
  56.0 2.3 %collective-permute-start.23 = (bf16[8,9,32,128]{3,2,1,0:T(8,128)(2,1)}, bf16[8,9,32,128]{3,2,1,0:T(8,128)(2,1)S(1)}, u32[]{:S(2)}, u32[]{:S(2)}) collective-permute-start(bf16[8,9,32,128]{3,2,1,0:T(8,128)(2,1)} %shard_map.106.refs_12_), channel_id=1, source_target_pairs={{0,6},{2,0},{4,2},{6,4},{8,14},{10,8},{12,10},{14,12},{1,7},{3,1},... | collective-permute-start | bytes 1769480 | tf_op jit(solution)/shard_map/ppermute | solution.py:396
  58.4 6.7 %collective-permute-start.26 = (bf16[8,9,32,128]{3,2,1,0:T(8,128)(2,1)}, bf16[8,9,32,128]{3,2,1,0:T(8,128)(2,1)S(1)}, u32[]{:S(2)}, u32[]{:S(2)}) collective-permute-start(bf16[8,9,32,128]{3,2,1,0:T(8,128)(2,1)} %shard_map.106.refs_12_), channel_id=1, source_target_pairs={{0,16},{16,0},{32,48},{48,32},{64,80},{80,64},{96,112},{112,96},{1... | collective-permute-start | bytes 1769480 | tf_op jit(solution)/shard_map/ppermute | solution.py:396
  66.9 6.1 %collective-permute-start.6 = (bf16[256,1536]{1,0:T(8,128)(2,1)S(1)}, bf16[256,1536]{1,0:T(8,128)(2,1)S(1)}, u32[]{:S(2)}, u32[]{:S(2)}) collective-permute-start(bf16[256,1536]{1,0:T(8,128)(2,1)S(1)} %constant_dynamic-update-slice_fusion.refs_0_), channel_id=1, source_target_pairs={{0,16},{16,0},{32,48},{48,32},{64,80},{80,64},{96,112},{112,96},{1... | collective-permute-start | bytes 2359304 | tf_op jit(solution)/shard_map/ppermute | solution.py:396
  73.2 3.5 %collective-permute-done.10.refs_6_ = bf16[52,32,128]{2,1,0:T(8,128)(2,1)S(1)} collective-permute-done((bf16[52,32,128]{2,1,0:T(8,128)(2,1)}, bf16[52,32,128]{2,1,0:T(8,128)(2,1)S(1)}, u32[]{:S(2)}, u32[]{:S(2)}) %collective-permute-start.10) | collective-permute-done | bytes 426016 | tf_op jit(solution)/shard_map/ppermute | solution.py:396
  76.7 2.0 %collective-permute-start.25 = (bf16[4,9,32,128]{3,2,1,0:T(8,128)(2,1)S(1)}, bf16[4,9,32,128]{3,2,1,0:T(8,128)(2,1)S(1)}, u32[]{:S(2)}, u32[]{:S(2)}) collective-permute-start(bf16[4,9,32,128]{3,2,1,0:T(8,128)(2,1)S(1)} %slice.19), channel_id=1, source_target_pairs={{0,6},{2,0},{4,2},{6,4},{8,14},{10,8},{12,10},{14,12},{1,7},{3,1},... | collective-permute-start | bytes 884744 | tf_op jit(solution)/shard_map/ppermute | solution.py:396
  78.7 3.0 %collective-permute-start.12 = (bf16[52,32,128]{2,1,0:T(8,128)(2,1)S(1)}, bf16[52,32,128]{2,1,0:T(8,128)(2,1)S(1)}, u32[]{:S(2)}, u32[]{:S(2)}) collective-permute-start(bf16[52,32,128]{2,1,0:T(8,128)(2,1)S(1)} %collective-permute-done.10.refs_6_), channel_id=1, source_target_pairs={{0,224},{16,240},{32,0},{48,16},{64,32},{80,48},{96,64},{112,80},{... | collective-permute-start | bytes 1277960 | tf_op jit(solution)/shard_map/ppermute | solution.py:396
  81.7 2.1 %collective-permute-start.27 = (bf16[8,9,32,128]{3,2,1,0:T(8,128)(2,1)S(1)}, bf16[8,9,32,128]{3,2,1,0:T(8,128)(2,1)S(1)}, u32[]{:S(2)}, u32[]{:S(2)}) collective-permute-start(bf16[8,9,32,128]{3,2,1,0:T(8,128)(2,1)S(1)} %collective-permute-done.22.refs_13_), channel_id=1, source_target_pairs={{0,16},{16,0},{32,48},{48,32},{64,80},{80,64},{96,112},{112,96},{1... | collective-permute-start | bytes 1769480 | tf_op jit(solution)/shard_map/ppermute | solution.py:396
  86.5 3.2 %collective-permute-done.12.refs_8_ = bf16[52,32,128]{2,1,0:T(8,128)(2,1)S(1)} collective-permute-done((bf16[52,32,128]{2,1,0:T(8,128)(2,1)S(1)}, bf16[52,32,128]{2,1,0:T(8,128)(2,1)S(1)}, u32[]{:S(2)}, u32[]{:S(2)}) %collective-permute-start.12) | collective-permute-done | bytes 426016 | tf_op jit(solution)/shard_map/ppermute | solution.py:396
  92.1 3.3 %collective-permute-start.14 = (bf16[26,32,128]{2,1,0:T(8,128)(2,1)S(1)}, bf16[26,32,128]{2,1,0:T(8,128)(2,1)S(1)}, u32[]{:S(2)}, u32[]{:S(2)}) collective-permute-start(bf16[26,32,128]{2,1,0:T(8,128)(2,1)S(1)} %slice.17), channel_id=1, source_target_pairs={{0,224},{16,240},{32,0},{48,16},{64,32},{80,48},{96,64},{112,80},{... | collective-permute-start | bytes 638984 | tf_op jit(solution)/shard_map/ppermute | solution.py:396
  95.4 4.8 %collective-permute-done.13.refs_9_ = bf16[26,32,128]{2,1,0:T(8,128)(2,1)S(1)} collective-permute-done((bf16[26,32,128]{2,1,0:T(8,128)(2,1)S(1)}, bf16[26,32,128]{2,1,0:T(8,128)(2,1)S(1)}, u32[]{:S(2)}, u32[]{:S(2)}) %collective-permute-start.13) | collective-permute-done | bytes 213024 | tf_op jit(solution)/shard_map/ppermute | solution.py:396
  101.1 24.5 %attend.1 = (bf16[256,512]{1,0:T(8,128)(2,1)}, bf16[256,512]{1,0:T(8,128)(2,1)}, f32[32,1,8]{2,1,0:T(1,128)}) custom-call(s32[1,32]{1,0:T(1,128)} %order.3, s32[32,128]{1,0:T(8,128)} %bitcast.15, bf16[256,1536]{1,0:T(8,128)(2,1)} %copy-done.16, bf16[256,1536]{1,0:T(8,128)(2,1)} %copy-done.17, bf16[52,32,128]{2,1,0:T(8,128)(2,1)} %get-tuple-element.27.refs_2_, ...), custom_call_target="tpu_custom_call" | custom-call | flops 21474836480 | bytes 12582912 | tf_op jit(solution)/shard_map/attend/pallas_call | solution.py:472
  126.9 6.7 %all-to-all-start = ((f32[32,1,8]{2,1,0:T(1,128)}), f32[32,1,8]{2,1,0:T(1,128)S(1)}, u32[]{:S(2)}, u32[]{:S(2)}) async-start(f32[32,1,8]{2,1,0:T(1,128)} %get-tuple-element.30), calls=%async_computation | async-start | bytes 32768 | tf_op jit(solution)/shard_map/all_to_all | solution.py:513
  135.4 7.4 %all-to-all-done.everyone = f32[32,1,8]{2,1,0:T(1,128)S(1)} async-done(((f32[32,1,8]{2,1,0:T(1,128)}), f32[32,1,8]{2,1,0:T(1,128)S(1)}, u32[]{:S(2)}, u32[]{:S(2)}) %all-to-all-start) | async-done | bytes 1056 | tf_op jit(solution)/shard_map/all_to_all | solution.py:513
  (118 shorter events, 25.5 us)
Async XLA Ops:
  2.7 8.4 %collective-permute-start.1 = (bf16[18,32,128]{2,1,0:T(8,128)(2,1)}, bf16[18,32,128]{2,1,0:T(8,128)(2,1)S(1)}, u32[]{:S(2)}, u32[]{:S(2)}) collective-permute-start(bf16[18,32,128]{2,1,0:T(8,128)(2,1)} %get-tuple-element.23), channel_id=1, source_target_pairs={{0,16},{16,0},{32,48},{48,32},{64,80},{80,64},{96,112},{112,96},{1... | collective-permute-start | bytes 442376 | tf_op jit(solution)/shard_map/ppermute | solution.py:396
  13.9 44.4 %collective-permute-start.7 = (bf16[52,32,128]{2,1,0:T(8,128)(2,1)}, bf16[52,32,128]{2,1,0:T(8,128)(2,1)S(1)}, u32[]{:S(2)}, u32[]{:S(2)}) collective-permute-start(bf16[52,32,128]{2,1,0:T(8,128)(2,1)} %get-tuple-element.27.refs_2_), channel_id=1, source_target_pairs={{0,32},{16,48},{32,64},{48,80},{64,96},{80,112},{96,128},{112,144}... | collective-permute-start | bytes 1277960 | tf_op jit(solution)/shard_map/ppermute | solution.py:396
  13.9 14.9 %collective-permute-start.15 = (bf16[9,32,128]{2,1,0:T(8,128)(2,1)}, bf16[9,32,128]{2,1,0:T(8,128)(2,1)S(1)}, u32[]{:S(2)}, u32[]{:S(2)}) collective-permute-start(bf16[9,32,128]{2,1,0:T(8,128)(2,1)} %get-tuple-element.29.refs_0_), channel_id=1, source_target_pairs={{0,32},{16,48},{32,64},{48,80},{64,96},{80,112},{96,128},{112,144}... | collective-permute-start | bytes 221192 | tf_op jit(solution)/shard_map/ppermute | solution.py:396
  15.4 16.1 %collective-permute-start.16 = (bf16[9,32,128]{2,1,0:T(8,128)(2,1)}, bf16[9,32,128]{2,1,0:T(8,128)(2,1)S(1)}, u32[]{:S(2)}, u32[]{:S(2)}) collective-permute-start(bf16[9,32,128]{2,1,0:T(8,128)(2,1)} %get-tuple-element.29.refs_0_), channel_id=1, source_target_pairs={{0,224},{16,240},{32,0},{48,16},{64,32},{80,48},{96,64},{112,80},{... | collective-permute-start | bytes 221192 | tf_op jit(solution)/shard_map/ppermute | solution.py:396
  28.8 36.3 %collective-permute-start.8 = (bf16[52,32,128]{2,1,0:T(8,128)(2,1)}, bf16[52,32,128]{2,1,0:T(8,128)(2,1)}, u32[]{:S(2)}, u32[]{:S(2)}) collective-permute-start(bf16[52,32,128]{2,1,0:T(8,128)(2,1)} %get-tuple-element.27.refs_2_), channel_id=1, source_target_pairs={{0,224},{16,240},{32,0},{48,16},{64,32},{80,48},{96,64},{112,80},{... | collective-permute-start | bytes 1277960 | tf_op jit(solution)/shard_map/ppermute | solution.py:396
  31.5 9.2 %collective-permute-start.18 = (bf16[9,32,128]{2,1,0:T(8,128)(2,1)S(1)}, bf16[9,32,128]{2,1,0:T(8,128)(2,1)S(1)}, u32[]{:S(2)}, u32[]{:S(2)}) collective-permute-start(bf16[9,32,128]{2,1,0:T(8,128)(2,1)S(1)} %collective-permute-done.16.refs_2_), channel_id=1, source_target_pairs={{0,224},{16,240},{32,0},{48,16},{64,32},{80,48},{96,64},{112,80},{... | collective-permute-start | bytes 221192 | tf_op jit(solution)/shard_map/ppermute | solution.py:396
  33.2 11.0 %collective-permute-start.19 = (bf16[9,32,128]{2,1,0:T(8,128)(2,1)S(1)}, bf16[9,32,128]{2,1,0:T(8,128)(2,1)S(1)}, u32[]{:S(2)}, u32[]{:S(2)}) collective-permute-start(bf16[9,32,128]{2,1,0:T(8,128)(2,1)S(1)} %collective-permute-done.17.refs_3_), channel_id=1, source_target_pairs={{0,32},{16,48},{32,64},{48,80},{64,96},{80,112},{96,128},{112,144}... | collective-permute-start | bytes 221192 | tf_op jit(solution)/shard_map/ppermute | solution.py:396
  33.2 22.1 %collective-permute-start.3 = (bf16[256,384]{1,0:T(8,128)(2,1)}, bf16[256,384]{1,0:T(8,128)(2,1)S(1)}, u32[]{:S(2)}, u32[]{:S(2)}) collective-permute-start(bf16[256,384]{1,0:T(8,128)(2,1)} %get-tuple-element.26), channel_id=1, source_target_pairs={{0,2},{2,4},{4,6},{6,0},{8,10},{10,12},{12,14},{14,8},{1,3},{3,5},... | collective-permute-start | bytes 589832 | tf_op jit(solution)/shard_map/ppermute | solution.py:396
  44.2 11.8 %collective-permute-start.4 = (bf16[256,384]{1,0:T(8,128)(2,1)}, bf16[256,384]{1,0:T(8,128)(2,1)S(1)}, u32[]{:S(2)}, u32[]{:S(2)}) collective-permute-start(bf16[256,384]{1,0:T(8,128)(2,1)} %get-tuple-element.26), channel_id=1, source_target_pairs={{0,6},{2,0},{4,2},{6,4},{8,14},{10,8},{12,10},{14,12},{1,7},{3,1},... | collective-permute-start | bytes 589832 | tf_op jit(solution)/shard_map/ppermute | solution.py:396
  55.4 17.7 %collective-permute-start.22 = (bf16[8,9,32,128]{3,2,1,0:T(8,128)(2,1)}, bf16[8,9,32,128]{3,2,1,0:T(8,128)(2,1)S(1)}, u32[]{:S(2)}, u32[]{:S(2)}) collective-permute-start(bf16[8,9,32,128]{3,2,1,0:T(8,128)(2,1)} %shard_map.106.refs_12_), channel_id=1, source_target_pairs={{0,2},{2,4},{4,6},{6,0},{8,10},{10,12},{12,14},{14,8},{1,3},{3,5},... | collective-permute-start | bytes 1769480 | tf_op jit(solution)/shard_map/ppermute | solution.py:396
  56.0 17.1 %collective-permute-start.23 = (bf16[8,9,32,128]{3,2,1,0:T(8,128)(2,1)}, bf16[8,9,32,128]{3,2,1,0:T(8,128)(2,1)S(1)}, u32[]{:S(2)}, u32[]{:S(2)}) collective-permute-start(bf16[8,9,32,128]{3,2,1,0:T(8,128)(2,1)} %shard_map.106.refs_12_), channel_id=1, source_target_pairs={{0,6},{2,0},{4,2},{6,4},{8,14},{10,8},{12,10},{14,12},{1,7},{3,1},... | collective-permute-start | bytes 1769480 | tf_op jit(solution)/shard_map/ppermute | solution.py:396
  58.3 8.6 %collective-permute-start.9 = (bf16[52,32,128]{2,1,0:T(8,128)(2,1)S(1)}, bf16[52,32,128]{2,1,0:T(8,128)(2,1)S(1)}, u32[]{:S(2)}, u32[]{:S(2)}) collective-permute-start(bf16[52,32,128]{2,1,0:T(8,128)(2,1)S(1)} %collective-permute-done.7.refs_3_), channel_id=1, source_target_pairs={{0,32},{16,48},{32,64},{48,80},{64,96},{80,112},{96,128},{112,144}... | collective-permute-start | bytes 1277960 | tf_op jit(solution)/shard_map/ppermute | solution.py:396
  58.4 20.4 %collective-permute-start.26 = (bf16[8,9,32,128]{3,2,1,0:T(8,128)(2,1)}, bf16[8,9,32,128]{3,2,1,0:T(8,128)(2,1)S(1)}, u32[]{:S(2)}, u32[]{:S(2)}) collective-permute-start(bf16[8,9,32,128]{3,2,1,0:T(8,128)(2,1)} %shard_map.106.refs_12_), channel_id=1, source_target_pairs={{0,16},{16,0},{32,48},{48,32},{64,80},{80,64},{96,112},{112,96},{1... | collective-permute-start | bytes 1769480 | tf_op jit(solution)/shard_map/ppermute | solution.py:396
  65.1 11.6 %collective-permute-start.10 = (bf16[52,32,128]{2,1,0:T(8,128)(2,1)}, bf16[52,32,128]{2,1,0:T(8,128)(2,1)S(1)}, u32[]{:S(2)}, u32[]{:S(2)}) collective-permute-start(bf16[52,32,128]{2,1,0:T(8,128)(2,1)} %collective-permute-done.8.refs_4_), channel_id=1, source_target_pairs={{0,224},{16,240},{32,0},{48,16},{64,32},{80,48},{96,64},{112,80},{... | collective-permute-start | bytes 1277960 | tf_op jit(solution)/shard_map/ppermute | solution.py:396
  66.9 24.9 %collective-permute-start.6 = (bf16[256,1536]{1,0:T(8,128)(2,1)S(1)}, bf16[256,1536]{1,0:T(8,128)(2,1)S(1)}, u32[]{:S(2)}, u32[]{:S(2)}) collective-permute-start(bf16[256,1536]{1,0:T(8,128)(2,1)S(1)} %constant_dynamic-update-slice_fusion.refs_0_), channel_id=1, source_target_pairs={{0,16},{16,0},{32,48},{48,32},{64,80},{80,64},{96,112},{112,96},{1... | collective-permute-start | bytes 2359304 | tf_op jit(solution)/shard_map/ppermute | solution.py:396
  73.0 13.1 %collective-permute-start.11 = (bf16[52,32,128]{2,1,0:T(8,128)(2,1)S(1)}, bf16[52,32,128]{2,1,0:T(8,128)(2,1)S(1)}, u32[]{:S(2)}, u32[]{:S(2)}) collective-permute-start(bf16[52,32,128]{2,1,0:T(8,128)(2,1)S(1)} %collective-permute-done.9.refs_5_), channel_id=1, source_target_pairs={{0,32},{16,48},{32,64},{48,80},{64,96},{80,112},{96,128},{112,144}... | collective-permute-start | bytes 1277960 | tf_op jit(solution)/shard_map/ppermute | solution.py:396
  73.1 8.6 %collective-permute-start.24 = (bf16[4,9,32,128]{3,2,1,0:T(8,128)(2,1)S(1)}, bf16[4,9,32,128]{3,2,1,0:T(8,128)(2,1)S(1)}, u32[]{:S(2)}, u32[]{:S(2)}) collective-permute-start(bf16[4,9,32,128]{3,2,1,0:T(8,128)(2,1)S(1)} %slice.18), channel_id=1, source_target_pairs={{0,2},{2,4},{4,6},{6,0},{8,10},{10,12},{12,14},{14,8},{1,3},{3,5},... | collective-permute-start | bytes 884744 | tf_op jit(solution)/shard_map/ppermute | solution.py:396
  78.7 11.0 %collective-permute-start.12 = (bf16[52,32,128]{2,1,0:T(8,128)(2,1)S(1)}, bf16[52,32,128]{2,1,0:T(8,128)(2,1)S(1)}, u32[]{:S(2)}, u32[]{:S(2)}) collective-permute-start(bf16[52,32,128]{2,1,0:T(8,128)(2,1)S(1)} %collective-permute-done.10.refs_6_), channel_id=1, source_target_pairs={{0,224},{16,240},{32,0},{48,16},{64,32},{80,48},{96,64},{112,80},{... | collective-permute-start | bytes 1277960 | tf_op jit(solution)/shard_map/ppermute | solution.py:396
  81.7 13.7 %collective-permute-start.27 = (bf16[8,9,32,128]{3,2,1,0:T(8,128)(2,1)S(1)}, bf16[8,9,32,128]{3,2,1,0:T(8,128)(2,1)S(1)}, u32[]{:S(2)}, u32[]{:S(2)}) collective-permute-start(bf16[8,9,32,128]{3,2,1,0:T(8,128)(2,1)S(1)} %collective-permute-done.22.refs_13_), channel_id=1, source_target_pairs={{0,16},{16,0},{32,48},{48,32},{64,80},{80,64},{96,112},{112,96},{1... | collective-permute-start | bytes 1769480 | tf_op jit(solution)/shard_map/ppermute | solution.py:396
  84.4 11.0 %collective-permute-start.28 = (bf16[8,9,32,128]{3,2,1,0:T(8,128)(2,1)S(1)}, bf16[8,9,32,128]{3,2,1,0:T(8,128)(2,1)S(1)}, u32[]{:S(2)}, u32[]{:S(2)}) collective-permute-start(bf16[8,9,32,128]{3,2,1,0:T(8,128)(2,1)S(1)} %collective-permute-done.23.refs_14_), channel_id=1, source_target_pairs={{0,16},{16,0},{32,48},{48,32},{64,80},{80,64},{96,112},{112,96},{1... | collective-permute-start | bytes 1769480 | tf_op jit(solution)/shard_map/ppermute | solution.py:396
  91.8 8.5 %collective-permute-start.13 = (bf16[26,32,128]{2,1,0:T(8,128)(2,1)S(1)}, bf16[26,32,128]{2,1,0:T(8,128)(2,1)S(1)}, u32[]{:S(2)}, u32[]{:S(2)}) collective-permute-start(bf16[26,32,128]{2,1,0:T(8,128)(2,1)S(1)} %slice.16), channel_id=1, source_target_pairs={{0,32},{16,48},{32,64},{48,80},{64,96},{80,112},{96,128},{112,144}... | collective-permute-start | bytes 638984 | tf_op jit(solution)/shard_map/ppermute | solution.py:396
  92.1 8.2 %collective-permute-start.14 = (bf16[26,32,128]{2,1,0:T(8,128)(2,1)S(1)}, bf16[26,32,128]{2,1,0:T(8,128)(2,1)S(1)}, u32[]{:S(2)}, u32[]{:S(2)}) collective-permute-start(bf16[26,32,128]{2,1,0:T(8,128)(2,1)S(1)} %slice.17), channel_id=1, source_target_pairs={{0,224},{16,240},{32,0},{48,16},{64,32},{80,48},{96,64},{112,80},{... | collective-permute-start | bytes 638984 | tf_op jit(solution)/shard_map/ppermute | solution.py:396
  125.6 8.0 %collective-permute-start.31 = (bf16[256,512]{1,0:T(8,128)(2,1)}, bf16[256,512]{1,0:T(8,128)(2,1)S(1)}, u32[]{:S(2)}, u32[]{:S(2)}) collective-permute-start(bf16[256,512]{1,0:T(8,128)(2,1)} %get-tuple-element.32), channel_id=1, source_target_pairs={{0,16},{16,0},{32,48},{48,32},{64,80},{80,64},{96,112},{112,96},{1... | collective-permute-start | bytes 786440 | tf_op jit(solution)/shard_map/ppermute | solution.py:396
  126.9 16.0 %all-to-all-start = ((f32[32,1,8]{2,1,0:T(1,128)}), f32[32,1,8]{2,1,0:T(1,128)S(1)}, u32[]{:S(2)}, u32[]{:S(2)}) async-start(f32[32,1,8]{2,1,0:T(1,128)} %get-tuple-element.30), calls=%async_computation | async-start | bytes 32768 | tf_op jit(solution)/shard_map/all_to_all | solution.py:513
  (39 other events, 398.7 us)

commit v5 on v4

--- a/solution.py
+++ b/solution.py
@@ -56,10 +56,8 @@
 ]
 
 
-def split_kernel(q_t, k_t, w_uq, w_uk, w_uv, kq, w_mine, w_send, kv_mine, kv_send):
+def split_kernel(w_uq, w_uk, w_uv, w_mine, w_send, kv_mine, kv_send):
     c = where_am_i()["c"]
-    kq[:64] = k_t[...]
-    kq[64:] = q_t[...]
 
     def halves(own):
         for to, half in ((w_mine, own), (w_send, 1 - own)):
@@ -105,9 +103,9 @@
     share[...] = fold[pl.ds(pl.multiple_of(m["y"] * 32, 32), 32), :]
 
 
-def pack_kernel(kq, kq_x, share, w_mine, w_other, kv_mine, kv_other, k_one, w_one, q_x):
+def pack_kernel(k_t, k_tx, q_t, q_tx, share, w_mine, w_other, kv_mine, kv_other, k_one, w_one, q_x):
     c = where_am_i()["c"]
-    lat = jnp.concatenate([kq[:64], kq_x[:64]], axis=0).T
+    lat = jnp.concatenate([k_t[...], k_tx[...]], axis=0).T
     for b in range(8):
         k_one[b] = lat[b * 32 : (b + 1) * 32]
     k_one[8] = share[...]
@@ -116,7 +114,7 @@
             w_one[pl.ds(n * 6 + core * 3, 3)] = w[n * 3 : n * 3 + 3]
         for n in range(8):
             w_one[36 + n * 2 + core] = kv[n]
-    q_x[...] = jnp.concatenate([kq[64:], kq_x[64:]], axis=0).T
+    q_x[...] = jnp.concatenate([q_t[...], q_tx[...]], axis=0).T
 
 
 def join_kernel(*refs):
@@ -427,12 +425,11 @@
 def on_device(query_latent, key_latent, rope_key, w_uq, w_uk, w_uv, block_order, segment_ids):
     bf16, f32 = jnp.bfloat16, jnp.float32
     c = where_am_i()["c"]
-    kq, w_mine, w_send, kv_mine, kv_send = call(
-        split_kernel,
-        [((256, 256), bf16)] + [((18, 32, 128), bf16)] * 2 + [((8, 32, 128), bf16)] * 2,
-        (query_latent[0].T, key_latent[0].T, w_uq, w_uk, w_uv),
-    )
-    kq_x = move(kq, "tp", XSWAP)
+    k_t, q_t = key_latent[0].T, query_latent[0].T
+    k_tx, q_tx = move(k_t, "tp", XSWAP), move(q_t, "tp", XSWAP)
+    w_mine, w_send, kv_mine, kv_send = call(
+        split_kernel, [((18, 32, 128), bf16)] * 2 + [((8, 32, 128), bf16)] * 2, (w_uq, w_uk, w_uv)
+    )
     w_other = swap(w_send)
     kv_other = swap(kv_send)
     cs, share = call(
@@ -445,7 +442,7 @@
     k_one, w_one, q_x = call(
         pack_kernel,
         [((9, 32, 128), bf16), ((52, 32, 128), bf16), ((256, 384), bf16)],
-        (kq, kq_x, share, w_mine, w_other, kv_mine, kv_other),
+        (k_t, k_tx, q_t, q_tx, share, w_mine, w_other, kv_mine, kv_other),
     )
 
     k_ring = ring(k_one)

time: 146 us -> 145 us (level)
    ppermute x32 -> x33, waiting for transfers between devices: 38.3 us -> 36.9 us  [move(): return lax.ppermute(x, axis, perm)]
    ppermute x32 -> x33, starting transfers between devices: 53.2 us -> 54.4 us  [move(): return lax.ppermute(x, axis, perm)]
  transfers between devices with their start and end apart: 33 -> 34, of which waited for: 10 -> 10; matrix products, arithmetic and copies ran while one was open for 1% -> 1% of each run, Pallas kernels for 3% -> 3%
where the time goes in v5:
time: 145 us
  starting transfers between devices  61.1 us (42%)
  waiting for transfers between devices  44.3 us (31%)
  Pallas kernels  34.5 us (24%)
  local copies, waits for them, and re-layouts  2.28 us (2%)
  other arithmetic  1.85 us (1%)
    ppermute x33, starting transfers between devices, move(): return lax.ppermute(x, axis, perm)  54.4 us
    ppermute x33, waiting for transfers between devices, move(): return lax.ppermute(x, axis, perm)  36.9 us
    pallas_call x1, Pallas kernels, on_device(): pl.pallas_call(attend_kernel, out_shape=[jax.ShapeDtypeStruct((256, 512),...  24.5 us
    pallas_call x5, Pallas kernels, call(): pl.pallas_call(kernel, out_shape=outs, in_specs=specs or [VMEM] * len(arg...  9.96 us
    all_to_all x1, waiting for transfers between devices, on_device(): lax.all_to_all(everyone, ('seq', 'dp'), split_axis=0, concat_axis=0, tile...  7.4 us
    all_to_all x1, starting transfers between devices, on_device(): lax.all_to_all(everyone, ('seq', 'dp'), split_axis=0, concat_axis=0, tile...  6.66 us
  transfers between devices with their start and end apart: 34, of which 10 were waited for; matrix products, arithmetic and copies ran while one was open for 1% of the time, Pallas kernels for 3%

profile of v5, /device:TPU:1, one launch (start us, length us, event | category | flops | bytes accessed | tf_op | source)
XLA Modules:
  0.0 145.1 jit_solution(5860959132034673966)
XLA Ops:
  2.6 3.2 %collective-permute-start.2 = (bf16[18,32,128]{2,1,0:T(8,128)(2,1)}, bf16[18,32,128]{2,1,0:T(8,128)(2,1)S(1)}, u32[]{:S(2)}, u32[]{:S(2)}) collective-permute-start(bf16[18,32,128]{2,1,0:T(8,128)(2,1)} %get-tuple-element.21), channel_id=1, source_target_pairs={{0,16},{16,0},{32,48},{48,32},{64,80},{80,64},{96,112},{112,96},{1... | collective-permute-start | bytes 442376 | tf_op jit(solution)/shard_map/ppermute | solution.py:394
  7.7 2.0 %shard_map.103 = (f32[512,256]{1,0:T(8,128)}, bf16[32,128]{1,0:T(8,128)(2,1)}) custom-call(s32[1,32]{1,0:T(1,128)} %order.3, bf16[64,256]{1,0:T(8,128)(2,1)} %bitcast.16), custom_call_target="tpu_custom_call" | custom-call | flops 1048576 | bytes 1064960 | tf_op jit(solution)/shard_map/pallas_call | solution.py:415
  11.6 2.1 %shard_map.105 = (bf16[9,32,128]{2,1,0:T(8,128)(2,1)}, bf16[52,32,128]{2,1,0:T(8,128)(2,1)}, bf16[256,384]{1,0:T(8,128)(2,1)}) custom-call(bf16[64,256]{1,0:T(8,128)(2,1)} %bitcast.14, bf16[64,256]{1,0:T(8,128)(2,1)} %copy-done.19, bf16[192,256]{1,0:T(8,128)(2,1)} %bitcast.12, bf16[192,256]{1,0:T(8,128)(2,1)} %copy-done.7, ...), custom_call_target="tpu_custom_call" | custom-call | flops 1048576 | bytes 1392640 | tf_op jit(solution)/shard_map/pallas_call | solution.py:415
  15.2 2.4 %collective-permute-start.17 = (bf16[9,32,128]{2,1,0:T(8,128)(2,1)}, bf16[9,32,128]{2,1,0:T(8,128)(2,1)S(1)}, u32[]{:S(2)}, u32[]{:S(2)}) collective-permute-start(bf16[9,32,128]{2,1,0:T(8,128)(2,1)} %get-tuple-element.27.refs_0_), channel_id=1, source_target_pairs={{0,224},{16,240},{32,0},{48,16},{64,32},{80,48},{96,64},{112,80},{... | collective-permute-start | bytes 221192 | tf_op jit(solution)/shard_map/ppermute | solution.py:394
  17.6 11.0 %collective-permute-done.16.refs_1_ = bf16[9,32,128]{2,1,0:T(8,128)(2,1)S(1)} collective-permute-done((bf16[9,32,128]{2,1,0:T(8,128)(2,1)}, bf16[9,32,128]{2,1,0:T(8,128)(2,1)S(1)}, u32[]{:S(2)}, u32[]{:S(2)}) %collective-permute-start.16) | collective-permute-done | bytes 73760 | tf_op jit(solution)/shard_map/ppermute | solution.py:394
  28.6 2.7 %collective-permute-start.9 = (bf16[52,32,128]{2,1,0:T(8,128)(2,1)}, bf16[52,32,128]{2,1,0:T(8,128)(2,1)}, u32[]{:S(2)}, u32[]{:S(2)}) collective-permute-start(bf16[52,32,128]{2,1,0:T(8,128)(2,1)} %get-tuple-element.25.refs_2_), channel_id=1, source_target_pairs={{0,224},{16,240},{32,0},{48,16},{64,32},{80,48},{96,64},{112,80},{... | collective-permute-start | bytes 1277960 | tf_op jit(solution)/shard_map/ppermute | solution.py:394
  34.4 6.1 %collective-permute-done.19.refs_4_ = bf16[9,32,128]{2,1,0:T(8,128)(2,1)S(1)} collective-permute-done((bf16[9,32,128]{2,1,0:T(8,128)(2,1)S(1)}, bf16[9,32,128]{2,1,0:T(8,128)(2,1)S(1)}, u32[]{:S(2)}, u32[]{:S(2)}) %collective-permute-start.19) | collective-permute-done | bytes 73760 | tf_op jit(solution)/shard_map/ppermute | solution.py:394
  40.5 3.5 %collective-permute-start.21 = (bf16[9,32,128]{2,1,0:T(8,128)(2,1)S(1)}, bf16[9,32,128]{2,1,0:T(8,128)(2,1)S(1)}, u32[]{:S(2)}, u32[]{:S(2)}) collective-permute-start(bf16[9,32,128]{2,1,0:T(8,128)(2,1)S(1)} %collective-permute-done.19.refs_4_), channel_id=1, source_target_pairs={{0,224},{16,240},{32,0},{48,16},{64,32},{80,48},{96,64},{112,80},{... | collective-permute-start | bytes 221192 | tf_op jit(solution)/shard_map/ppermute | solution.py:394
  44.0 2.7 %collective-permute-start.5 = (bf16[256,384]{1,0:T(8,128)(2,1)}, bf16[256,384]{1,0:T(8,128)(2,1)S(1)}, u32[]{:S(2)}, u32[]{:S(2)}) collective-permute-start(bf16[256,384]{1,0:T(8,128)(2,1)} %get-tuple-element.24), channel_id=1, source_target_pairs={{0,6},{2,0},{4,2},{6,4},{8,14},{10,8},{12,10},{14,12},{1,7},{3,1},... | collective-permute-start | bytes 589832 | tf_op jit(solution)/shard_map/ppermute | solution.py:394
  46.7 4.4 %collective-permute-done.22.refs_7_ = bf16[9,32,128]{2,1,0:T(8,128)(2,1)S(1)} collective-permute-done((bf16[9,32,128]{2,1,0:T(8,128)(2,1)S(1)}, bf16[9,32,128]{2,1,0:T(8,128)(2,1)S(1)}, u32[]{:S(2)}, u32[]{:S(2)}) %collective-permute-start.22) | collective-permute-done | bytes 73760 | tf_op jit(solution)/shard_map/ppermute | solution.py:394
  53.1 2.0 %shard_map.106.refs_12_ = bf16[8,9,32,128]{3,2,1,0:T(8,128)(2,1)} custom-call(bf16[9,32,128]{2,1,0:T(8,128)(2,1)} %get-tuple-element.27.refs_0_, bf16[9,32,128]{2,1,0:T(8,128)(2,1)} %copy-done.8, bf16[9,32,128]{2,1,0:T(8,128)(2,1)} %copy-done.9, bf16[9,32,128]{2,1,0:T(8,128)(2,1)} %copy-done.10, bf16[9,32,128]{2,1,0:T(8,128)(2,1)} %copy-done.11, ...), custom_call_target="tpu_custom_call" | custom-call | flops 1048576 | bytes 1179648 | tf_op jit(solution)/shard_map/pallas_call | solution.py:415
  55.6 2.3 %collective-permute-start.24 = (bf16[8,9,32,128]{3,2,1,0:T(8,128)(2,1)}, bf16[8,9,32,128]{3,2,1,0:T(8,128)(2,1)S(1)}, u32[]{:S(2)}, u32[]{:S(2)}) collective-permute-start(bf16[8,9,32,128]{3,2,1,0:T(8,128)(2,1)} %shard_map.106.refs_12_), channel_id=1, source_target_pairs={{0,6},{2,0},{4,2},{6,4},{8,14},{10,8},{12,10},{14,12},{1,7},{3,1},... | collective-permute-start | bytes 1769480 | tf_op jit(solution)/shard_map/ppermute | solution.py:394
  58.0 6.9 %collective-permute-start.27 = (bf16[8,9,32,128]{3,2,1,0:T(8,128)(2,1)}, bf16[8,9,32,128]{3,2,1,0:T(8,128)(2,1)S(1)}, u32[]{:S(2)}, u32[]{:S(2)}) collective-permute-start(bf16[8,9,32,128]{3,2,1,0:T(8,128)(2,1)} %shard_map.106.refs_12_), channel_id=1, source_target_pairs={{0,16},{16,0},{32,48},{48,32},{64,80},{80,64},{96,112},{112,96},{1... | collective-permute-start | bytes 1769480 | tf_op jit(solution)/shard_map/ppermute | solution.py:394
  66.5 6.1 %collective-permute-start.7 = (bf16[256,1536]{1,0:T(8,128)(2,1)S(1)}, bf16[256,1536]{1,0:T(8,128)(2,1)S(1)}, u32[]{:S(2)}, u32[]{:S(2)}) collective-permute-start(bf16[256,1536]{1,0:T(8,128)(2,1)S(1)} %constant_dynamic-update-slice_fusion.refs_0_), channel_id=1, source_target_pairs={{0,16},{16,0},{32,48},{48,32},{64,80},{80,64},{96,112},{112,96},{1... | collective-permute-start | bytes 2359304 | tf_op jit(solution)/shard_map/ppermute | solution.py:394
  72.8 3.6 %collective-permute-done.11.refs_6_ = bf16[52,32,128]{2,1,0:T(8,128)(2,1)S(1)} collective-permute-done((bf16[52,32,128]{2,1,0:T(8,128)(2,1)}, bf16[52,32,128]{2,1,0:T(8,128)(2,1)S(1)}, u32[]{:S(2)}, u32[]{:S(2)}) %collective-permute-start.11) | collective-permute-done | bytes 426016 | tf_op jit(solution)/shard_map/ppermute | solution.py:394
  76.5 2.0 %collective-permute-start.26 = (bf16[4,9,32,128]{3,2,1,0:T(8,128)(2,1)S(1)}, bf16[4,9,32,128]{3,2,1,0:T(8,128)(2,1)S(1)}, u32[]{:S(2)}, u32[]{:S(2)}) collective-permute-start(bf16[4,9,32,128]{3,2,1,0:T(8,128)(2,1)S(1)} %slice.19), channel_id=1, source_target_pairs={{0,6},{2,0},{4,2},{6,4},{8,14},{10,8},{12,10},{14,12},{1,7},{3,1},... | collective-permute-start | bytes 884744 | tf_op jit(solution)/shard_map/ppermute | solution.py:394
  78.5 3.0 %collective-permute-start.13 = (bf16[52,32,128]{2,1,0:T(8,128)(2,1)S(1)}, bf16[52,32,128]{2,1,0:T(8,128)(2,1)S(1)}, u32[]{:S(2)}, u32[]{:S(2)}) collective-permute-start(bf16[52,32,128]{2,1,0:T(8,128)(2,1)S(1)} %collective-permute-done.11.refs_6_), channel_id=1, source_target_pairs={{0,224},{16,240},{32,0},{48,16},{64,32},{80,48},{96,64},{112,80},{... | collective-permute-start | bytes 1277960 | tf_op jit(solution)/shard_map/ppermute | solution.py:394
  86.1 3.4 %collective-permute-done.13.refs_8_ = bf16[52,32,128]{2,1,0:T(8,128)(2,1)S(1)} collective-permute-done((bf16[52,32,128]{2,1,0:T(8,128)(2,1)S(1)}, bf16[52,32,128]{2,1,0:T(8,128)(2,1)S(1)}, u32[]{:S(2)}, u32[]{:S(2)}) %collective-permute-start.13) | collective-permute-done | bytes 426016 | tf_op jit(solution)/shard_map/ppermute | solution.py:394
  89.5 2.0 %collective-permute-start.31 = (bf16[4,9,32,128]{3,2,1,0:T(8,128)(2,1)S(1)}, bf16[4,9,32,128]{3,2,1,0:T(8,128)(2,1)S(1)}, u32[]{:S(2)}, u32[]{:S(2)}) collective-permute-start(bf16[4,9,32,128]{3,2,1,0:T(8,128)(2,1)S(1)} %collective-permute-done.26.refs_16_), channel_id=1, source_target_pairs={{0,16},{16,0},{32,48},{48,32},{64,80},{80,64},{96,112},{112,96},{1... | collective-permute-start | bytes 884744 | tf_op jit(solution)/shard_map/ppermute | solution.py:394
  91.9 3.3 %collective-permute-start.15 = (bf16[26,32,128]{2,1,0:T(8,128)(2,1)S(1)}, bf16[26,32,128]{2,1,0:T(8,128)(2,1)S(1)}, u32[]{:S(2)}, u32[]{:S(2)}) collective-permute-start(bf16[26,32,128]{2,1,0:T(8,128)(2,1)S(1)} %slice.17), channel_id=1, source_target_pairs={{0,224},{16,240},{32,0},{48,16},{64,32},{80,48},{96,64},{112,80},{... | collective-permute-start | bytes 638984 | tf_op jit(solution)/shard_map/ppermute | solution.py:394
  95.2 4.8 %collective-permute-done.14.refs_9_ = bf16[26,32,128]{2,1,0:T(8,128)(2,1)S(1)} collective-permute-done((bf16[26,32,128]{2,1,0:T(8,128)(2,1)S(1)}, bf16[26,32,128]{2,1,0:T(8,128)(2,1)S(1)}, u32[]{:S(2)}, u32[]{:S(2)}) %collective-permute-start.14) | collective-permute-done | bytes 213024 | tf_op jit(solution)/shard_map/ppermute | solution.py:394
  100.9 24.5 %attend.1 = (bf16[256,512]{1,0:T(8,128)(2,1)}, bf16[256,512]{1,0:T(8,128)(2,1)}, f32[32,1,8]{2,1,0:T(1,128)}) custom-call(s32[1,32]{1,0:T(1,128)} %order.3, s32[32,128]{1,0:T(8,128)} %bitcast.17, bf16[256,1536]{1,0:T(8,128)(2,1)} %copy-done.17, bf16[256,1536]{1,0:T(8,128)(2,1)} %copy-done.20, bf16[52,32,128]{2,1,0:T(8,128)(2,1)} %get-tuple-element.25.refs_2_, ...), custom_call_target="tpu_custom_call" | custom-call | flops 21474836480 | bytes 12582912 | tf_op jit(solution)/shard_map/attend/pallas_call | solution.py:469
  126.7 6.7 %all-to-all-start = ((f32[32,1,8]{2,1,0:T(1,128)}), f32[32,1,8]{2,1,0:T(1,128)S(1)}, u32[]{:S(2)}, u32[]{:S(2)}) async-start(f32[32,1,8]{2,1,0:T(1,128)} %get-tuple-element.28), calls=%async_computation | async-start | bytes 32768 | tf_op jit(solution)/shard_map/all_to_all | solution.py:510
  135.2 7.4 %all-to-all-done.everyone = f32[32,1,8]{2,1,0:T(1,128)S(1)} async-done(((f32[32,1,8]{2,1,0:T(1,128)}), f32[32,1,8]{2,1,0:T(1,128)S(1)}, u32[]{:S(2)}, u32[]{:S(2)}) %all-to-all-start) | async-done | bytes 1056 | tf_op jit(solution)/shard_map/all_to_all | solution.py:510
  (126 shorter events, 26.0 us)
Async XLA Ops:
  2.6 8.2 %collective-permute-start.2 = (bf16[18,32,128]{2,1,0:T(8,128)(2,1)}, bf16[18,32,128]{2,1,0:T(8,128)(2,1)S(1)}, u32[]{:S(2)}, u32[]{:S(2)}) collective-permute-start(bf16[18,32,128]{2,1,0:T(8,128)(2,1)} %get-tuple-element.21), channel_id=1, source_target_pairs={{0,16},{16,0},{32,48},{48,32},{64,80},{80,64},{96,112},{112,96},{1... | collective-permute-start | bytes 442376 | tf_op jit(solution)/shard_map/ppermute | solution.py:394
  13.7 44.3 %collective-permute-start.8 = (bf16[52,32,128]{2,1,0:T(8,128)(2,1)}, bf16[52,32,128]{2,1,0:T(8,128)(2,1)S(1)}, u32[]{:S(2)}, u32[]{:S(2)}) collective-permute-start(bf16[52,32,128]{2,1,0:T(8,128)(2,1)} %get-tuple-element.25.refs_2_), channel_id=1, source_target_pairs={{0,32},{16,48},{32,64},{48,80},{64,96},{80,112},{96,128},{112,144}... | collective-permute-start | bytes 1277960 | tf_op jit(solution)/shard_map/ppermute | solution.py:394
  13.7 14.9 %collective-permute-start.16 = (bf16[9,32,128]{2,1,0:T(8,128)(2,1)}, bf16[9,32,128]{2,1,0:T(8,128)(2,1)S(1)}, u32[]{:S(2)}, u32[]{:S(2)}) collective-permute-start(bf16[9,32,128]{2,1,0:T(8,128)(2,1)} %get-tuple-element.27.refs_0_), channel_id=1, source_target_pairs={{0,32},{16,48},{32,64},{48,80},{64,96},{80,112},{96,128},{112,144}... | collective-permute-start | bytes 221192 | tf_op jit(solution)/shard_map/ppermute | solution.py:394
  15.2 16.0 %collective-permute-start.17 = (bf16[9,32,128]{2,1,0:T(8,128)(2,1)}, bf16[9,32,128]{2,1,0:T(8,128)(2,1)S(1)}, u32[]{:S(2)}, u32[]{:S(2)}) collective-permute-start(bf16[9,32,128]{2,1,0:T(8,128)(2,1)} %get-tuple-element.27.refs_0_), channel_id=1, source_target_pairs={{0,224},{16,240},{32,0},{48,16},{64,32},{80,48},{96,64},{112,80},{... | collective-permute-start | bytes 221192 | tf_op jit(solution)/shard_map/ppermute | solution.py:394
  28.6 36.3 %collective-permute-start.9 = (bf16[52,32,128]{2,1,0:T(8,128)(2,1)}, bf16[52,32,128]{2,1,0:T(8,128)(2,1)}, u32[]{:S(2)}, u32[]{:S(2)}) collective-permute-start(bf16[52,32,128]{2,1,0:T(8,128)(2,1)} %get-tuple-element.25.refs_2_), channel_id=1, source_target_pairs={{0,224},{16,240},{32,0},{48,16},{64,32},{80,48},{96,64},{112,80},{... | collective-permute-start | bytes 1277960 | tf_op jit(solution)/shard_map/ppermute | solution.py:394
  31.3 9.2 %collective-permute-start.19 = (bf16[9,32,128]{2,1,0:T(8,128)(2,1)S(1)}, bf16[9,32,128]{2,1,0:T(8,128)(2,1)S(1)}, u32[]{:S(2)}, u32[]{:S(2)}) collective-permute-start(bf16[9,32,128]{2,1,0:T(8,128)(2,1)S(1)} %collective-permute-done.17.refs_2_), channel_id=1, source_target_pairs={{0,224},{16,240},{32,0},{48,16},{64,32},{80,48},{96,64},{112,80},{... | collective-permute-start | bytes 221192 | tf_op jit(solution)/shard_map/ppermute | solution.py:394
  33.0 11.0 %collective-permute-start.20 = (bf16[9,32,128]{2,1,0:T(8,128)(2,1)S(1)}, bf16[9,32,128]{2,1,0:T(8,128)(2,1)S(1)}, u32[]{:S(2)}, u32[]{:S(2)}) collective-permute-start(bf16[9,32,128]{2,1,0:T(8,128)(2,1)S(1)} %collective-permute-done.18.refs_3_), channel_id=1, source_target_pairs={{0,32},{16,48},{32,64},{48,80},{64,96},{80,112},{96,128},{112,144}... | collective-permute-start | bytes 221192 | tf_op jit(solution)/shard_map/ppermute | solution.py:394
  33.0 22.1 %collective-permute-start.4 = (bf16[256,384]{1,0:T(8,128)(2,1)}, bf16[256,384]{1,0:T(8,128)(2,1)S(1)}, u32[]{:S(2)}, u32[]{:S(2)}) collective-permute-start(bf16[256,384]{1,0:T(8,128)(2,1)} %get-tuple-element.24), channel_id=1, source_target_pairs={{0,2},{2,4},{4,6},{6,0},{8,10},{10,12},{12,14},{14,8},{1,3},{3,5},... | collective-permute-start | bytes 589832 | tf_op jit(solution)/shard_map/ppermute | solution.py:394
  44.0 11.6 %collective-permute-start.5 = (bf16[256,384]{1,0:T(8,128)(2,1)}, bf16[256,384]{1,0:T(8,128)(2,1)S(1)}, u32[]{:S(2)}, u32[]{:S(2)}) collective-permute-start(bf16[256,384]{1,0:T(8,128)(2,1)} %get-tuple-element.24), channel_id=1, source_target_pairs={{0,6},{2,0},{4,2},{6,4},{8,14},{10,8},{12,10},{14,12},{1,7},{3,1},... | collective-permute-start | bytes 589832 | tf_op jit(solution)/shard_map/ppermute | solution.py:394
  55.1 17.5 %collective-permute-start.23 = (bf16[8,9,32,128]{3,2,1,0:T(8,128)(2,1)}, bf16[8,9,32,128]{3,2,1,0:T(8,128)(2,1)S(1)}, u32[]{:S(2)}, u32[]{:S(2)}) collective-permute-start(bf16[8,9,32,128]{3,2,1,0:T(8,128)(2,1)} %shard_map.106.refs_12_), channel_id=1, source_target_pairs={{0,2},{2,4},{4,6},{6,0},{8,10},{10,12},{12,14},{14,8},{1,3},{3,5},... | collective-permute-start | bytes 1769480 | tf_op jit(solution)/shard_map/ppermute | solution.py:394
  55.6 17.1 %collective-permute-start.24 = (bf16[8,9,32,128]{3,2,1,0:T(8,128)(2,1)}, bf16[8,9,32,128]{3,2,1,0:T(8,128)(2,1)S(1)}, u32[]{:S(2)}, u32[]{:S(2)}) collective-permute-start(bf16[8,9,32,128]{3,2,1,0:T(8,128)(2,1)} %shard_map.106.refs_12_), channel_id=1, source_target_pairs={{0,6},{2,0},{4,2},{6,4},{8,14},{10,8},{12,10},{14,12},{1,7},{3,1},... | collective-permute-start | bytes 1769480 | tf_op jit(solution)/shard_map/ppermute | solution.py:394
  57.9 8.6 %collective-permute-start.10 = (bf16[52,32,128]{2,1,0:T(8,128)(2,1)S(1)}, bf16[52,32,128]{2,1,0:T(8,128)(2,1)S(1)}, u32[]{:S(2)}, u32[]{:S(2)}) collective-permute-start(bf16[52,32,128]{2,1,0:T(8,128)(2,1)S(1)} %collective-permute-done.8.refs_3_), channel_id=1, source_target_pairs={{0,32},{16,48},{32,64},{48,80},{64,96},{80,112},{96,128},{112,144}... | collective-permute-start | bytes 1277960 | tf_op jit(solution)/shard_map/ppermute | solution.py:394
  58.0 20.5 %collective-permute-start.27 = (bf16[8,9,32,128]{3,2,1,0:T(8,128)(2,1)}, bf16[8,9,32,128]{3,2,1,0:T(8,128)(2,1)S(1)}, u32[]{:S(2)}, u32[]{:S(2)}) collective-permute-start(bf16[8,9,32,128]{3,2,1,0:T(8,128)(2,1)} %shard_map.106.refs_12_), channel_id=1, source_target_pairs={{0,16},{16,0},{32,48},{48,32},{64,80},{80,64},{96,112},{112,96},{1... | collective-permute-start | bytes 1769480 | tf_op jit(solution)/shard_map/ppermute | solution.py:394
  64.9 11.6 %collective-permute-start.11 = (bf16[52,32,128]{2,1,0:T(8,128)(2,1)}, bf16[52,32,128]{2,1,0:T(8,128)(2,1)S(1)}, u32[]{:S(2)}, u32[]{:S(2)}) collective-permute-start(bf16[52,32,128]{2,1,0:T(8,128)(2,1)} %collective-permute-done.9.refs_4_), channel_id=1, source_target_pairs={{0,224},{16,240},{32,0},{48,16},{64,32},{80,48},{96,64},{112,80},{... | collective-permute-start | bytes 1277960 | tf_op jit(solution)/shard_map/ppermute | solution.py:394
  66.5 25.0 %collective-permute-start.7 = (bf16[256,1536]{1,0:T(8,128)(2,1)S(1)}, bf16[256,1536]{1,0:T(8,128)(2,1)S(1)}, u32[]{:S(2)}, u32[]{:S(2)}) collective-permute-start(bf16[256,1536]{1,0:T(8,128)(2,1)S(1)} %constant_dynamic-update-slice_fusion.refs_0_), channel_id=1, source_target_pairs={{0,16},{16,0},{32,48},{48,32},{64,80},{80,64},{96,112},{112,96},{1... | collective-permute-start | bytes 2359304 | tf_op jit(solution)/shard_map/ppermute | solution.py:394
  72.6 13.2 %collective-permute-start.12 = (bf16[52,32,128]{2,1,0:T(8,128)(2,1)S(1)}, bf16[52,32,128]{2,1,0:T(8,128)(2,1)S(1)}, u32[]{:S(2)}, u32[]{:S(2)}) collective-permute-start(bf16[52,32,128]{2,1,0:T(8,128)(2,1)S(1)} %collective-permute-done.10.refs_5_), channel_id=1, source_target_pairs={{0,32},{16,48},{32,64},{48,80},{64,96},{80,112},{96,128},{112,144}... | collective-permute-start | bytes 1277960 | tf_op jit(solution)/shard_map/ppermute | solution.py:394
  72.7 8.8 %collective-permute-start.25 = (bf16[4,9,32,128]{3,2,1,0:T(8,128)(2,1)S(1)}, bf16[4,9,32,128]{3,2,1,0:T(8,128)(2,1)S(1)}, u32[]{:S(2)}, u32[]{:S(2)}) collective-permute-start(bf16[4,9,32,128]{3,2,1,0:T(8,128)(2,1)S(1)} %slice.18), channel_id=1, source_target_pairs={{0,2},{2,4},{4,6},{6,0},{8,10},{10,12},{12,14},{14,8},{1,3},{3,5},... | collective-permute-start | bytes 884744 | tf_op jit(solution)/shard_map/ppermute | solution.py:394
  78.5 11.0 %collective-permute-start.13 = (bf16[52,32,128]{2,1,0:T(8,128)(2,1)S(1)}, bf16[52,32,128]{2,1,0:T(8,128)(2,1)S(1)}, u32[]{:S(2)}, u32[]{:S(2)}) collective-permute-start(bf16[52,32,128]{2,1,0:T(8,128)(2,1)S(1)} %collective-permute-done.11.refs_6_), channel_id=1, source_target_pairs={{0,224},{16,240},{32,0},{48,16},{64,32},{80,48},{96,64},{112,80},{... | collective-permute-start | bytes 1277960 | tf_op jit(solution)/shard_map/ppermute | solution.py:394
  81.5 13.7 %collective-permute-start.28 = (bf16[8,9,32,128]{3,2,1,0:T(8,128)(2,1)S(1)}, bf16[8,9,32,128]{3,2,1,0:T(8,128)(2,1)S(1)}, u32[]{:S(2)}, u32[]{:S(2)}) collective-permute-start(bf16[8,9,32,128]{3,2,1,0:T(8,128)(2,1)S(1)} %collective-permute-done.23.refs_13_), channel_id=1, source_target_pairs={{0,16},{16,0},{32,48},{48,32},{64,80},{80,64},{96,112},{112,96},{1... | collective-permute-start | bytes 1769480 | tf_op jit(solution)/shard_map/ppermute | solution.py:394
  84.2 11.0 %collective-permute-start.29 = (bf16[8,9,32,128]{3,2,1,0:T(8,128)(2,1)S(1)}, bf16[8,9,32,128]{3,2,1,0:T(8,128)(2,1)S(1)}, u32[]{:S(2)}, u32[]{:S(2)}) collective-permute-start(bf16[8,9,32,128]{3,2,1,0:T(8,128)(2,1)S(1)} %collective-permute-done.24.refs_14_), channel_id=1, source_target_pairs={{0,16},{16,0},{32,48},{48,32},{64,80},{80,64},{96,112},{112,96},{1... | collective-permute-start | bytes 1769480 | tf_op jit(solution)/shard_map/ppermute | solution.py:394
  91.6 8.5 %collective-permute-start.14 = (bf16[26,32,128]{2,1,0:T(8,128)(2,1)S(1)}, bf16[26,32,128]{2,1,0:T(8,128)(2,1)S(1)}, u32[]{:S(2)}, u32[]{:S(2)}) collective-permute-start(bf16[26,32,128]{2,1,0:T(8,128)(2,1)S(1)} %slice.16), channel_id=1, source_target_pairs={{0,32},{16,48},{32,64},{48,80},{64,96},{80,112},{96,128},{112,144}... | collective-permute-start | bytes 638984 | tf_op jit(solution)/shard_map/ppermute | solution.py:394
  91.9 8.1 %collective-permute-start.15 = (bf16[26,32,128]{2,1,0:T(8,128)(2,1)S(1)}, bf16[26,32,128]{2,1,0:T(8,128)(2,1)S(1)}, u32[]{:S(2)}, u32[]{:S(2)}) collective-permute-start(bf16[26,32,128]{2,1,0:T(8,128)(2,1)S(1)} %slice.17), channel_id=1, source_target_pairs={{0,224},{16,240},{32,0},{48,16},{64,32},{80,48},{96,64},{112,80},{... | collective-permute-start | bytes 638984 | tf_op jit(solution)/shard_map/ppermute | solution.py:394
  125.4 8.0 %collective-permute-start.32 = (bf16[256,512]{1,0:T(8,128)(2,1)}, bf16[256,512]{1,0:T(8,128)(2,1)S(1)}, u32[]{:S(2)}, u32[]{:S(2)}) collective-permute-start(bf16[256,512]{1,0:T(8,128)(2,1)} %get-tuple-element.30), channel_id=1, source_target_pairs={{0,16},{16,0},{32,48},{48,32},{64,80},{80,64},{96,112},{112,96},{1... | collective-permute-start | bytes 786440 | tf_op jit(solution)/shard_map/ppermute | solution.py:394
  126.7 15.9 %all-to-all-start = ((f32[32,1,8]{2,1,0:T(1,128)}), f32[32,1,8]{2,1,0:T(1,128)S(1)}, u32[]{:S(2)}, u32[]{:S(2)}) async-start(f32[32,1,8]{2,1,0:T(1,128)} %get-tuple-element.28), calls=%async_computation | async-start | bytes 32768 | tf_op jit(solution)/shard_map/all_to_all | solution.py:510
  (43 other events, 415.2 us)

commit v6 on v5

--- a/solution.py
+++ b/solution.py
@@ -103,17 +103,20 @@
     share[...] = fold[pl.ds(pl.multiple_of(m["y"] * 32, 32), 32), :]
 
 
-def pack_kernel(k_t, k_tx, q_t, q_tx, share, w_mine, w_other, kv_mine, kv_other, k_one, w_one, q_x):
+def pack_w_kernel(w_mine, w_other, kv_mine, kv_other, w_one):
     c = where_am_i()["c"]
-    lat = jnp.concatenate([k_t[...], k_tx[...]], axis=0).T
-    for b in range(8):
-        k_one[b] = lat[b * 32 : (b + 1) * 32]
-    k_one[8] = share[...]
     for core, w, kv in ((c, w_mine, kv_mine), (1 - c, w_other, kv_other)):
         for n in range(6):
             w_one[pl.ds(n * 6 + core * 3, 3)] = w[n * 3 : n * 3 + 3]
         for n in range(8):
             w_one[36 + n * 2 + core] = kv[n]
+
+
+def pack_kernel(k_t, k_tx, q_t, q_tx, share, k_one, q_x):
+    lat = jnp.concatenate([k_t[...], k_tx[...]], axis=0).T
+    for b in range(8):
+        k_one[b] = lat[b * 32 : (b + 1) * 32]
+    k_one[8] = share[...]
     q_x[...] = jnp.concatenate([q_t[...], q_tx[...]], axis=0).T
 
 
@@ -439,11 +442,10 @@
         specs=[SMEM, VMEM],
         scratch=[pltpu.VMEM((128, 128), bf16)],
     )
-    k_one, w_one, q_x = call(
-        pack_kernel,
-        [((9, 32, 128), bf16), ((52, 32, 128), bf16), ((256, 384), bf16)],
-        (k_t, k_tx, q_t, q_tx, share, w_mine, w_other, kv_mine, kv_other),
-    )
+    k_one, q_x = call(
+        pack_kernel, [((9, 32, 128), bf16), ((256, 384), bf16)], (k_t, k_tx, q_t, q_tx, share)
+    )
+    (w_one,) = call(pack_w_kernel, [((52, 32, 128), bf16)], (w_mine, w_other, kv_mine, kv_other))
 
     k_ring = ring(k_one)
     w_ring = ring(w_one, 3)

time: 145 us -> 134 us (0.924)
  waiting for transfers between devices: 44.3 us -> 30.5 us
  Pallas kernels: 34.5 us -> 36 us
    ppermute x33, waiting for transfers between devices: 36.9 us -> 23.1 us  [move(): return lax.ppermute(x, axis, perm)]
    pallas_call x5 -> x6, Pallas kernels: 9.96 us -> 11.5 us  [call(): pl.pallas_call(kernel, out_shape=outs, in_specs=specs or [VMEM] * len(arg...]
  transfers between devices with their start and end apart: 34 -> 34, of which waited for: 10 -> 10; matrix products, arithmetic and copies ran while one was open for 1% -> 2% of each run, Pallas kernels for 3% -> 7%
where the time goes in v6:
time: 134 us; the launch traced here: 133 us
  starting transfers between devices  60.9 us (45%)
  Pallas kernels  36 us (27%)
  waiting for transfers between devices  30.5 us (23%)
  local copies, waits for them, and re-layouts  2.89 us (2%)
  other arithmetic  1.85 us (1%)
    ppermute x33, starting transfers between devices, move(): return lax.ppermute(x, axis, perm)  53.5 us
    pallas_call x1, Pallas kernels, on_device(): pl.pallas_call(attend_kernel, out_shape=[jax.ShapeDtypeStruct((256, 512),...  24.5 us
    ppermute x33, waiting for transfers between devices, move(): return lax.ppermute(x, axis, perm)  23.1 us
    pallas_call x6, Pallas kernels, call(): pl.pallas_call(kernel, out_shape=outs, in_specs=specs or [VMEM] * len(arg...  11.5 us
    all_to_all x1, starting transfers between devices, on_device(): lax.all_to_all(everyone, ('seq', 'dp'), split_axis=0, concat_axis=0, tile...  7.44 us
    all_to_all x1, waiting for transfers between devices, on_device(): lax.all_to_all(everyone, ('seq', 'dp'), split_axis=0, concat_axis=0, tile...  7.4 us
    unnamed x67, local copies, waits for them, and re-layouts  2.78 us
  transfers between devices with their start and end apart: 34, of which 10 were waited for; matrix products, arithmetic and copies ran while one was open for 2% of the time, Pallas kernels for 7%

profile of v6, /device:TPU:1, one launch (start us, length us, event | category | flops | bytes accessed | tf_op | source)
XLA Modules:
  0.0 133.2 jit_solution(10440802585347296418)
XLA Ops:
  0.6 2.1 %collective-permute-start.1 = (bf16[192,256]{1,0:T(8,128)(2,1)}, bf16[192,256]{1,0:T(8,128)(2,1)S(1)}, u32[]{:S(2)}, u32[]{:S(2)}) collective-permute-start(bf16[192,256]{1,0:T(8,128)(2,1)} %bitcast.12), channel_id=1, source_target_pairs={{0,8},{2,10},{4,12},{6,14},{8,0},{10,2},{12,4},{14,6},{1,9},{3,11}... | collective-permute-start | bytes 294920 | tf_op jit(solution)/shard_map/ppermute | solution.py:397
  8.0 2.0 %shard_map.103 = (f32[512,256]{1,0:T(8,128)}, bf16[32,128]{1,0:T(8,128)(2,1)}) custom-call(s32[1,32]{1,0:T(1,128)} %order.3, bf16[64,256]{1,0:T(8,128)(2,1)} %bitcast.16), custom_call_target="tpu_custom_call" | custom-call | flops 1048576 | bytes 1064960 | tf_op jit(solution)/shard_map/pallas_call | solution.py:418
  16.7 2.3 %collective-permute-start.17 = (bf16[9,32,128]{2,1,0:T(8,128)(2,1)S(1)}, bf16[9,32,128]{2,1,0:T(8,128)(2,1)S(1)}, u32[]{:S(2)}, u32[]{:S(2)}) collective-permute-start(bf16[9,32,128]{2,1,0:T(8,128)(2,1)S(1)} %copy-done.7), channel_id=1, source_target_pairs={{0,224},{16,240},{32,0},{48,16},{64,32},{80,48},{96,64},{112,80},{... | collective-permute-start | bytes 221192 | tf_op jit(solution)/shard_map/ppermute | solution.py:397
  20.4 3.0 %collective-permute-start.19 = (bf16[9,32,128]{2,1,0:T(8,128)(2,1)S(1)}, bf16[9,32,128]{2,1,0:T(8,128)(2,1)S(1)}, u32[]{:S(2)}, u32[]{:S(2)}) collective-permute-start(bf16[9,32,128]{2,1,0:T(8,128)(2,1)S(1)} %collective-permute-done.17.refs_2_), channel_id=1, source_target_pairs={{0,224},{16,240},{32,0},{48,16},{64,32},{80,48},{96,64},{112,80},{... | collective-permute-start | bytes 221192 | tf_op jit(solution)/shard_map/ppermute | solution.py:397
  23.4 6.4 %collective-permute-done.18.refs_3_ = bf16[9,32,128]{2,1,0:T(8,128)(2,1)S(1)} collective-permute-done((bf16[9,32,128]{2,1,0:T(8,128)(2,1)S(1)}, bf16[9,32,128]{2,1,0:T(8,128)(2,1)S(1)}, u32[]{:S(2)}, u32[]{:S(2)}) %collective-permute-start.18) | collective-permute-done | bytes 73760 | tf_op jit(solution)/shard_map/ppermute | solution.py:397
  31.3 2.6 %collective-permute-start.21 = (bf16[9,32,128]{2,1,0:T(8,128)(2,1)S(1)}, bf16[9,32,128]{2,1,0:T(8,128)(2,1)S(1)}, u32[]{:S(2)}, u32[]{:S(2)}) collective-permute-start(bf16[9,32,128]{2,1,0:T(8,128)(2,1)S(1)} %collective-permute-done.19.refs_4_), channel_id=1, source_target_pairs={{0,224},{16,240},{32,0},{48,16},{64,32},{80,48},{96,64},{112,80},{... | collective-permute-start | bytes 221192 | tf_op jit(solution)/shard_map/ppermute | solution.py:397
  34.3 2.7 %collective-permute-start.3 = (bf16[256,384]{1,0:T(8,128)(2,1)S(1)}, bf16[256,384]{1,0:T(8,128)(2,1)S(1)}, u32[]{:S(2)}, u32[]{:S(2)}) collective-permute-start(bf16[256,384]{1,0:T(8,128)(2,1)S(1)} %copy-done), channel_id=1, source_target_pairs={{0,6},{2,0},{4,2},{6,4},{8,14},{10,8},{12,10},{14,12},{1,7},{3,1},... | collective-permute-start | bytes 589832 | tf_op jit(solution)/shard_map/ppermute | solution.py:397
  38.7 2.2 %collective-permute-start.9 = (bf16[52,32,128]{2,1,0:T(8,128)(2,1)}, bf16[52,32,128]{2,1,0:T(8,128)(2,1)}, u32[]{:S(2)}, u32[]{:S(2)}) collective-permute-start(bf16[52,32,128]{2,1,0:T(8,128)(2,1)} %shard_map.106.refs_2_), channel_id=1, source_target_pairs={{0,224},{16,240},{32,0},{48,16},{64,32},{80,48},{96,64},{112,80},{... | collective-permute-start | bytes 1277960 | tf_op jit(solution)/shard_map/ppermute | solution.py:397
  40.9 2.0 %shard_map.107.refs_12_ = bf16[8,9,32,128]{3,2,1,0:T(8,128)(2,1)} custom-call(bf16[9,32,128]{2,1,0:T(8,128)(2,1)} %get-tuple-element.25.refs_0_, bf16[9,32,128]{2,1,0:T(8,128)(2,1)} %copy-done.8, bf16[9,32,128]{2,1,0:T(8,128)(2,1)} %copy-done.9, bf16[9,32,128]{2,1,0:T(8,128)(2,1)} %copy-done.10, bf16[9,32,128]{2,1,0:T(8,128)(2,1)} %copy-done.11, ...), custom_call_target="tpu_custom_call" | custom-call | flops 1048576 | bytes 1179648 | tf_op jit(solution)/shard_map/pallas_call | solution.py:418
  43.1 2.7 %collective-permute-start.24 = (bf16[8,9,32,128]{3,2,1,0:T(8,128)(2,1)}, bf16[8,9,32,128]{3,2,1,0:T(8,128)(2,1)S(1)}, u32[]{:S(2)}, u32[]{:S(2)}) collective-permute-start(bf16[8,9,32,128]{3,2,1,0:T(8,128)(2,1)} %shard_map.107.refs_12_), channel_id=1, source_target_pairs={{0,6},{2,0},{4,2},{6,4},{8,14},{10,8},{12,10},{14,12},{1,7},{3,1},... | collective-permute-start | bytes 1769480 | tf_op jit(solution)/shard_map/ppermute | solution.py:397
  45.8 4.5 %collective-permute-start.27 = (bf16[8,9,32,128]{3,2,1,0:T(8,128)(2,1)}, bf16[8,9,32,128]{3,2,1,0:T(8,128)(2,1)S(1)}, u32[]{:S(2)}, u32[]{:S(2)}) collective-permute-start(bf16[8,9,32,128]{3,2,1,0:T(8,128)(2,1)} %shard_map.107.refs_12_), channel_id=1, source_target_pairs={{0,16},{16,0},{32,48},{48,32},{64,80},{80,64},{96,112},{112,96},{1... | collective-permute-start | bytes 1769480 | tf_op jit(solution)/shard_map/ppermute | solution.py:397
  50.4 2.7 %collective-permute-start.11 = (bf16[52,32,128]{2,1,0:T(8,128)(2,1)}, bf16[52,32,128]{2,1,0:T(8,128)(2,1)S(1)}, u32[]{:S(2)}, u32[]{:S(2)}) collective-permute-start(bf16[52,32,128]{2,1,0:T(8,128)(2,1)} %collective-permute-done.9.refs_4_), channel_id=1, source_target_pairs={{0,224},{16,240},{32,0},{48,16},{64,32},{80,48},{96,64},{112,80},{... | collective-permute-start | bytes 1277960 | tf_op jit(solution)/shard_map/ppermute | solution.py:397
  53.2 2.2 %collective-permute-done.23.refs_13_ = bf16[8,9,32,128]{3,2,1,0:T(8,128)(2,1)S(1)} collective-permute-done((bf16[8,9,32,128]{3,2,1,0:T(8,128)(2,1)}, bf16[8,9,32,128]{3,2,1,0:T(8,128)(2,1)S(1)}, u32[]{:S(2)}, u32[]{:S(2)}) %collective-permute-start.23) | collective-permute-done | bytes 589856 | tf_op jit(solution)/shard_map/ppermute | solution.py:397
  55.4 4.8 %collective-permute-start.5 = (bf16[256,1536]{1,0:T(8,128)(2,1)S(1)}, bf16[256,1536]{1,0:T(8,128)(2,1)S(1)}, u32[]{:S(2)}, u32[]{:S(2)}) collective-permute-start(bf16[256,1536]{1,0:T(8,128)(2,1)S(1)} %constant_dynamic-update-slice_fusion.refs_0_), channel_id=1, source_target_pairs={{0,16},{16,0},{32,48},{48,32},{64,80},{80,64},{96,112},{112,96},{1... | collective-permute-start | bytes 2359304 | tf_op jit(solution)/shard_map/ppermute | solution.py:397
  60.2 2.8 %collective-permute-done.10.refs_5_ = bf16[52,32,128]{2,1,0:T(8,128)(2,1)S(1)} collective-permute-done((bf16[52,32,128]{2,1,0:T(8,128)(2,1)}, bf16[52,32,128]{2,1,0:T(8,128)(2,1)S(1)}, u32[]{:S(2)}, u32[]{:S(2)}) %collective-permute-start.10) | collective-permute-done | bytes 426016 | tf_op jit(solution)/shard_map/ppermute | solution.py:397
  63.2 2.7 %collective-permute-start.26 = (bf16[4,9,32,128]{3,2,1,0:T(8,128)(2,1)S(1)}, bf16[4,9,32,128]{3,2,1,0:T(8,128)(2,1)S(1)}, u32[]{:S(2)}, u32[]{:S(2)}) collective-permute-start(bf16[4,9,32,128]{3,2,1,0:T(8,128)(2,1)S(1)} %slice.19), channel_id=1, source_target_pairs={{0,6},{2,0},{4,2},{6,4},{8,14},{10,8},{12,10},{14,12},{1,7},{3,1},... | collective-permute-start | bytes 884744 | tf_op jit(solution)/shard_map/ppermute | solution.py:397
  65.9 2.7 %collective-permute-start.13 = (bf16[52,32,128]{2,1,0:T(8,128)(2,1)S(1)}, bf16[52,32,128]{2,1,0:T(8,128)(2,1)S(1)}, u32[]{:S(2)}, u32[]{:S(2)}) collective-permute-start(bf16[52,32,128]{2,1,0:T(8,128)(2,1)S(1)} %collective-permute-done.11.refs_6_), channel_id=1, source_target_pairs={{0,224},{16,240},{32,0},{48,16},{64,32},{80,48},{96,64},{112,80},{... | collective-permute-start | bytes 1277960 | tf_op jit(solution)/shard_map/ppermute | solution.py:397
  68.6 3.4 %collective-permute-done.25.refs_15_ = bf16[4,9,32,128]{3,2,1,0:T(8,128)(2,1)S(1)} collective-permute-done((bf16[4,9,32,128]{3,2,1,0:T(8,128)(2,1)S(1)}, bf16[4,9,32,128]{3,2,1,0:T(8,128)(2,1)S(1)}, u32[]{:S(2)}, u32[]{:S(2)}) %collective-permute-start.25) | collective-permute-done | bytes 294944 | tf_op jit(solution)/shard_map/ppermute | solution.py:397
  76.5 2.2 %collective-permute-start.31 = (bf16[4,9,32,128]{3,2,1,0:T(8,128)(2,1)S(1)}, bf16[4,9,32,128]{3,2,1,0:T(8,128)(2,1)S(1)}, u32[]{:S(2)}, u32[]{:S(2)}) collective-permute-start(bf16[4,9,32,128]{3,2,1,0:T(8,128)(2,1)S(1)} %collective-permute-done.26.refs_16_), channel_id=1, source_target_pairs={{0,16},{16,0},{32,48},{48,32},{64,80},{80,64},{96,112},{112,96},{1... | collective-permute-start | bytes 884744 | tf_op jit(solution)/shard_map/ppermute | solution.py:397
  78.7 2.0 %collective-permute-start.14 = (bf16[26,32,128]{2,1,0:T(8,128)(2,1)S(1)}, bf16[26,32,128]{2,1,0:T(8,128)(2,1)S(1)}, u32[]{:S(2)}, u32[]{:S(2)}) collective-permute-start(bf16[26,32,128]{2,1,0:T(8,128)(2,1)S(1)} %slice.16), channel_id=1, source_target_pairs={{0,32},{16,48},{32,64},{48,80},{64,96},{80,112},{96,128},{112,144}... | collective-permute-start | bytes 638984 | tf_op jit(solution)/shard_map/ppermute | solution.py:397
  82.4 4.8 %collective-permute-done.14.refs_9_ = bf16[26,32,128]{2,1,0:T(8,128)(2,1)S(1)} collective-permute-done((bf16[26,32,128]{2,1,0:T(8,128)(2,1)S(1)}, bf16[26,32,128]{2,1,0:T(8,128)(2,1)S(1)}, u32[]{:S(2)}, u32[]{:S(2)}) %collective-permute-start.14) | collective-permute-done | bytes 213024 | tf_op jit(solution)/shard_map/ppermute | solution.py:397
  88.0 24.5 %attend.1 = (bf16[256,512]{1,0:T(8,128)(2,1)}, bf16[256,512]{1,0:T(8,128)(2,1)}, f32[32,1,8]{2,1,0:T(1,128)}) custom-call(s32[1,32]{1,0:T(1,128)} %order.3, s32[32,128]{1,0:T(8,128)} %bitcast.17, bf16[256,1536]{1,0:T(8,128)(2,1)} %copy-done.17, bf16[256,1536]{1,0:T(8,128)(2,1)} %copy-done.20, bf16[52,32,128]{2,1,0:T(8,128)(2,1)} %shard_map.106.refs_2_, ...), custom_call_target="tpu_custom_call" | custom-call | flops 21474836480 | bytes 12582912 | tf_op jit(solution)/shard_map/attend/pallas_call | solution.py:471
  114.0 7.4 %all-to-all-start = ((f32[32,1,8]{2,1,0:T(1,128)}), f32[32,1,8]{2,1,0:T(1,128)S(1)}, u32[]{:S(2)}, u32[]{:S(2)}) async-start(f32[32,1,8]{2,1,0:T(1,128)} %get-tuple-element.26), calls=%async_computation | async-start | bytes 32768 | tf_op jit(solution)/shard_map/all_to_all | solution.py:512
  123.3 7.4 %all-to-all-done.everyone = f32[32,1,8]{2,1,0:T(1,128)S(1)} async-done(((f32[32,1,8]{2,1,0:T(1,128)}), f32[32,1,8]{2,1,0:T(1,128)S(1)}, u32[]{:S(2)}, u32[]{:S(2)}) %all-to-all-start) | async-done | bytes 1056 | tf_op jit(solution)/shard_map/all_to_all | solution.py:512
  (125 shorter events, 29.8 us)
Async XLA Ops:
  0.6 9.4 %collective-permute-start.1 = (bf16[192,256]{1,0:T(8,128)(2,1)}, bf16[192,256]{1,0:T(8,128)(2,1)S(1)}, u32[]{:S(2)}, u32[]{:S(2)}) collective-permute-start(bf16[192,256]{1,0:T(8,128)(2,1)} %bitcast.12), channel_id=1, source_target_pairs={{0,8},{2,10},{4,12},{6,14},{8,0},{10,2},{12,4},{14,6},{1,9},{3,11}... | collective-permute-start | bytes 294920 | tf_op jit(solution)/shard_map/ppermute | solution.py:397
  4.7 7.8 %collective-permute-start.6 = (bf16[18,32,128]{2,1,0:T(8,128)(2,1)}, bf16[18,32,128]{2,1,0:T(8,128)(2,1)S(1)}, u32[]{:S(2)}, u32[]{:S(2)}) collective-permute-start(bf16[18,32,128]{2,1,0:T(8,128)(2,1)} %get-tuple-element.21), channel_id=1, source_target_pairs={{0,16},{16,0},{32,48},{48,32},{64,80},{80,64},{96,112},{112,96},{1... | collective-permute-start | bytes 442376 | tf_op jit(solution)/shard_map/ppermute | solution.py:397
  15.1 35.2 %collective-permute-start.8 = (bf16[52,32,128]{2,1,0:T(8,128)(2,1)}, bf16[52,32,128]{2,1,0:T(8,128)(2,1)}, u32[]{:S(2)}, u32[]{:S(2)}) collective-permute-start(bf16[52,32,128]{2,1,0:T(8,128)(2,1)} %shard_map.106.refs_2_), channel_id=1, source_target_pairs={{0,32},{16,48},{32,64},{48,80},{64,96},{80,112},{96,128},{112,144}... | collective-permute-start | bytes 1277960 | tf_op jit(solution)/shard_map/ppermute | solution.py:397
  19.0 10.8 %collective-permute-start.18 = (bf16[9,32,128]{2,1,0:T(8,128)(2,1)S(1)}, bf16[9,32,128]{2,1,0:T(8,128)(2,1)S(1)}, u32[]{:S(2)}, u32[]{:S(2)}) collective-permute-start(bf16[9,32,128]{2,1,0:T(8,128)(2,1)S(1)} %collective-permute-done.16.refs_1_), channel_id=1, source_target_pairs={{0,32},{16,48},{32,64},{48,80},{64,96},{80,112},{96,128},{112,144}... | collective-permute-start | bytes 221192 | tf_op jit(solution)/shard_map/ppermute | solution.py:397
  20.4 10.8 %collective-permute-start.19 = (bf16[9,32,128]{2,1,0:T(8,128)(2,1)S(1)}, bf16[9,32,128]{2,1,0:T(8,128)(2,1)S(1)}, u32[]{:S(2)}, u32[]{:S(2)}) collective-permute-start(bf16[9,32,128]{2,1,0:T(8,128)(2,1)S(1)} %collective-permute-done.17.refs_2_), channel_id=1, source_target_pairs={{0,224},{16,240},{32,0},{48,16},{64,32},{80,48},{96,64},{112,80},{... | collective-permute-start | bytes 221192 | tf_op jit(solution)/shard_map/ppermute | solution.py:397
  29.9 13.1 %collective-permute-start.2 = (bf16[256,384]{1,0:T(8,128)(2,1)S(1)}, bf16[256,384]{1,0:T(8,128)(2,1)S(1)}, u32[]{:S(2)}, u32[]{:S(2)}) collective-permute-start(bf16[256,384]{1,0:T(8,128)(2,1)S(1)} %copy-done), channel_id=1, source_target_pairs={{0,2},{2,4},{4,6},{6,0},{8,10},{10,12},{12,14},{14,8},{1,3},{3,5},... | collective-permute-start | bytes 589832 | tf_op jit(solution)/shard_map/ppermute | solution.py:397
  34.3 8.8 %collective-permute-start.3 = (bf16[256,384]{1,0:T(8,128)(2,1)S(1)}, bf16[256,384]{1,0:T(8,128)(2,1)S(1)}, u32[]{:S(2)}, u32[]{:S(2)}) collective-permute-start(bf16[256,384]{1,0:T(8,128)(2,1)S(1)} %copy-done), channel_id=1, source_target_pairs={{0,6},{2,0},{4,2},{6,4},{8,14},{10,8},{12,10},{14,12},{1,7},{3,1},... | collective-permute-start | bytes 589832 | tf_op jit(solution)/shard_map/ppermute | solution.py:397
  37.0 8.7 %collective-permute-start.4 = (bf16[256,384]{1,0:T(8,128)(2,1)S(1)}, bf16[256,384]{1,0:T(8,128)(2,1)S(1)}, u32[]{:S(2)}, u32[]{:S(2)}) collective-permute-start(bf16[256,384]{1,0:T(8,128)(2,1)S(1)} %copy-done), channel_id=1, source_target_pairs={{0,4},{2,6},{4,0},{6,2},{8,12},{10,14},{12,8},{14,10},{1,5},{3,7},... | collective-permute-start | bytes 589832 | tf_op jit(solution)/shard_map/ppermute | solution.py:397
  38.7 11.7 %collective-permute-start.9 = (bf16[52,32,128]{2,1,0:T(8,128)(2,1)}, bf16[52,32,128]{2,1,0:T(8,128)(2,1)}, u32[]{:S(2)}, u32[]{:S(2)}) collective-permute-start(bf16[52,32,128]{2,1,0:T(8,128)(2,1)} %shard_map.106.refs_2_), channel_id=1, source_target_pairs={{0,224},{16,240},{32,0},{48,16},{64,32},{80,48},{96,64},{112,80},{... | collective-permute-start | bytes 1277960 | tf_op jit(solution)/shard_map/ppermute | solution.py:397
  43.0 12.4 %collective-permute-start.23 = (bf16[8,9,32,128]{3,2,1,0:T(8,128)(2,1)}, bf16[8,9,32,128]{3,2,1,0:T(8,128)(2,1)S(1)}, u32[]{:S(2)}, u32[]{:S(2)}) collective-permute-start(bf16[8,9,32,128]{3,2,1,0:T(8,128)(2,1)} %shard_map.107.refs_12_), channel_id=1, source_target_pairs={{0,2},{2,4},{4,6},{6,0},{8,10},{10,12},{12,14},{14,8},{1,3},{3,5},... | collective-permute-start | bytes 1769480 | tf_op jit(solution)/shard_map/ppermute | solution.py:397
  43.1 19.9 %collective-permute-start.24 = (bf16[8,9,32,128]{3,2,1,0:T(8,128)(2,1)}, bf16[8,9,32,128]{3,2,1,0:T(8,128)(2,1)S(1)}, u32[]{:S(2)}, u32[]{:S(2)}) collective-permute-start(bf16[8,9,32,128]{3,2,1,0:T(8,128)(2,1)} %shard_map.107.refs_12_), channel_id=1, source_target_pairs={{0,6},{2,0},{4,2},{6,4},{8,14},{10,8},{12,10},{14,12},{1,7},{3,1},... | collective-permute-start | bytes 1769480 | tf_op jit(solution)/shard_map/ppermute | solution.py:397
  45.8 17.4 %collective-permute-start.27 = (bf16[8,9,32,128]{3,2,1,0:T(8,128)(2,1)}, bf16[8,9,32,128]{3,2,1,0:T(8,128)(2,1)S(1)}, u32[]{:S(2)}, u32[]{:S(2)}) collective-permute-start(bf16[8,9,32,128]{3,2,1,0:T(8,128)(2,1)} %shard_map.107.refs_12_), channel_id=1, source_target_pairs={{0,16},{16,0},{32,48},{48,32},{64,80},{80,64},{96,112},{112,96},{1... | collective-permute-start | bytes 1769480 | tf_op jit(solution)/shard_map/ppermute | solution.py:397
  50.3 12.7 %collective-permute-start.10 = (bf16[52,32,128]{2,1,0:T(8,128)(2,1)}, bf16[52,32,128]{2,1,0:T(8,128)(2,1)S(1)}, u32[]{:S(2)}, u32[]{:S(2)}) collective-permute-start(bf16[52,32,128]{2,1,0:T(8,128)(2,1)} %collective-permute-done.8.refs_3_), channel_id=1, source_target_pairs={{0,32},{16,48},{32,64},{48,80},{64,96},{80,112},{96,128},{112,144}... | collective-permute-start | bytes 1277960 | tf_op jit(solution)/shard_map/ppermute | solution.py:397
  50.4 15.6 %collective-permute-start.11 = (bf16[52,32,128]{2,1,0:T(8,128)(2,1)}, bf16[52,32,128]{2,1,0:T(8,128)(2,1)S(1)}, u32[]{:S(2)}, u32[]{:S(2)}) collective-permute-start(bf16[52,32,128]{2,1,0:T(8,128)(2,1)} %collective-permute-done.9.refs_4_), channel_id=1, source_target_pairs={{0,224},{16,240},{32,0},{48,16},{64,32},{80,48},{96,64},{112,80},{... | collective-permute-start | bytes 1277960 | tf_op jit(solution)/shard_map/ppermute | solution.py:397
  55.4 23.3 %collective-permute-start.5 = (bf16[256,1536]{1,0:T(8,128)(2,1)S(1)}, bf16[256,1536]{1,0:T(8,128)(2,1)S(1)}, u32[]{:S(2)}, u32[]{:S(2)}) collective-permute-start(bf16[256,1536]{1,0:T(8,128)(2,1)S(1)} %constant_dynamic-update-slice_fusion.refs_0_), channel_id=1, source_target_pairs={{0,16},{16,0},{32,48},{48,32},{64,80},{80,64},{96,112},{112,96},{1... | collective-permute-start | bytes 2359304 | tf_op jit(solution)/shard_map/ppermute | solution.py:397
  63.0 11.6 %collective-permute-start.12 = (bf16[52,32,128]{2,1,0:T(8,128)(2,1)S(1)}, bf16[52,32,128]{2,1,0:T(8,128)(2,1)S(1)}, u32[]{:S(2)}, u32[]{:S(2)}) collective-permute-start(bf16[52,32,128]{2,1,0:T(8,128)(2,1)S(1)} %collective-permute-done.10.refs_5_), channel_id=1, source_target_pairs={{0,32},{16,48},{32,64},{48,80},{64,96},{80,112},{96,128},{112,144}... | collective-permute-start | bytes 1277960 | tf_op jit(solution)/shard_map/ppermute | solution.py:397
  63.1 8.9 %collective-permute-start.25 = (bf16[4,9,32,128]{3,2,1,0:T(8,128)(2,1)S(1)}, bf16[4,9,32,128]{3,2,1,0:T(8,128)(2,1)S(1)}, u32[]{:S(2)}, u32[]{:S(2)}) collective-permute-start(bf16[4,9,32,128]{3,2,1,0:T(8,128)(2,1)S(1)} %slice.18), channel_id=1, source_target_pairs={{0,2},{2,4},{4,6},{6,0},{8,10},{10,12},{12,14},{14,8},{1,3},{3,5},... | collective-permute-start | bytes 884744 | tf_op jit(solution)/shard_map/ppermute | solution.py:397
  63.2 10.6 %collective-permute-start.26 = (bf16[4,9,32,128]{3,2,1,0:T(8,128)(2,1)S(1)}, bf16[4,9,32,128]{3,2,1,0:T(8,128)(2,1)S(1)}, u32[]{:S(2)}, u32[]{:S(2)}) collective-permute-start(bf16[4,9,32,128]{3,2,1,0:T(8,128)(2,1)S(1)} %slice.19), channel_id=1, source_target_pairs={{0,6},{2,0},{4,2},{6,4},{8,14},{10,8},{12,10},{14,12},{1,7},{3,1},... | collective-permute-start | bytes 884744 | tf_op jit(solution)/shard_map/ppermute | solution.py:397
  65.9 10.5 %collective-permute-start.13 = (bf16[52,32,128]{2,1,0:T(8,128)(2,1)S(1)}, bf16[52,32,128]{2,1,0:T(8,128)(2,1)S(1)}, u32[]{:S(2)}, u32[]{:S(2)}) collective-permute-start(bf16[52,32,128]{2,1,0:T(8,128)(2,1)S(1)} %collective-permute-done.11.refs_6_), channel_id=1, source_target_pairs={{0,224},{16,240},{32,0},{48,16},{64,32},{80,48},{96,64},{112,80},{... | collective-permute-start | bytes 1277960 | tf_op jit(solution)/shard_map/ppermute | solution.py:397
  72.0 10.4 %collective-permute-start.28 = (bf16[8,9,32,128]{3,2,1,0:T(8,128)(2,1)S(1)}, bf16[8,9,32,128]{3,2,1,0:T(8,128)(2,1)S(1)}, u32[]{:S(2)}, u32[]{:S(2)}) collective-permute-start(bf16[8,9,32,128]{3,2,1,0:T(8,128)(2,1)S(1)} %collective-permute-done.23.refs_13_), channel_id=1, source_target_pairs={{0,16},{16,0},{32,48},{48,32},{64,80},{80,64},{96,112},{112,96},{1... | collective-permute-start | bytes 1769480 | tf_op jit(solution)/shard_map/ppermute | solution.py:397
  73.8 8.6 %collective-permute-start.29 = (bf16[8,9,32,128]{3,2,1,0:T(8,128)(2,1)S(1)}, bf16[8,9,32,128]{3,2,1,0:T(8,128)(2,1)S(1)}, u32[]{:S(2)}, u32[]{:S(2)}) collective-permute-start(bf16[8,9,32,128]{3,2,1,0:T(8,128)(2,1)S(1)} %collective-permute-done.24.refs_14_), channel_id=1, source_target_pairs={{0,16},{16,0},{32,48},{48,32},{64,80},{80,64},{96,112},{112,96},{1... | collective-permute-start | bytes 1769480 | tf_op jit(solution)/shard_map/ppermute | solution.py:397
  78.7 8.5 %collective-permute-start.14 = (bf16[26,32,128]{2,1,0:T(8,128)(2,1)S(1)}, bf16[26,32,128]{2,1,0:T(8,128)(2,1)S(1)}, u32[]{:S(2)}, u32[]{:S(2)}) collective-permute-start(bf16[26,32,128]{2,1,0:T(8,128)(2,1)S(1)} %slice.16), channel_id=1, source_target_pairs={{0,32},{16,48},{32,64},{48,80},{64,96},{80,112},{96,128},{112,144}... | collective-permute-start | bytes 638984 | tf_op jit(solution)/shard_map/ppermute | solution.py:397
  112.5 8.9 %collective-permute-start.32 = (bf16[256,512]{1,0:T(8,128)(2,1)}, bf16[256,512]{1,0:T(8,128)(2,1)S(1)}, u32[]{:S(2)}, u32[]{:S(2)}) collective-permute-start(bf16[256,512]{1,0:T(8,128)(2,1)} %get-tuple-element.28), channel_id=1, source_target_pairs={{0,16},{16,0},{32,48},{48,32},{64,80},{80,64},{96,112},{112,96},{1... | collective-permute-start | bytes 786440 | tf_op jit(solution)/shard_map/ppermute | solution.py:397
  114.0 16.7 %all-to-all-start = ((f32[32,1,8]{2,1,0:T(1,128)}), f32[32,1,8]{2,1,0:T(1,128)S(1)}, u32[]{:S(2)}, u32[]{:S(2)}) async-start(f32[32,1,8]{2,1,0:T(1,128)} %get-tuple-element.26), calls=%async_computation | async-start | bytes 32768 | tf_op jit(solution)/shard_map/all_to_all | solution.py:512
  (42 other events, 358.9 us)
